TPU v7x, 32 devices: a whole 2x2x4 slice. The times are simulated.
32 devices in a mesh: inner: 4 (over y, x), wide: 8 (over z, core).
Axes of the slice: x: 2, y: 2, z: 4, core: 2. Of those that a mesh axis runs over, the one named last changes fastest.
Arguments:
- response: float32 [65536, 512], P(('inner', 'wide')), as said below
Outputs:
- upper_factor: float32 [512, 512], replicated
- q_rows: float32 [65536, 512], P(('inner', 'wide'))
Inputs may be any that keep to these rules, and one draw needn't show every extreme that they name: `response`: real and imaginary parts of measured receiver responses; the panel has full column rank.
All inputs are finite; a program needn't handle non-finite values.
Results may differ from a plain program's by a relative error of at most 0.0001.
Values sent between devices are 32-bit elements; how exact they have to be, the bound alone decides.
No kernel may reach another device: no remote copies, remote signals or barrier semaphores. Data moves between devices by JAX's collectives and lax.ppermute only.
A program may use at most 128 MiB of HBM per device.

v0:
```python
import jax
import jax.numpy as jnp
from jax import lax
from jax.experimental import pallas as pl
from jax.experimental.pallas import tpu as pltpu
from jax.sharding import PartitionSpec as P


BLOCK = 128
SLAB = 8


def hdot(left, right):
    return jnp.dot(left, right, precision=lax.Precision.HIGHEST, preferred_element_type=jnp.float32)


def sweep_block(diag):
    size = diag.shape[0]
    eye = (lax.broadcasted_iota(jnp.int32, (size, size), 0) == lax.broadcasted_iota(jnp.int32, (size, size), 1)).astype(jnp.float32)
    joined = jnp.concatenate([diag, eye], axis=1)
    slabs = [joined[s * SLAB:(s + 1) * SLAB] for s in range(size // SLAB)]
    rows = lax.broadcasted_iota(jnp.int32, (SLAB, 1), 0)
    for j in range(size):
        s, t = divmod(j, SLAB)
        scale = lax.rsqrt(slabs[s][t:t + 1, j:j + 1])
        top = slabs[s][t:t + 1, :] * scale
        for q in range(s + 1, len(slabs)):
            slabs[q] = slabs[q] - (slabs[q][:, j:j + 1] * scale) * top
        here = slabs[s]
        updated = here - (here[:, j:j + 1] * scale) * top
        slabs[s] = jnp.where(rows > t, updated, jnp.where(rows == t, top, here))
    joined = jnp.concatenate(slabs, axis=0)
    r = lax.broadcasted_iota(jnp.int32, (size, size), 0)
    c = lax.broadcasted_iota(jnp.int32, (size, size), 1)
    return jnp.where(c >= r, joined[:, :size], 0.0), joined[:, size:]


def chol_kernel(g_ref, u_ref, inv_ref, work_ref, aug_ref):
    n = g_ref.shape[0]
    g = g_ref[...]
    work_ref[...] = (g + g.T) * 0.5
    aug_ref[...] = jnp.zeros_like(aug_ref)
    u_ref[...] = jnp.zeros_like(u_ref)
    inv_ref[...] = jnp.zeros_like(inv_ref)
    blocks = n // BLOCK
    for k in range(blocks):
        lo, hi = k * BLOCK, (k + 1) * BLOCK
        u_kk, inv_kk = sweep_block(work_ref[lo:hi, lo:hi])
        u_ref[lo:hi, lo:hi] = u_kk
        if k > 0:
            inv_ref[lo:hi, 0:lo] = hdot(inv_kk, aug_ref[lo:hi, 0:lo])
        inv_ref[lo:hi, lo:hi] = inv_kk
        if hi < n:
            u_off = hdot(inv_kk, work_ref[lo:hi, hi:n])
            u_ref[lo:hi, hi:n] = u_off
            u_off_t = u_off.T
            work_ref[hi:n, hi:n] = work_ref[hi:n, hi:n] - hdot(u_off_t, u_off)
            aug_ref[hi:n, 0:hi] = aug_ref[hi:n, 0:hi] - hdot(u_off_t, inv_ref[lo:hi, 0:hi])


def cholesky_and_inverse(gram_matrix):
    n = gram_matrix.shape[0]
    spec = pl.BlockSpec(memory_space=pltpu.VMEM)
    return pl.pallas_call(
        chol_kernel,
        out_shape=(jax.ShapeDtypeStruct((n, n), jnp.float32), jax.ShapeDtypeStruct((n, n), jnp.float32)),
        in_specs=[spec],
        out_specs=(spec, spec),
        scratch_shapes=[pltpu.VMEM((n, n), jnp.float32), pltpu.VMEM((n, n), jnp.float32)],
    )(gram_matrix)


def matmul(left, right):
    return jnp.dot(left, right, precision=lax.Precision.HIGHEST, preferred_element_type=jnp.float32)


def gram_of(matrix):
    return lax.dot_general(
        matrix,
        matrix,
        (((0,), (0,)), ((), ())),
        precision=lax.Precision.HIGHEST,
        preferred_element_type=jnp.float32,
    )


def group_index(axis, shift, size):
    return (lax.axis_index(axis) >> shift) & (size - 1)


def partner_xor(value, axis, shift, offset):
    mask = offset << shift
    pairs = [(source, source ^ mask) for source in range(lax.axis_size(axis))]
    return lax.ppermute(value, axis, pairs)


def scatter_sum(value, axis, shift, size):
    height = value.shape[0] // size
    index = group_index(axis, shift, size)
    chunk = lambda j: lax.dynamic_slice_in_dim(value, j * height, height, 0)
    total = chunk(index)
    for offset in range(1, size):
        total = total + partner_xor(chunk(index ^ offset), axis, shift, offset)
    return total


def gather_all(chunk, axis, shift, size):
    height = chunk.shape[0]
    index = group_index(axis, shift, size)
    whole = jnp.zeros((height * size, chunk.shape[1]), chunk.dtype)
    whole = lax.dynamic_update_slice_in_dim(whole, chunk, index * height, 0)
    for offset in range(1, size):
        got = partner_xor(chunk, axis, shift, offset)
        whole = lax.dynamic_update_slice_in_dim(whole, got, (index ^ offset) * height, 0)
    return whole


def axis_groups(axis, first):
    bits = lax.axis_size(axis).bit_length() - 1
    groups = []
    shift = first
    while shift < bits:
        width = min(2, bits - shift)
        groups.append((axis, shift, 2**width))
        shift += width
    return groups


def all_sum(gram_matrix):
    groups = [("wide", 0, 2)] + axis_groups("inner", 0) + axis_groups("wide", 1)
    for group in groups:
        gram_matrix = scatter_sum(gram_matrix, *group)
    for group in reversed(groups):
        gram_matrix = gather_all(gram_matrix, *group)
    return gram_matrix


def on_device(response):
    row_count = response.shape[0] * lax.axis_size("inner") * lax.axis_size("wide")
    gram_matrix = gram_of(response) / row_count
    gram_matrix = all_sum(gram_matrix)
    upper_factor, inverse_lower = cholesky_and_inverse(gram_matrix)
    q_rows = lax.dot_general(
        response,
        inverse_lower,
        (((1,), (1,)), ((), ())),
        precision=lax.Precision.HIGHEST,
        preferred_element_type=jnp.float32,
    )
    return (upper_factor, q_rows)


def solution(mesh):
    in_specs = (P(("inner", "wide"), None),)
    out_specs = (P(), P(("inner", "wide"), None))
    return jax.shard_map(
        on_device, mesh=mesh, in_specs=in_specs, out_specs=out_specs, check_vma=False
    )
```

profile of v0, /device:TPU:0, one launch (start us, length us, event | category | flops | bytes accessed | tf_op | source)
XLA Modules:
  0.0 117.6 jit_solution(16238644497529086355)
XLA Ops:
  0.6 10.5 %convolution_multiply_fusion = f32[512,512]{1,0:T(8,128)S(1)} fusion(f32[2048,512]{1,0:T(8,128)} %param.1), kind=kOutput, calls=%fused_computation.1 | convolution fusion | flops 6442713088 | bytes 5242880 | tf_op jit(solution)/shard_map/dot_general | solution.py:78
  11.7 1.5 %collective-permute-done = f32[256,512]{1,0:T(8,128)S(1)} collective-permute-done((f32[256,512]{1,0:T(8,128)S(1)}, f32[256,512]{1,0:T(8,128)S(1)}, u32[]{:S(2)}, u32[]{:S(2)}) %collective-permute-start) | collective-permute-done | bytes 524320 | tf_op jit(solution)/shard_map/ppermute | solution.py:94
  13.4 2.9 %collective-permute-start.1 = (f32[64,512]{1,0:T(8,128)S(1)}, f32[64,512]{1,0:T(8,128)S(1)}, u32[]{:S(2)}, u32[]{:S(2)}) collective-permute-start(f32[64,512]{1,0:T(8,128)S(1)} %get-tuple-element.10), channel_id=1, source_target_pairs={{0,8},{8,0},{16,24},{24,16},{1,9},{9,1},{17,25},{25,17},{2,10},{10... | collective-permute-start | bytes 393224 | tf_op jit(solution)/shard_map/ppermute | solution.py:94
  16.3 1.5 %collective-permute-start.3 = (f32[64,512]{1,0:T(8,128)S(1)}, f32[64,512]{1,0:T(8,128)S(1)}, u32[]{:S(2)}, u32[]{:S(2)}) collective-permute-start(f32[64,512]{1,0:T(8,128)S(1)} %get-tuple-element.11), channel_id=1, source_target_pairs={{0,24},{8,16},{16,8},{24,0},{1,25},{9,17},{17,9},{25,1},{2,26},{10... | collective-permute-start | bytes 393224 | tf_op jit(solution)/shard_map/ppermute | solution.py:94
  17.9 2.6 %collective-permute-done.1 = f32[64,512]{1,0:T(8,128)S(1)} collective-permute-done((f32[64,512]{1,0:T(8,128)S(1)}, f32[64,512]{1,0:T(8,128)S(1)}, u32[]{:S(2)}, u32[]{:S(2)}) %collective-permute-start.1) | collective-permute-done | bytes 131104 | tf_op jit(solution)/shard_map/ppermute | solution.py:94
  20.4 3.8 %collective-permute-done.3 = f32[64,512]{1,0:T(8,128)S(1)} collective-permute-done((f32[64,512]{1,0:T(8,128)S(1)}, f32[64,512]{1,0:T(8,128)S(1)}, u32[]{:S(2)}, u32[]{:S(2)}) %collective-permute-start.3) | collective-permute-done | bytes 131104 | tf_op jit(solution)/shard_map/ppermute | solution.py:94
  24.2 1.4 %collective-permute-done.2 = f32[64,512]{1,0:T(8,128)S(1)} collective-permute-done((f32[64,512]{1,0:T(8,128)S(1)}, f32[64,512]{1,0:T(8,128)S(1)}, u32[]{:S(2)}, u32[]{:S(2)}) %collective-permute-start.2) | collective-permute-done | bytes 131104 | tf_op jit(solution)/shard_map/ppermute | solution.py:94
  25.7 1.6 %collective-permute-start.4 = (f32[16,512]{1,0:T(8,128)S(1)}, f32[16,512]{1,0:T(8,128)S(1)}, u32[]{:S(2)}, u32[]{:S(2)}) collective-permute-start(f32[16,512]{1,0:T(8,128)S(1)} %get-tuple-element.13), channel_id=1, source_target_pairs={{0,2},{1,3},{2,0},{3,1},{4,6},{5,7},{6,4},{7,5},{8,10},{9,11},{10,... | collective-permute-start | bytes 98312 | tf_op jit(solution)/shard_map/ppermute | solution.py:94
  27.3 2.5 %collective-permute-start.6 = (f32[16,512]{1,0:T(8,128)S(1)}, f32[16,512]{1,0:T(8,128)S(1)}, u32[]{:S(2)}, u32[]{:S(2)}) collective-permute-start(f32[16,512]{1,0:T(8,128)S(1)} %get-tuple-element.14), channel_id=1, source_target_pairs={{0,6},{1,7},{2,4},{3,5},{4,2},{5,3},{6,0},{7,1},{8,14},{9,15},{10,... | collective-permute-start | bytes 98312 | tf_op jit(solution)/shard_map/ppermute | solution.py:94
  29.9 3.1 %collective-permute-done.6 = f32[16,512]{1,0:T(8,128)S(1)} collective-permute-done((f32[16,512]{1,0:T(8,128)S(1)}, f32[16,512]{1,0:T(8,128)S(1)}, u32[]{:S(2)}, u32[]{:S(2)}) %collective-permute-start.6) | collective-permute-done | bytes 32800 | tf_op jit(solution)/shard_map/ppermute | solution.py:94
  33.0 1.9 %collective-permute-done.5 = f32[16,512]{1,0:T(8,128)S(1)} collective-permute-done((f32[16,512]{1,0:T(8,128)S(1)}, f32[16,512]{1,0:T(8,128)S(1)}, u32[]{:S(2)}, u32[]{:S(2)}) %collective-permute-start.5) | collective-permute-done | bytes 32800 | tf_op jit(solution)/shard_map/ppermute | solution.py:94
  35.5 1.4 %collective-permute-start.8 = (f32[16,512]{1,0:T(8,128)S(1)}, f32[16,512]{1,0:T(8,128)S(1)}, u32[]{:S(2)}, u32[]{:S(2)}) collective-permute-start(f32[16,512]{1,0:T(8,128)S(1)} %get-tuple-element.9), channel_id=1, source_target_pairs={{0,4},{1,5},{2,6},{3,7},{4,0},{5,1},{6,2},{7,3},{8,12},{9,13},{10,... | collective-permute-start | bytes 98312 | tf_op jit(solution)/shard_map/ppermute | solution.py:94
  36.9 2.6 %collective-permute-start.9 = (f32[16,512]{1,0:T(8,128)S(1)}, f32[16,512]{1,0:T(8,128)S(1)}, u32[]{:S(2)}, u32[]{:S(2)}) collective-permute-start(f32[16,512]{1,0:T(8,128)S(1)} %get-tuple-element.9), channel_id=1, source_target_pairs={{0,6},{1,7},{2,4},{3,5},{4,2},{5,3},{6,0},{7,1},{8,14},{9,15},{10,... | collective-permute-start | bytes 98312 | tf_op jit(solution)/shard_map/ppermute | solution.py:94
  39.4 0.8 collective-permute-done.8
  40.3 2.3 %collective-permute-done.9 = f32[16,512]{1,0:T(8,128)S(1)} collective-permute-done((f32[16,512]{1,0:T(8,128)S(1)}, f32[16,512]{1,0:T(8,128)S(1)}, u32[]{:S(2)}, u32[]{:S(2)}) %collective-permute-start.9) | collective-permute-done | bytes 32800 | tf_op jit(solution)/shard_map/ppermute | solution.py:94
  42.6 1.5 %collective-permute-start.10 = (f32[64,512]{1,0:T(8,128)S(1)}, f32[64,512]{1,0:T(8,128)S(1)}, u32[]{:S(2)}, u32[]{:S(2)}) collective-permute-start(f32[64,512]{1,0:T(8,128)S(1)} %constant_dynamic-update-slice_fusion.6), channel_id=1, source_target_pairs={{0,8},{8,0},{16,24},{24,16},{1,9},{9,1},{17,25},{25,17},{2,10},{10... | collective-permute-start | bytes 393224 | tf_op jit(solution)/shard_map/ppermute | solution.py:94
  44.5 1.5 %collective-permute-start.11 = (f32[64,512]{1,0:T(8,128)S(1)}, f32[64,512]{1,0:T(8,128)S(1)}, u32[]{:S(2)}, u32[]{:S(2)}) collective-permute-start(f32[64,512]{1,0:T(8,128)S(1)} %constant_dynamic-update-slice_fusion.6), channel_id=1, source_target_pairs={{0,16},{8,24},{16,0},{24,8},{1,17},{9,25},{17,1},{25,9},{2,18},{10... | collective-permute-start | bytes 393224 | tf_op jit(solution)/shard_map/ppermute | solution.py:94
  46.2 1.4 %collective-permute-done.10 = f32[64,512]{1,0:T(8,128)S(1)} collective-permute-done((f32[64,512]{1,0:T(8,128)S(1)}, f32[64,512]{1,0:T(8,128)S(1)}, u32[]{:S(2)}, u32[]{:S(2)}) %collective-permute-start.10) | collective-permute-done | bytes 131104 | tf_op jit(solution)/shard_map/ppermute | solution.py:94
  47.6 3.4 %collective-permute-done.11 = f32[64,512]{1,0:T(8,128)S(1)} collective-permute-done((f32[64,512]{1,0:T(8,128)S(1)}, f32[64,512]{1,0:T(8,128)S(1)}, u32[]{:S(2)}, u32[]{:S(2)}) %collective-permute-start.11) | collective-permute-done | bytes 131104 | tf_op jit(solution)/shard_map/ppermute | solution.py:94
  51.2 1.7 %collective-permute-done.13 = f32[256,512]{1,0:T(8,128)S(1)} collective-permute-done((f32[256,512]{1,0:T(8,128)S(1)}, f32[256,512]{1,0:T(8,128)S(1)}, u32[]{:S(2)}, u32[]{:S(2)}) %collective-permute-start.13) | collective-permute-done | bytes 524320 | tf_op jit(solution)/shard_map/ppermute | solution.py:94
  53.0 1.0 copy-done
  54.0 47.9 %shard_map.30 = (f32[512,512]{1,0:T(8,128)}, f32[512,512]{1,0:T(8,128)}) custom-call(f32[512,512]{1,0:T(8,128)} %copy-done), custom_call_target="tpu_custom_call" | custom-call | tf_op jit(solution)/shard_map/pallas_call | solution.py:64
  101.9 10.4 %convolution_bitcast_fusion = f32[2048,512]{0,1:T(8,128)} fusion(f32[512,512]{1,0:T(8,128)} %get-tuple-element.5, f32[2048,512]{1,0:T(8,128)} %param.1), kind=kOutput, calls=%fused_computation | convolution fusion | flops 6442450944 | bytes 9437184 | tf_op jit(solution)/shard_map/dot_general | solution.py:143
  112.3 5.3 %copy.3 = f32[2048,512]{1,0:T(8,128)} copy(f32[2048,512]{0,1:T(8,128)} %convolution_bitcast_fusion) | data formatting | bytes 8388608
  (28 shorter events, 2.3 us)
Async XLA Ops:
  11.2 2.1 %collective-permute-start = (f32[256,512]{1,0:T(8,128)S(1)}, f32[256,512]{1,0:T(8,128)S(1)}, u32[]{:S(2)}, u32[]{:S(2)}) collective-permute-start(f32[256,512]{1,0:T(8,128)S(1)} %constant_dynamic-slice_fusion.6), channel_id=1, source_target_pairs={{0,1},{1,0},{2,3},{3,2},{4,5},{5,4},{6,7},{7,6},{8,9},{9,8},{10,11... | collective-permute-start | bytes 1572872 | tf_op jit(solution)/shard_map/ppermute | solution.py:94
  13.4 7.0 %collective-permute-start.1 = (f32[64,512]{1,0:T(8,128)S(1)}, f32[64,512]{1,0:T(8,128)S(1)}, u32[]{:S(2)}, u32[]{:S(2)}) collective-permute-start(f32[64,512]{1,0:T(8,128)S(1)} %get-tuple-element.10), channel_id=1, source_target_pairs={{0,8},{8,0},{16,24},{24,16},{1,9},{9,1},{17,25},{25,17},{2,10},{10... | collective-permute-start | bytes 393224 | tf_op jit(solution)/shard_map/ppermute | solution.py:94
  16.3 7.9 %collective-permute-start.3 = (f32[64,512]{1,0:T(8,128)S(1)}, f32[64,512]{1,0:T(8,128)S(1)}, u32[]{:S(2)}, u32[]{:S(2)}) collective-permute-start(f32[64,512]{1,0:T(8,128)S(1)} %get-tuple-element.11), channel_id=1, source_target_pairs={{0,24},{8,16},{16,8},{24,0},{1,25},{9,17},{17,9},{25,1},{2,26},{10... | collective-permute-start | bytes 393224 | tf_op jit(solution)/shard_map/ppermute | solution.py:94
  17.8 7.8 %collective-permute-start.2 = (f32[64,512]{1,0:T(8,128)S(1)}, f32[64,512]{1,0:T(8,128)S(1)}, u32[]{:S(2)}, u32[]{:S(2)}) collective-permute-start(f32[64,512]{1,0:T(8,128)S(1)} %get-tuple-element.12), channel_id=1, source_target_pairs={{0,16},{8,24},{16,0},{24,8},{1,17},{9,25},{17,1},{25,9},{2,18},{10... | collective-permute-start | bytes 393224 | tf_op jit(solution)/shard_map/ppermute | solution.py:94
  25.7 4.2 %collective-permute-start.4 = (f32[16,512]{1,0:T(8,128)S(1)}, f32[16,512]{1,0:T(8,128)S(1)}, u32[]{:S(2)}, u32[]{:S(2)}) collective-permute-start(f32[16,512]{1,0:T(8,128)S(1)} %get-tuple-element.13), channel_id=1, source_target_pairs={{0,2},{1,3},{2,0},{3,1},{4,6},{5,7},{6,4},{7,5},{8,10},{9,11},{10,... | collective-permute-start | bytes 98312 | tf_op jit(solution)/shard_map/ppermute | solution.py:94
  27.3 5.7 %collective-permute-start.6 = (f32[16,512]{1,0:T(8,128)S(1)}, f32[16,512]{1,0:T(8,128)S(1)}, u32[]{:S(2)}, u32[]{:S(2)}) collective-permute-start(f32[16,512]{1,0:T(8,128)S(1)} %get-tuple-element.14), channel_id=1, source_target_pairs={{0,6},{1,7},{2,4},{3,5},{4,2},{5,3},{6,0},{7,1},{8,14},{9,15},{10,... | collective-permute-start | bytes 98312 | tf_op jit(solution)/shard_map/ppermute | solution.py:94
  29.8 5.2 %collective-permute-start.5 = (f32[16,512]{1,0:T(8,128)S(1)}, f32[16,512]{1,0:T(8,128)S(1)}, u32[]{:S(2)}, u32[]{:S(2)}) collective-permute-start(f32[16,512]{1,0:T(8,128)S(1)} %get-tuple-element.15), channel_id=1, source_target_pairs={{0,4},{1,5},{2,6},{3,7},{4,0},{5,1},{6,2},{7,3},{8,12},{9,13},{10,... | collective-permute-start | bytes 98312 | tf_op jit(solution)/shard_map/ppermute | solution.py:94
  35.0 4.5 %collective-permute-start.7 = (f32[16,512]{1,0:T(8,128)S(1)}, f32[16,512]{1,0:T(8,128)S(1)}, u32[]{:S(2)}, u32[]{:S(2)}) collective-permute-start(f32[16,512]{1,0:T(8,128)S(1)} %get-tuple-element.9), channel_id=1, source_target_pairs={{0,2},{1,3},{2,0},{3,1},{4,6},{5,7},{6,4},{7,5},{8,10},{9,11},{10,... | collective-permute-start | bytes 98312 | tf_op jit(solution)/shard_map/ppermute | solution.py:94
  35.5 4.8 %collective-permute-start.8 = (f32[16,512]{1,0:T(8,128)S(1)}, f32[16,512]{1,0:T(8,128)S(1)}, u32[]{:S(2)}, u32[]{:S(2)}) collective-permute-start(f32[16,512]{1,0:T(8,128)S(1)} %get-tuple-element.9), channel_id=1, source_target_pairs={{0,4},{1,5},{2,6},{3,7},{4,0},{5,1},{6,2},{7,3},{8,12},{9,13},{10,... | collective-permute-start | bytes 98312 | tf_op jit(solution)/shard_map/ppermute | solution.py:94
  36.9 5.7 %collective-permute-start.9 = (f32[16,512]{1,0:T(8,128)S(1)}, f32[16,512]{1,0:T(8,128)S(1)}, u32[]{:S(2)}, u32[]{:S(2)}) collective-permute-start(f32[16,512]{1,0:T(8,128)S(1)} %get-tuple-element.9), channel_id=1, source_target_pairs={{0,6},{1,7},{2,4},{3,5},{4,2},{5,3},{6,0},{7,1},{8,14},{9,15},{10,... | collective-permute-start | bytes 98312 | tf_op jit(solution)/shard_map/ppermute | solution.py:94
  42.6 5.0 %collective-permute-start.10 = (f32[64,512]{1,0:T(8,128)S(1)}, f32[64,512]{1,0:T(8,128)S(1)}, u32[]{:S(2)}, u32[]{:S(2)}) collective-permute-start(f32[64,512]{1,0:T(8,128)S(1)} %constant_dynamic-update-slice_fusion.6), channel_id=1, source_target_pairs={{0,8},{8,0},{16,24},{24,16},{1,9},{9,1},{17,25},{25,17},{2,10},{10... | collective-permute-start | bytes 393224 | tf_op jit(solution)/shard_map/ppermute | solution.py:94
  44.1 6.9 %collective-permute-start.12 = (f32[64,512]{1,0:T(8,128)S(1)}, f32[64,512]{1,0:T(8,128)S(1)}, u32[]{:S(2)}, u32[]{:S(2)}) collective-permute-start(f32[64,512]{1,0:T(8,128)S(1)} %constant_dynamic-update-slice_fusion.6), channel_id=1, source_target_pairs={{0,24},{8,16},{16,8},{24,0},{1,25},{9,17},{17,9},{25,1},{2,26},{10... | collective-permute-start | bytes 393224 | tf_op jit(solution)/shard_map/ppermute | solution.py:94
  44.5 6.4 %collective-permute-start.11 = (f32[64,512]{1,0:T(8,128)S(1)}, f32[64,512]{1,0:T(8,128)S(1)}, u32[]{:S(2)}, u32[]{:S(2)}) collective-permute-start(f32[64,512]{1,0:T(8,128)S(1)} %constant_dynamic-update-slice_fusion.6), channel_id=1, source_target_pairs={{0,16},{8,24},{16,0},{24,8},{1,17},{9,25},{17,1},{25,9},{2,18},{10... | collective-permute-start | bytes 393224 | tf_op jit(solution)/shard_map/ppermute | solution.py:94
  51.0 2.0 %collective-permute-start.13 = (f32[256,512]{1,0:T(8,128)S(1)}, f32[256,512]{1,0:T(8,128)S(1)}, u32[]{:S(2)}, u32[]{:S(2)}) collective-permute-start(f32[256,512]{1,0:T(8,128)S(1)} %constant_dynamic-update-slice_fusion.2), channel_id=1, source_target_pairs={{0,1},{1,0},{2,3},{3,2},{4,5},{5,4},{6,7},{7,6},{8,9},{9,8},{10,11... | collective-permute-start | bytes 1572872 | tf_op jit(solution)/shard_map/ppermute | solution.py:94
  53.0 1.0 copy-start
where the time goes:
time: 118 us
  Pallas kernels  47.9 us (41%)
  waiting for transfers between devices  23.9 us (20%)
  matrix products  20.9 us (18%)
  starting transfers between devices  17.2 us (15%)
  local copies, waits for them, and re-layouts  6.73 us (6%)
    pallas_call x1, Pallas kernels, cholesky_and_inverse(): pl.pallas_call(chol_kernel, out_shape=(jax.ShapeDtypeStruct((n, n), jnp.f...  47.9 us
    ppermute x14, waiting for transfers between devices, partner_xor(): return lax.ppermute(value, axis, pairs)  23.9 us
    ppermute x14, starting transfers between devices, partner_xor(): return lax.ppermute(value, axis, pairs)  17.2 us
    dot_general x1, matrix products, gram_of(): lax.dot_general(matrix, matrix, (((0,), (0,)), ((), ())), precision=lax.P...  10.5 us
    dot_general x1, matrix products, on_device(): lax.dot_general(response, inverse_lower, (((1,), (1,)), ((), ())), precis...  10.4 us
    unnamed x3, local copies, waits for them, and re-layouts  6.3 us
  transfers between devices with their start and end apart: 14, of which 11 were waited for; matrix products, arithmetic and copies ran while one was open for 0% of the time, Pallas kernels for 0%

commit v1 on v0

--- a/solution.py
+++ b/solution.py
@@ -35,12 +35,13 @@
     return jnp.where(c >= r, joined[:, :size], 0.0), joined[:, size:]
 
 
-def chol_kernel(g_ref, u_ref, inv_ref, work_ref, aug_ref):
+def chol_kernel(g_ref, u_ref, uinv_ref, work_ref, aug_ref, inv_ref):
     n = g_ref.shape[0]
     g = g_ref[...]
     work_ref[...] = (g + g.T) * 0.5
     aug_ref[...] = jnp.zeros_like(aug_ref)
     u_ref[...] = jnp.zeros_like(u_ref)
+    uinv_ref[...] = jnp.zeros_like(uinv_ref)
     inv_ref[...] = jnp.zeros_like(inv_ref)
     blocks = n // BLOCK
     for k in range(blocks):
@@ -48,8 +49,11 @@
         u_kk, inv_kk = sweep_block(work_ref[lo:hi, lo:hi])
         u_ref[lo:hi, lo:hi] = u_kk
         if k > 0:
-            inv_ref[lo:hi, 0:lo] = hdot(inv_kk, aug_ref[lo:hi, 0:lo])
+            inv_row = hdot(inv_kk, aug_ref[lo:hi, 0:lo])
+            inv_ref[lo:hi, 0:lo] = inv_row
+            uinv_ref[0:lo, lo:hi] = inv_row.T
         inv_ref[lo:hi, lo:hi] = inv_kk
+        uinv_ref[lo:hi, lo:hi] = inv_kk.T
         if hi < n:
             u_off = hdot(inv_kk, work_ref[lo:hi, hi:n])
             u_ref[lo:hi, hi:n] = u_off
@@ -66,8 +70,27 @@
         out_shape=(jax.ShapeDtypeStruct((n, n), jnp.float32), jax.ShapeDtypeStruct((n, n), jnp.float32)),
         in_specs=[spec],
         out_specs=(spec, spec),
-        scratch_shapes=[pltpu.VMEM((n, n), jnp.float32), pltpu.VMEM((n, n), jnp.float32)],
+        scratch_shapes=[pltpu.VMEM((n, n), jnp.float32) for _ in range(3)],
     )(gram_matrix)
+
+
+def rows_kernel(a_ref, w_ref, o_ref):
+    o_ref[...] = hdot(a_ref[...], w_ref[...])
+
+
+def rows_times(matrix, weights):
+    rows, width = matrix.shape
+    tile = min(rows, 512)
+    return pl.pallas_call(
+        rows_kernel,
+        out_shape=jax.ShapeDtypeStruct((rows, weights.shape[1]), jnp.float32),
+        grid=(rows // tile,),
+        in_specs=[
+            pl.BlockSpec((tile, width), lambda i: (i, 0)),
+            pl.BlockSpec(weights.shape, lambda i: (0, 0)),
+        ],
+        out_specs=pl.BlockSpec((tile, weights.shape[1]), lambda i: (i, 0)),
+    )(matrix, weights)
 
 
 def matmul(left, right):
@@ -139,14 +162,8 @@
     row_count = response.shape[0] * lax.axis_size("inner") * lax.axis_size("wide")
     gram_matrix = gram_of(response) / row_count
     gram_matrix = all_sum(gram_matrix)
-    upper_factor, inverse_lower = cholesky_and_inverse(gram_matrix)
-    q_rows = lax.dot_general(
-        response,
-        inverse_lower,
-        (((1,), (1,)), ((), ())),
-        precision=lax.Precision.HIGHEST,
-        preferred_element_type=jnp.float32,
-    )
+    upper_factor, inverse_upper = cholesky_and_inverse(gram_matrix)
+    q_rows = rows_times(response, inverse_upper)
     return (upper_factor, q_rows)
 
 

time: 118 us -> 112 us (0.949)
  matrix products: 20.9 us -> 10.5 us
  Pallas kernels: 47.9 us -> 57.8 us
  local copies, waits for them, and re-layouts: 6.73 us -> 1.39 us
    dot_general x1 -> x0, matrix products: 10.4 us -> none  [on_device(): lax.dot_general(response, inverse_lower, (((1,), (1,)), ((), ())), precis...]
    pallas_call x0 -> x1, Pallas kernels: none -> 9.87 us  [rows_times(): pl.pallas_call(rows_kernel, out_shape=jax.ShapeDtypeStruct((rows, weights...]
    unnamed x3 -> x2, local copies, waits for them, and re-layouts: 6.3 us -> 0.96 us
where the time goes in v1:
time: 112 us
  Pallas kernels  57.8 us (52%)
  waiting for transfers between devices  23.9 us (21%)
  starting transfers between devices  17.2 us (15%)
  matrix products  10.5 us (9%)
  local copies, waits for them, and re-layouts  1.39 us (1%)
    pallas_call x1, Pallas kernels, cholesky_and_inverse(): pl.pallas_call(chol_kernel, out_shape=(jax.ShapeDtypeStruct((n, n), jnp.f...  48 us
    ppermute x14, waiting for transfers between devices, partner_xor(): return lax.ppermute(value, axis, pairs)  23.9 us
    ppermute x14, starting transfers between devices, partner_xor(): return lax.ppermute(value, axis, pairs)  17.2 us
    dot_general x1, matrix products, gram_of(): lax.dot_general(matrix, matrix, (((0,), (0,)), ((), ())), precision=lax.P...  10.5 us
    pallas_call x1, Pallas kernels, rows_times(): pl.pallas_call(rows_kernel, out_shape=jax.ShapeDtypeStruct((rows, weights...  9.87 us
  transfers between devices with their start and end apart: 14, of which 11 were waited for; matrix products, arithmetic and copies ran while one was open for 0% of the time, Pallas kernels for 0%

profile of v1, /device:TPU:0, one launch (start us, length us, event | category | flops | bytes accessed | tf_op | source)
XLA Modules:
  0.0 111.8 jit_solution(8419091588113564885)
XLA Ops:
  0.6 10.5 %convolution_multiply_fusion = f32[512,512]{1,0:T(8,128)S(1)} fusion(f32[2048,512]{1,0:T(8,128)} %a_ref.1), kind=kOutput, calls=%fused_computation | convolution fusion | flops 6442713088 | bytes 5242880 | tf_op jit(solution)/shard_map/dot_general | solution.py:101
  11.2 0.5 collective-permute-start
  11.7 1.5 %collective-permute-done = f32[256,512]{1,0:T(8,128)S(1)} collective-permute-done((f32[256,512]{1,0:T(8,128)S(1)}, f32[256,512]{1,0:T(8,128)S(1)}, u32[]{:S(2)}, u32[]{:S(2)}) %collective-permute-start) | collective-permute-done | bytes 524320 | tf_op jit(solution)/shard_map/ppermute | solution.py:117
  13.4 2.9 %collective-permute-start.1 = (f32[64,512]{1,0:T(8,128)S(1)}, f32[64,512]{1,0:T(8,128)S(1)}, u32[]{:S(2)}, u32[]{:S(2)}) collective-permute-start(f32[64,512]{1,0:T(8,128)S(1)} %get-tuple-element.8), channel_id=1, source_target_pairs={{0,8},{8,0},{16,24},{24,16},{1,9},{9,1},{17,25},{25,17},{2,10},{10... | collective-permute-start | bytes 393224 | tf_op jit(solution)/shard_map/ppermute | solution.py:117
  16.3 1.5 %collective-permute-start.3 = (f32[64,512]{1,0:T(8,128)S(1)}, f32[64,512]{1,0:T(8,128)S(1)}, u32[]{:S(2)}, u32[]{:S(2)}) collective-permute-start(f32[64,512]{1,0:T(8,128)S(1)} %get-tuple-element.9), channel_id=1, source_target_pairs={{0,24},{8,16},{16,8},{24,0},{1,25},{9,17},{17,9},{25,1},{2,26},{10... | collective-permute-start | bytes 393224 | tf_op jit(solution)/shard_map/ppermute | solution.py:117
  17.8 2.6 %collective-permute-done.1 = f32[64,512]{1,0:T(8,128)S(1)} collective-permute-done((f32[64,512]{1,0:T(8,128)S(1)}, f32[64,512]{1,0:T(8,128)S(1)}, u32[]{:S(2)}, u32[]{:S(2)}) %collective-permute-start.1) | collective-permute-done | bytes 131104 | tf_op jit(solution)/shard_map/ppermute | solution.py:117
  20.4 3.8 %collective-permute-done.3 = f32[64,512]{1,0:T(8,128)S(1)} collective-permute-done((f32[64,512]{1,0:T(8,128)S(1)}, f32[64,512]{1,0:T(8,128)S(1)}, u32[]{:S(2)}, u32[]{:S(2)}) %collective-permute-start.3) | collective-permute-done | bytes 131104 | tf_op jit(solution)/shard_map/ppermute | solution.py:117
  24.2 1.4 %collective-permute-done.2 = f32[64,512]{1,0:T(8,128)S(1)} collective-permute-done((f32[64,512]{1,0:T(8,128)S(1)}, f32[64,512]{1,0:T(8,128)S(1)}, u32[]{:S(2)}, u32[]{:S(2)}) %collective-permute-start.2) | collective-permute-done | bytes 131104 | tf_op jit(solution)/shard_map/ppermute | solution.py:117
  25.7 1.6 %collective-permute-start.4 = (f32[16,512]{1,0:T(8,128)S(1)}, f32[16,512]{1,0:T(8,128)S(1)}, u32[]{:S(2)}, u32[]{:S(2)}) collective-permute-start(f32[16,512]{1,0:T(8,128)S(1)} %get-tuple-element.11), channel_id=1, source_target_pairs={{0,2},{1,3},{2,0},{3,1},{4,6},{5,7},{6,4},{7,5},{8,10},{9,11},{10,... | collective-permute-start | bytes 98312 | tf_op jit(solution)/shard_map/ppermute | solution.py:117
  27.3 2.5 %collective-permute-start.6 = (f32[16,512]{1,0:T(8,128)S(1)}, f32[16,512]{1,0:T(8,128)S(1)}, u32[]{:S(2)}, u32[]{:S(2)}) collective-permute-start(f32[16,512]{1,0:T(8,128)S(1)} %get-tuple-element.12), channel_id=1, source_target_pairs={{0,6},{1,7},{2,4},{3,5},{4,2},{5,3},{6,0},{7,1},{8,14},{9,15},{10,... | collective-permute-start | bytes 98312 | tf_op jit(solution)/shard_map/ppermute | solution.py:117
  29.9 3.1 %collective-permute-done.6 = f32[16,512]{1,0:T(8,128)S(1)} collective-permute-done((f32[16,512]{1,0:T(8,128)S(1)}, f32[16,512]{1,0:T(8,128)S(1)}, u32[]{:S(2)}, u32[]{:S(2)}) %collective-permute-start.6) | collective-permute-done | bytes 32800 | tf_op jit(solution)/shard_map/ppermute | solution.py:117
  33.0 1.9 %collective-permute-done.5 = f32[16,512]{1,0:T(8,128)S(1)} collective-permute-done((f32[16,512]{1,0:T(8,128)S(1)}, f32[16,512]{1,0:T(8,128)S(1)}, u32[]{:S(2)}, u32[]{:S(2)}) %collective-permute-start.5) | collective-permute-done | bytes 32800 | tf_op jit(solution)/shard_map/ppermute | solution.py:117
  35.5 1.4 %collective-permute-start.8 = (f32[16,512]{1,0:T(8,128)S(1)}, f32[16,512]{1,0:T(8,128)S(1)}, u32[]{:S(2)}, u32[]{:S(2)}) collective-permute-start(f32[16,512]{1,0:T(8,128)S(1)} %get-tuple-element.7), channel_id=1, source_target_pairs={{0,4},{1,5},{2,6},{3,7},{4,0},{5,1},{6,2},{7,3},{8,12},{9,13},{10,... | collective-permute-start | bytes 98312 | tf_op jit(solution)/shard_map/ppermute | solution.py:117
  36.9 2.6 %collective-permute-start.9 = (f32[16,512]{1,0:T(8,128)S(1)}, f32[16,512]{1,0:T(8,128)S(1)}, u32[]{:S(2)}, u32[]{:S(2)}) collective-permute-start(f32[16,512]{1,0:T(8,128)S(1)} %get-tuple-element.7), channel_id=1, source_target_pairs={{0,6},{1,7},{2,4},{3,5},{4,2},{5,3},{6,0},{7,1},{8,14},{9,15},{10,... | collective-permute-start | bytes 98312 | tf_op jit(solution)/shard_map/ppermute | solution.py:117
  39.4 0.8 collective-permute-done.8
  40.3 2.3 %collective-permute-done.9 = f32[16,512]{1,0:T(8,128)S(1)} collective-permute-done((f32[16,512]{1,0:T(8,128)S(1)}, f32[16,512]{1,0:T(8,128)S(1)}, u32[]{:S(2)}, u32[]{:S(2)}) %collective-permute-start.9) | collective-permute-done | bytes 32800 | tf_op jit(solution)/shard_map/ppermute | solution.py:117
  42.6 1.5 %collective-permute-start.10 = (f32[64,512]{1,0:T(8,128)S(1)}, f32[64,512]{1,0:T(8,128)S(1)}, u32[]{:S(2)}, u32[]{:S(2)}) collective-permute-start(f32[64,512]{1,0:T(8,128)S(1)} %constant_dynamic-update-slice_fusion.6), channel_id=1, source_target_pairs={{0,8},{8,0},{16,24},{24,16},{1,9},{9,1},{17,25},{25,17},{2,10},{10... | collective-permute-start | bytes 393224 | tf_op jit(solution)/shard_map/ppermute | solution.py:117
  44.5 1.5 %collective-permute-start.11 = (f32[64,512]{1,0:T(8,128)S(1)}, f32[64,512]{1,0:T(8,128)S(1)}, u32[]{:S(2)}, u32[]{:S(2)}) collective-permute-start(f32[64,512]{1,0:T(8,128)S(1)} %constant_dynamic-update-slice_fusion.6), channel_id=1, source_target_pairs={{0,16},{8,24},{16,0},{24,8},{1,17},{9,25},{17,1},{25,9},{2,18},{10... | collective-permute-start | bytes 393224 | tf_op jit(solution)/shard_map/ppermute | solution.py:117
  46.1 1.4 %collective-permute-done.10 = f32[64,512]{1,0:T(8,128)S(1)} collective-permute-done((f32[64,512]{1,0:T(8,128)S(1)}, f32[64,512]{1,0:T(8,128)S(1)}, u32[]{:S(2)}, u32[]{:S(2)}) %collective-permute-start.10) | collective-permute-done | bytes 131104 | tf_op jit(solution)/shard_map/ppermute | solution.py:117
  47.6 3.4 %collective-permute-done.11 = f32[64,512]{1,0:T(8,128)S(1)} collective-permute-done((f32[64,512]{1,0:T(8,128)S(1)}, f32[64,512]{1,0:T(8,128)S(1)}, u32[]{:S(2)}, u32[]{:S(2)}) %collective-permute-start.11) | collective-permute-done | bytes 131104 | tf_op jit(solution)/shard_map/ppermute | solution.py:117
  51.2 1.7 %collective-permute-done.13 = f32[256,512]{1,0:T(8,128)S(1)} collective-permute-done((f32[256,512]{1,0:T(8,128)S(1)}, f32[256,512]{1,0:T(8,128)S(1)}, u32[]{:S(2)}, u32[]{:S(2)}) %collective-permute-start.13) | collective-permute-done | bytes 524320 | tf_op jit(solution)/shard_map/ppermute | solution.py:117
  53.0 1.0 copy-done
  54.0 48.0 %shard_map.30 = (f32[512,512]{1,0:T(8,128)}, f32[512,512]{1,0:T(8,128)}) custom-call(f32[512,512]{1,0:T(8,128)} %copy-done), custom_call_target="tpu_custom_call" | custom-call | tf_op jit(solution)/shard_map/pallas_call | solution.py:68
  101.9 9.9 %shard_map.31 = f32[2048,512]{1,0:T(8,128)} custom-call(f32[2048,512]{1,0:T(8,128)} %a_ref.1, f32[512,512]{1,0:T(8,128)} %get-tuple-element.5.w_ref), custom_call_target="tpu_custom_call" | custom-call | tf_op jit(solution)/shard_map/pallas_call | solution.py:84
  (27 shorter events, 1.8 us)
Async XLA Ops:
  11.2 2.1 %collective-permute-start = (f32[256,512]{1,0:T(8,128)S(1)}, f32[256,512]{1,0:T(8,128)S(1)}, u32[]{:S(2)}, u32[]{:S(2)}) collective-permute-start(f32[256,512]{1,0:T(8,128)S(1)} %constant_dynamic-slice_fusion.6), channel_id=1, source_target_pairs={{0,1},{1,0},{2,3},{3,2},{4,5},{5,4},{6,7},{7,6},{8,9},{9,8},{10,11... | collective-permute-start | bytes 1572872 | tf_op jit(solution)/shard_map/ppermute | solution.py:117
  13.4 7.0 %collective-permute-start.1 = (f32[64,512]{1,0:T(8,128)S(1)}, f32[64,512]{1,0:T(8,128)S(1)}, u32[]{:S(2)}, u32[]{:S(2)}) collective-permute-start(f32[64,512]{1,0:T(8,128)S(1)} %get-tuple-element.8), channel_id=1, source_target_pairs={{0,8},{8,0},{16,24},{24,16},{1,9},{9,1},{17,25},{25,17},{2,10},{10... | collective-permute-start | bytes 393224 | tf_op jit(solution)/shard_map/ppermute | solution.py:117
  16.3 7.9 %collective-permute-start.3 = (f32[64,512]{1,0:T(8,128)S(1)}, f32[64,512]{1,0:T(8,128)S(1)}, u32[]{:S(2)}, u32[]{:S(2)}) collective-permute-start(f32[64,512]{1,0:T(8,128)S(1)} %get-tuple-element.9), channel_id=1, source_target_pairs={{0,24},{8,16},{16,8},{24,0},{1,25},{9,17},{17,9},{25,1},{2,26},{10... | collective-permute-start | bytes 393224 | tf_op jit(solution)/shard_map/ppermute | solution.py:117
  17.8 7.8 %collective-permute-start.2 = (f32[64,512]{1,0:T(8,128)S(1)}, f32[64,512]{1,0:T(8,128)S(1)}, u32[]{:S(2)}, u32[]{:S(2)}) collective-permute-start(f32[64,512]{1,0:T(8,128)S(1)} %get-tuple-element.10), channel_id=1, source_target_pairs={{0,16},{8,24},{16,0},{24,8},{1,17},{9,25},{17,1},{25,9},{2,18},{10... | collective-permute-start | bytes 393224 | tf_op jit(solution)/shard_map/ppermute | solution.py:117
  25.7 4.2 %collective-permute-start.4 = (f32[16,512]{1,0:T(8,128)S(1)}, f32[16,512]{1,0:T(8,128)S(1)}, u32[]{:S(2)}, u32[]{:S(2)}) collective-permute-start(f32[16,512]{1,0:T(8,128)S(1)} %get-tuple-element.11), channel_id=1, source_target_pairs={{0,2},{1,3},{2,0},{3,1},{4,6},{5,7},{6,4},{7,5},{8,10},{9,11},{10,... | collective-permute-start | bytes 98312 | tf_op jit(solution)/shard_map/ppermute | solution.py:117
  27.3 5.7 %collective-permute-start.6 = (f32[16,512]{1,0:T(8,128)S(1)}, f32[16,512]{1,0:T(8,128)S(1)}, u32[]{:S(2)}, u32[]{:S(2)}) collective-permute-start(f32[16,512]{1,0:T(8,128)S(1)} %get-tuple-element.12), channel_id=1, source_target_pairs={{0,6},{1,7},{2,4},{3,5},{4,2},{5,3},{6,0},{7,1},{8,14},{9,15},{10,... | collective-permute-start | bytes 98312 | tf_op jit(solution)/shard_map/ppermute | solution.py:117
  29.8 5.2 %collective-permute-start.5 = (f32[16,512]{1,0:T(8,128)S(1)}, f32[16,512]{1,0:T(8,128)S(1)}, u32[]{:S(2)}, u32[]{:S(2)}) collective-permute-start(f32[16,512]{1,0:T(8,128)S(1)} %get-tuple-element.13), channel_id=1, source_target_pairs={{0,4},{1,5},{2,6},{3,7},{4,0},{5,1},{6,2},{7,3},{8,12},{9,13},{10,... | collective-permute-start | bytes 98312 | tf_op jit(solution)/shard_map/ppermute | solution.py:117
  35.0 4.5 %collective-permute-start.7 = (f32[16,512]{1,0:T(8,128)S(1)}, f32[16,512]{1,0:T(8,128)S(1)}, u32[]{:S(2)}, u32[]{:S(2)}) collective-permute-start(f32[16,512]{1,0:T(8,128)S(1)} %get-tuple-element.7), channel_id=1, source_target_pairs={{0,2},{1,3},{2,0},{3,1},{4,6},{5,7},{6,4},{7,5},{8,10},{9,11},{10,... | collective-permute-start | bytes 98312 | tf_op jit(solution)/shard_map/ppermute | solution.py:117
  35.5 4.8 %collective-permute-start.8 = (f32[16,512]{1,0:T(8,128)S(1)}, f32[16,512]{1,0:T(8,128)S(1)}, u32[]{:S(2)}, u32[]{:S(2)}) collective-permute-start(f32[16,512]{1,0:T(8,128)S(1)} %get-tuple-element.7), channel_id=1, source_target_pairs={{0,4},{1,5},{2,6},{3,7},{4,0},{5,1},{6,2},{7,3},{8,12},{9,13},{10,... | collective-permute-start | bytes 98312 | tf_op jit(solution)/shard_map/ppermute | solution.py:117
  36.9 5.7 %collective-permute-start.9 = (f32[16,512]{1,0:T(8,128)S(1)}, f32[16,512]{1,0:T(8,128)S(1)}, u32[]{:S(2)}, u32[]{:S(2)}) collective-permute-start(f32[16,512]{1,0:T(8,128)S(1)} %get-tuple-element.7), channel_id=1, source_target_pairs={{0,6},{1,7},{2,4},{3,5},{4,2},{5,3},{6,0},{7,1},{8,14},{9,15},{10,... | collective-permute-start | bytes 98312 | tf_op jit(solution)/shard_map/ppermute | solution.py:117
  42.6 5.0 %collective-permute-start.10 = (f32[64,512]{1,0:T(8,128)S(1)}, f32[64,512]{1,0:T(8,128)S(1)}, u32[]{:S(2)}, u32[]{:S(2)}) collective-permute-start(f32[64,512]{1,0:T(8,128)S(1)} %constant_dynamic-update-slice_fusion.6), channel_id=1, source_target_pairs={{0,8},{8,0},{16,24},{24,16},{1,9},{9,1},{17,25},{25,17},{2,10},{10... | collective-permute-start | bytes 393224 | tf_op jit(solution)/shard_map/ppermute | solution.py:117
  44.1 6.9 %collective-permute-start.12 = (f32[64,512]{1,0:T(8,128)S(1)}, f32[64,512]{1,0:T(8,128)S(1)}, u32[]{:S(2)}, u32[]{:S(2)}) collective-permute-start(f32[64,512]{1,0:T(8,128)S(1)} %constant_dynamic-update-slice_fusion.6), channel_id=1, source_target_pairs={{0,24},{8,16},{16,8},{24,0},{1,25},{9,17},{17,9},{25,1},{2,26},{10... | collective-permute-start | bytes 393224 | tf_op jit(solution)/shard_map/ppermute | solution.py:117
  44.5 6.4 %collective-permute-start.11 = (f32[64,512]{1,0:T(8,128)S(1)}, f32[64,512]{1,0:T(8,128)S(1)}, u32[]{:S(2)}, u32[]{:S(2)}) collective-permute-start(f32[64,512]{1,0:T(8,128)S(1)} %constant_dynamic-update-slice_fusion.6), channel_id=1, source_target_pairs={{0,16},{8,24},{16,0},{24,8},{1,17},{9,25},{17,1},{25,9},{2,18},{10... | collective-permute-start | bytes 393224 | tf_op jit(solution)/shard_map/ppermute | solution.py:117
  51.0 2.0 %collective-permute-start.13 = (f32[256,512]{1,0:T(8,128)S(1)}, f32[256,512]{1,0:T(8,128)S(1)}, u32[]{:S(2)}, u32[]{:S(2)}) collective-permute-start(f32[256,512]{1,0:T(8,128)S(1)} %constant_dynamic-update-slice_fusion.2), channel_id=1, source_target_pairs={{0,1},{1,0},{2,3},{3,2},{4,5},{5,4},{6,7},{7,6},{8,9},{9,8},{10,11... | collective-permute-start | bytes 1572872 | tf_op jit(solution)/shard_map/ppermute | solution.py:117
  53.0 1.0 copy-start

commit v2 on v1

--- a/solution.py
+++ b/solution.py
@@ -75,7 +75,10 @@
 
 
 def rows_kernel(a_ref, w_ref, o_ref):
-    o_ref[...] = hdot(a_ref[...], w_ref[...])
+    width = w_ref.shape[1]
+    half = width // 2
+    o_ref[:, 0:half] = hdot(a_ref[:, 0:half], w_ref[0:half, 0:half])
+    o_ref[:, half:width] = hdot(a_ref[...], w_ref[:, half:width])
 
 
 def rows_times(matrix, weights):
@@ -97,14 +100,22 @@
     return jnp.dot(left, right, precision=lax.Precision.HIGHEST, preferred_element_type=jnp.float32)
 
 
-def gram_of(matrix):
+def cross(left, right):
     return lax.dot_general(
-        matrix,
-        matrix,
+        left,
+        right,
         (((0,), (0,)), ((), ())),
         precision=lax.Precision.HIGHEST,
         preferred_element_type=jnp.float32,
     )
+
+
+def gram_of(matrix):
+    half = matrix.shape[1] // 2
+    first = cross(matrix, matrix[:, :half])
+    corner = cross(matrix[:, half:], matrix[:, half:])
+    second = jnp.concatenate([first[half:].T, corner], axis=0)
+    return jnp.concatenate([first, second], axis=1)
 
 
 def group_index(axis, shift, size):

time: 112 us -> 116 us (1.036)
  matrix products: 10.5 us -> 15.4 us
  Pallas kernels: 57.8 us -> 56.5 us
    dot_general x1 -> x2, matrix products: 10.5 us -> 15.4 us  [cross(): lax.dot_general(left, right, (((0,), (0,)), ((), ())), precision=lax.Prec...]
    pallas_call x1, Pallas kernels: 9.87 us -> 8.46 us  [rows_times(): pl.pallas_call(rows_kernel, out_shape=jax.ShapeDtypeStruct((rows, weights...]
where the time goes in v2:
time: 116 us
  Pallas kernels  56.5 us (49%)
  waiting for transfers between devices  23.9 us (21%)
  starting transfers between devices  17.2 us (15%)
  matrix products  15.4 us (13%)
  local copies, waits for them, and re-layouts  1.61 us (1%)
    pallas_call x1, Pallas kernels, cholesky_and_inverse(): pl.pallas_call(chol_kernel, out_shape=(jax.ShapeDtypeStruct((n, n), jnp.f...  48 us
    ppermute x14, waiting for transfers between devices, partner_xor(): return lax.ppermute(value, axis, pairs)  23.9 us
    ppermute x14, starting transfers between devices, partner_xor(): return lax.ppermute(value, axis, pairs)  17.2 us
    dot_general x2, matrix products, cross(): lax.dot_general(left, right, (((0,), (0,)), ((), ())), precision=lax.Prec...  15.4 us
    pallas_call x1, Pallas kernels, rows_times(): pl.pallas_call(rows_kernel, out_shape=jax.ShapeDtypeStruct((rows, weights...  8.46 us
  transfers between devices with their start and end apart: 14, of which 11 were waited for; matrix products, arithmetic and copies ran while one was open for 0% of the time, Pallas kernels for 0%

profile of v2, /device:TPU:0, one launch (start us, length us, event | category | flops | bytes accessed | tf_op | source)
XLA Modules:
  0.0 115.7 jit_solution(6667064770997168526)
XLA Ops:
  0.6 5.8 %fusion = f32[256,256]{1,0:T(8,128)S(1)} fusion(f32[2048,512]{1,0:T(8,128)} %a_ref.1), kind=kOutput, calls=%fused_computation | convolution fusion | flops 1610612736 | bytes 2359296 | tf_op jit(solution)/shard_map/dot_general | solution.py:104
  6.4 9.6 %fusion.2 = f32[512,256]{0,1:T(8,128)S(1)} fusion(f32[2048,512]{1,0:T(8,128)} %a_ref.1), kind=kOutput, calls=%fused_computation.2 | convolution fusion | flops 3221225472 | bytes 6815744 | tf_op jit(solution)/shard_map/dot_general | solution.py:104
  17.0 1.5 %collective-permute-done = f32[256,512]{1,0:T(8,128)S(1)} collective-permute-done((f32[256,512]{1,0:T(8,128)S(1)}, f32[256,512]{1,0:T(8,128)S(1)}, u32[]{:S(2)}, u32[]{:S(2)}) %collective-permute-start) | collective-permute-done | bytes 524320 | tf_op jit(solution)/shard_map/ppermute | solution.py:128
  18.6 2.9 %collective-permute-start.1 = (f32[64,512]{1,0:T(8,128)S(1)}, f32[64,512]{1,0:T(8,128)S(1)}, u32[]{:S(2)}, u32[]{:S(2)}) collective-permute-start(f32[64,512]{1,0:T(8,128)S(1)} %get-tuple-element.8), channel_id=1, source_target_pairs={{0,8},{8,0},{16,24},{24,16},{1,9},{9,1},{17,25},{25,17},{2,10},{10... | collective-permute-start | bytes 393224 | tf_op jit(solution)/shard_map/ppermute | solution.py:128
  21.6 1.5 %collective-permute-start.3 = (f32[64,512]{1,0:T(8,128)S(1)}, f32[64,512]{1,0:T(8,128)S(1)}, u32[]{:S(2)}, u32[]{:S(2)}) collective-permute-start(f32[64,512]{1,0:T(8,128)S(1)} %get-tuple-element.9), channel_id=1, source_target_pairs={{0,24},{8,16},{16,8},{24,0},{1,25},{9,17},{17,9},{25,1},{2,26},{10... | collective-permute-start | bytes 393224 | tf_op jit(solution)/shard_map/ppermute | solution.py:128
  23.1 2.6 %collective-permute-done.1 = f32[64,512]{1,0:T(8,128)S(1)} collective-permute-done((f32[64,512]{1,0:T(8,128)S(1)}, f32[64,512]{1,0:T(8,128)S(1)}, u32[]{:S(2)}, u32[]{:S(2)}) %collective-permute-start.1) | collective-permute-done | bytes 131104 | tf_op jit(solution)/shard_map/ppermute | solution.py:128
  25.7 3.8 %collective-permute-done.3 = f32[64,512]{1,0:T(8,128)S(1)} collective-permute-done((f32[64,512]{1,0:T(8,128)S(1)}, f32[64,512]{1,0:T(8,128)S(1)}, u32[]{:S(2)}, u32[]{:S(2)}) %collective-permute-start.3) | collective-permute-done | bytes 131104 | tf_op jit(solution)/shard_map/ppermute | solution.py:128
  29.5 1.4 %collective-permute-done.2 = f32[64,512]{1,0:T(8,128)S(1)} collective-permute-done((f32[64,512]{1,0:T(8,128)S(1)}, f32[64,512]{1,0:T(8,128)S(1)}, u32[]{:S(2)}, u32[]{:S(2)}) %collective-permute-start.2) | collective-permute-done | bytes 131104 | tf_op jit(solution)/shard_map/ppermute | solution.py:128
  30.9 1.6 %collective-permute-start.4 = (f32[16,512]{1,0:T(8,128)S(1)}, f32[16,512]{1,0:T(8,128)S(1)}, u32[]{:S(2)}, u32[]{:S(2)}) collective-permute-start(f32[16,512]{1,0:T(8,128)S(1)} %get-tuple-element.11), channel_id=1, source_target_pairs={{0,2},{1,3},{2,0},{3,1},{4,6},{5,7},{6,4},{7,5},{8,10},{9,11},{10,... | collective-permute-start | bytes 98312 | tf_op jit(solution)/shard_map/ppermute | solution.py:128
  32.5 2.5 %collective-permute-start.6 = (f32[16,512]{1,0:T(8,128)S(1)}, f32[16,512]{1,0:T(8,128)S(1)}, u32[]{:S(2)}, u32[]{:S(2)}) collective-permute-start(f32[16,512]{1,0:T(8,128)S(1)} %get-tuple-element.12), channel_id=1, source_target_pairs={{0,6},{1,7},{2,4},{3,5},{4,2},{5,3},{6,0},{7,1},{8,14},{9,15},{10,... | collective-permute-start | bytes 98312 | tf_op jit(solution)/shard_map/ppermute | solution.py:128
  35.1 3.1 %collective-permute-done.6 = f32[16,512]{1,0:T(8,128)S(1)} collective-permute-done((f32[16,512]{1,0:T(8,128)S(1)}, f32[16,512]{1,0:T(8,128)S(1)}, u32[]{:S(2)}, u32[]{:S(2)}) %collective-permute-start.6) | collective-permute-done | bytes 32800 | tf_op jit(solution)/shard_map/ppermute | solution.py:128
  38.3 1.9 %collective-permute-done.5 = f32[16,512]{1,0:T(8,128)S(1)} collective-permute-done((f32[16,512]{1,0:T(8,128)S(1)}, f32[16,512]{1,0:T(8,128)S(1)}, u32[]{:S(2)}, u32[]{:S(2)}) %collective-permute-start.5) | collective-permute-done | bytes 32800 | tf_op jit(solution)/shard_map/ppermute | solution.py:128
  40.7 1.4 %collective-permute-start.8 = (f32[16,512]{1,0:T(8,128)S(1)}, f32[16,512]{1,0:T(8,128)S(1)}, u32[]{:S(2)}, u32[]{:S(2)}) collective-permute-start(f32[16,512]{1,0:T(8,128)S(1)} %get-tuple-element.7), channel_id=1, source_target_pairs={{0,4},{1,5},{2,6},{3,7},{4,0},{5,1},{6,2},{7,3},{8,12},{9,13},{10,... | collective-permute-start | bytes 98312 | tf_op jit(solution)/shard_map/ppermute | solution.py:128
  42.1 2.6 %collective-permute-start.9 = (f32[16,512]{1,0:T(8,128)S(1)}, f32[16,512]{1,0:T(8,128)S(1)}, u32[]{:S(2)}, u32[]{:S(2)}) collective-permute-start(f32[16,512]{1,0:T(8,128)S(1)} %get-tuple-element.7), channel_id=1, source_target_pairs={{0,6},{1,7},{2,4},{3,5},{4,2},{5,3},{6,0},{7,1},{8,14},{9,15},{10,... | collective-permute-start | bytes 98312 | tf_op jit(solution)/shard_map/ppermute | solution.py:128
  44.7 0.8 collective-permute-done.8
  45.5 2.3 %collective-permute-done.9 = f32[16,512]{1,0:T(8,128)S(1)} collective-permute-done((f32[16,512]{1,0:T(8,128)S(1)}, f32[16,512]{1,0:T(8,128)S(1)}, u32[]{:S(2)}, u32[]{:S(2)}) %collective-permute-start.9) | collective-permute-done | bytes 32800 | tf_op jit(solution)/shard_map/ppermute | solution.py:128
  47.8 1.5 %collective-permute-start.10 = (f32[64,512]{1,0:T(8,128)S(1)}, f32[64,512]{1,0:T(8,128)S(1)}, u32[]{:S(2)}, u32[]{:S(2)}) collective-permute-start(f32[64,512]{1,0:T(8,128)S(1)} %constant_dynamic-update-slice_fusion.6), channel_id=1, source_target_pairs={{0,8},{8,0},{16,24},{24,16},{1,9},{9,1},{17,25},{25,17},{2,10},{10... | collective-permute-start | bytes 393224 | tf_op jit(solution)/shard_map/ppermute | solution.py:128
  49.8 1.5 %collective-permute-start.11 = (f32[64,512]{1,0:T(8,128)S(1)}, f32[64,512]{1,0:T(8,128)S(1)}, u32[]{:S(2)}, u32[]{:S(2)}) collective-permute-start(f32[64,512]{1,0:T(8,128)S(1)} %constant_dynamic-update-slice_fusion.6), channel_id=1, source_target_pairs={{0,16},{8,24},{16,0},{24,8},{1,17},{9,25},{17,1},{25,9},{2,18},{10... | collective-permute-start | bytes 393224 | tf_op jit(solution)/shard_map/ppermute | solution.py:128
  51.4 1.4 %collective-permute-done.10 = f32[64,512]{1,0:T(8,128)S(1)} collective-permute-done((f32[64,512]{1,0:T(8,128)S(1)}, f32[64,512]{1,0:T(8,128)S(1)}, u32[]{:S(2)}, u32[]{:S(2)}) %collective-permute-start.10) | collective-permute-done | bytes 131104 | tf_op jit(solution)/shard_map/ppermute | solution.py:128
  52.8 3.4 %collective-permute-done.11 = f32[64,512]{1,0:T(8,128)S(1)} collective-permute-done((f32[64,512]{1,0:T(8,128)S(1)}, f32[64,512]{1,0:T(8,128)S(1)}, u32[]{:S(2)}, u32[]{:S(2)}) %collective-permute-start.11) | collective-permute-done | bytes 131104 | tf_op jit(solution)/shard_map/ppermute | solution.py:128
  56.5 1.7 %collective-permute-done.13 = f32[256,512]{1,0:T(8,128)S(1)} collective-permute-done((f32[256,512]{1,0:T(8,128)S(1)}, f32[256,512]{1,0:T(8,128)S(1)}, u32[]{:S(2)}, u32[]{:S(2)}) %collective-permute-start.13) | collective-permute-done | bytes 524320 | tf_op jit(solution)/shard_map/ppermute | solution.py:128
  58.3 1.0 copy-done
  59.2 48.0 %shard_map.30 = (f32[512,512]{1,0:T(8,128)}, f32[512,512]{1,0:T(8,128)}) custom-call(f32[512,512]{1,0:T(8,128)} %copy-done), custom_call_target="tpu_custom_call" | custom-call | tf_op jit(solution)/shard_map/pallas_call | solution.py:68
  107.2 8.5 %shard_map.31 = f32[2048,512]{1,0:T(8,128)} custom-call(f32[2048,512]{1,0:T(8,128)} %a_ref.1, f32[512,512]{1,0:T(8,128)} %get-tuple-element.5.w_ref), custom_call_target="tpu_custom_call" | custom-call | tf_op jit(solution)/shard_map/pallas_call | solution.py:87
  (31 shorter events, 2.7 us)
Async XLA Ops:
  16.4 2.1 %collective-permute-start = (f32[256,512]{1,0:T(8,128)S(1)}, f32[256,512]{1,0:T(8,128)S(1)}, u32[]{:S(2)}, u32[]{:S(2)}) collective-permute-start(f32[256,512]{1,0:T(8,128)S(1)} %constant_dynamic-slice_fusion.6), channel_id=1, source_target_pairs={{0,1},{1,0},{2,3},{3,2},{4,5},{5,4},{6,7},{7,6},{8,9},{9,8},{10,11... | collective-permute-start | bytes 1572872 | tf_op jit(solution)/shard_map/ppermute | solution.py:128
  18.6 7.0 %collective-permute-start.1 = (f32[64,512]{1,0:T(8,128)S(1)}, f32[64,512]{1,0:T(8,128)S(1)}, u32[]{:S(2)}, u32[]{:S(2)}) collective-permute-start(f32[64,512]{1,0:T(8,128)S(1)} %get-tuple-element.8), channel_id=1, source_target_pairs={{0,8},{8,0},{16,24},{24,16},{1,9},{9,1},{17,25},{25,17},{2,10},{10... | collective-permute-start | bytes 393224 | tf_op jit(solution)/shard_map/ppermute | solution.py:128
  21.6 7.9 %collective-permute-start.3 = (f32[64,512]{1,0:T(8,128)S(1)}, f32[64,512]{1,0:T(8,128)S(1)}, u32[]{:S(2)}, u32[]{:S(2)}) collective-permute-start(f32[64,512]{1,0:T(8,128)S(1)} %get-tuple-element.9), channel_id=1, source_target_pairs={{0,24},{8,16},{16,8},{24,0},{1,25},{9,17},{17,9},{25,1},{2,26},{10... | collective-permute-start | bytes 393224 | tf_op jit(solution)/shard_map/ppermute | solution.py:128
  23.0 7.8 %collective-permute-start.2 = (f32[64,512]{1,0:T(8,128)S(1)}, f32[64,512]{1,0:T(8,128)S(1)}, u32[]{:S(2)}, u32[]{:S(2)}) collective-permute-start(f32[64,512]{1,0:T(8,128)S(1)} %get-tuple-element.10), channel_id=1, source_target_pairs={{0,16},{8,24},{16,0},{24,8},{1,17},{9,25},{17,1},{25,9},{2,18},{10... | collective-permute-start | bytes 393224 | tf_op jit(solution)/shard_map/ppermute | solution.py:128
  30.9 4.2 %collective-permute-start.4 = (f32[16,512]{1,0:T(8,128)S(1)}, f32[16,512]{1,0:T(8,128)S(1)}, u32[]{:S(2)}, u32[]{:S(2)}) collective-permute-start(f32[16,512]{1,0:T(8,128)S(1)} %get-tuple-element.11), channel_id=1, source_target_pairs={{0,2},{1,3},{2,0},{3,1},{4,6},{5,7},{6,4},{7,5},{8,10},{9,11},{10,... | collective-permute-start | bytes 98312 | tf_op jit(solution)/shard_map/ppermute | solution.py:128
  32.5 5.7 %collective-permute-start.6 = (f32[16,512]{1,0:T(8,128)S(1)}, f32[16,512]{1,0:T(8,128)S(1)}, u32[]{:S(2)}, u32[]{:S(2)}) collective-permute-start(f32[16,512]{1,0:T(8,128)S(1)} %get-tuple-element.12), channel_id=1, source_target_pairs={{0,6},{1,7},{2,4},{3,5},{4,2},{5,3},{6,0},{7,1},{8,14},{9,15},{10,... | collective-permute-start | bytes 98312 | tf_op jit(solution)/shard_map/ppermute | solution.py:128
  35.0 5.2 %collective-permute-start.5 = (f32[16,512]{1,0:T(8,128)S(1)}, f32[16,512]{1,0:T(8,128)S(1)}, u32[]{:S(2)}, u32[]{:S(2)}) collective-permute-start(f32[16,512]{1,0:T(8,128)S(1)} %get-tuple-element.13), channel_id=1, source_target_pairs={{0,4},{1,5},{2,6},{3,7},{4,0},{5,1},{6,2},{7,3},{8,12},{9,13},{10,... | collective-permute-start | bytes 98312 | tf_op jit(solution)/shard_map/ppermute | solution.py:128
  40.2 4.5 %collective-permute-start.7 = (f32[16,512]{1,0:T(8,128)S(1)}, f32[16,512]{1,0:T(8,128)S(1)}, u32[]{:S(2)}, u32[]{:S(2)}) collective-permute-start(f32[16,512]{1,0:T(8,128)S(1)} %get-tuple-element.7), channel_id=1, source_target_pairs={{0,2},{1,3},{2,0},{3,1},{4,6},{5,7},{6,4},{7,5},{8,10},{9,11},{10,... | collective-permute-start | bytes 98312 | tf_op jit(solution)/shard_map/ppermute | solution.py:128
  40.7 4.8 %collective-permute-start.8 = (f32[16,512]{1,0:T(8,128)S(1)}, f32[16,512]{1,0:T(8,128)S(1)}, u32[]{:S(2)}, u32[]{:S(2)}) collective-permute-start(f32[16,512]{1,0:T(8,128)S(1)} %get-tuple-element.7), channel_id=1, source_target_pairs={{0,4},{1,5},{2,6},{3,7},{4,0},{5,1},{6,2},{7,3},{8,12},{9,13},{10,... | collective-permute-start | bytes 98312 | tf_op jit(solution)/shard_map/ppermute | solution.py:128
  42.1 5.7 %collective-permute-start.9 = (f32[16,512]{1,0:T(8,128)S(1)}, f32[16,512]{1,0:T(8,128)S(1)}, u32[]{:S(2)}, u32[]{:S(2)}) collective-permute-start(f32[16,512]{1,0:T(8,128)S(1)} %get-tuple-element.7), channel_id=1, source_target_pairs={{0,6},{1,7},{2,4},{3,5},{4,2},{5,3},{6,0},{7,1},{8,14},{9,15},{10,... | collective-permute-start | bytes 98312 | tf_op jit(solution)/shard_map/ppermute | solution.py:128
  47.8 5.0 %collective-permute-start.10 = (f32[64,512]{1,0:T(8,128)S(1)}, f32[64,512]{1,0:T(8,128)S(1)}, u32[]{:S(2)}, u32[]{:S(2)}) collective-permute-start(f32[64,512]{1,0:T(8,128)S(1)} %constant_dynamic-update-slice_fusion.6), channel_id=1, source_target_pairs={{0,8},{8,0},{16,24},{24,16},{1,9},{9,1},{17,25},{25,17},{2,10},{10... | collective-permute-start | bytes 393224 | tf_op jit(solution)/shard_map/ppermute | solution.py:128
  49.3 6.9 %collective-permute-start.12 = (f32[64,512]{1,0:T(8,128)S(1)}, f32[64,512]{1,0:T(8,128)S(1)}, u32[]{:S(2)}, u32[]{:S(2)}) collective-permute-start(f32[64,512]{1,0:T(8,128)S(1)} %constant_dynamic-update-slice_fusion.6), channel_id=1, source_target_pairs={{0,24},{8,16},{16,8},{24,0},{1,25},{9,17},{17,9},{25,1},{2,26},{10... | collective-permute-start | bytes 393224 | tf_op jit(solution)/shard_map/ppermute | solution.py:128
  49.8 6.4 %collective-permute-start.11 = (f32[64,512]{1,0:T(8,128)S(1)}, f32[64,512]{1,0:T(8,128)S(1)}, u32[]{:S(2)}, u32[]{:S(2)}) collective-permute-start(f32[64,512]{1,0:T(8,128)S(1)} %constant_dynamic-update-slice_fusion.6), channel_id=1, source_target_pairs={{0,16},{8,24},{16,0},{24,8},{1,17},{9,25},{17,1},{25,9},{2,18},{10... | collective-permute-start | bytes 393224 | tf_op jit(solution)/shard_map/ppermute | solution.py:128
  56.2 2.0 %collective-permute-start.13 = (f32[256,512]{1,0:T(8,128)S(1)}, f32[256,512]{1,0:T(8,128)S(1)}, u32[]{:S(2)}, u32[]{:S(2)}) collective-permute-start(f32[256,512]{1,0:T(8,128)S(1)} %constant_dynamic-update-slice_fusion.2), channel_id=1, source_target_pairs={{0,1},{1,0},{2,3},{3,2},{4,5},{5,4},{6,7},{7,6},{8,9},{9,8},{10,11... | collective-permute-start | bytes 1572872 | tf_op jit(solution)/shard_map/ppermute | solution.py:128
  58.2 1.0 copy-start

commit v3 on v1

--- a/solution.py
+++ b/solution.py
@@ -75,7 +75,10 @@
 
 
 def rows_kernel(a_ref, w_ref, o_ref):
-    o_ref[...] = hdot(a_ref[...], w_ref[...])
+    width = w_ref.shape[1]
+    half = width // 2
+    o_ref[:, 0:half] = hdot(a_ref[:, 0:half], w_ref[0:half, 0:half])
+    o_ref[:, half:width] = hdot(a_ref[...], w_ref[:, half:width])
 
 
 def rows_times(matrix, weights):

time: 112 us -> 111 us (level)
  Pallas kernels: 57.8 us -> 56.4 us
    pallas_call x1, Pallas kernels: 9.87 us -> 8.46 us  [rows_times(): pl.pallas_call(rows_kernel, out_shape=jax.ShapeDtypeStruct((rows, weights...]
where the time goes in v3:
time: 111 us; the launch traced here: 110 us
  Pallas kernels  56.4 us (51%)
  waiting for transfers between devices  23.9 us (22%)
  starting transfers between devices  17.2 us (15%)
  matrix products  10.5 us (9%)
  local copies, waits for them, and re-layouts  1.39 us (1%)
    pallas_call x1, Pallas kernels, cholesky_and_inverse(): pl.pallas_call(chol_kernel, out_shape=(jax.ShapeDtypeStruct((n, n), jnp.f...  48 us
    ppermute x14, waiting for transfers between devices, partner_xor(): return lax.ppermute(value, axis, pairs)  23.9 us
    ppermute x14, starting transfers between devices, partner_xor(): return lax.ppermute(value, axis, pairs)  17.2 us
    dot_general x1, matrix products, gram_of(): lax.dot_general(matrix, matrix, (((0,), (0,)), ((), ())), precision=lax.P...  10.5 us
    pallas_call x1, Pallas kernels, rows_times(): pl.pallas_call(rows_kernel, out_shape=jax.ShapeDtypeStruct((rows, weights...  8.46 us
  transfers between devices with their start and end apart: 14, of which 11 were waited for; matrix products, arithmetic and copies ran while one was open for 0% of the time, Pallas kernels for 0%

profile of v3, /device:TPU:0, one launch (start us, length us, event | category | flops | bytes accessed | tf_op | source)
XLA Modules:
  0.0 110.4 jit_solution(10321260157433197910)
XLA Ops:
  0.6 10.5 %convolution_multiply_fusion = f32[512,512]{1,0:T(8,128)S(1)} fusion(f32[2048,512]{1,0:T(8,128)} %a_ref.1), kind=kOutput, calls=%fused_computation | convolution fusion | flops 6442713088 | bytes 5242880 | tf_op jit(solution)/shard_map/dot_general | solution.py:104
  11.2 0.5 collective-permute-start
  11.7 1.5 %collective-permute-done = f32[256,512]{1,0:T(8,128)S(1)} collective-permute-done((f32[256,512]{1,0:T(8,128)S(1)}, f32[256,512]{1,0:T(8,128)S(1)}, u32[]{:S(2)}, u32[]{:S(2)}) %collective-permute-start) | collective-permute-done | bytes 524320 | tf_op jit(solution)/shard_map/ppermute | solution.py:120
  13.4 2.9 %collective-permute-start.1 = (f32[64,512]{1,0:T(8,128)S(1)}, f32[64,512]{1,0:T(8,128)S(1)}, u32[]{:S(2)}, u32[]{:S(2)}) collective-permute-start(f32[64,512]{1,0:T(8,128)S(1)} %get-tuple-element.8), channel_id=1, source_target_pairs={{0,8},{8,0},{16,24},{24,16},{1,9},{9,1},{17,25},{25,17},{2,10},{10... | collective-permute-start | bytes 393224 | tf_op jit(solution)/shard_map/ppermute | solution.py:120
  16.3 1.5 %collective-permute-start.3 = (f32[64,512]{1,0:T(8,128)S(1)}, f32[64,512]{1,0:T(8,128)S(1)}, u32[]{:S(2)}, u32[]{:S(2)}) collective-permute-start(f32[64,512]{1,0:T(8,128)S(1)} %get-tuple-element.9), channel_id=1, source_target_pairs={{0,24},{8,16},{16,8},{24,0},{1,25},{9,17},{17,9},{25,1},{2,26},{10... | collective-permute-start | bytes 393224 | tf_op jit(solution)/shard_map/ppermute | solution.py:120
  17.8 2.6 %collective-permute-done.1 = f32[64,512]{1,0:T(8,128)S(1)} collective-permute-done((f32[64,512]{1,0:T(8,128)S(1)}, f32[64,512]{1,0:T(8,128)S(1)}, u32[]{:S(2)}, u32[]{:S(2)}) %collective-permute-start.1) | collective-permute-done | bytes 131104 | tf_op jit(solution)/shard_map/ppermute | solution.py:120
  20.4 3.8 %collective-permute-done.3 = f32[64,512]{1,0:T(8,128)S(1)} collective-permute-done((f32[64,512]{1,0:T(8,128)S(1)}, f32[64,512]{1,0:T(8,128)S(1)}, u32[]{:S(2)}, u32[]{:S(2)}) %collective-permute-start.3) | collective-permute-done | bytes 131104 | tf_op jit(solution)/shard_map/ppermute | solution.py:120
  24.2 1.4 %collective-permute-done.2 = f32[64,512]{1,0:T(8,128)S(1)} collective-permute-done((f32[64,512]{1,0:T(8,128)S(1)}, f32[64,512]{1,0:T(8,128)S(1)}, u32[]{:S(2)}, u32[]{:S(2)}) %collective-permute-start.2) | collective-permute-done | bytes 131104 | tf_op jit(solution)/shard_map/ppermute | solution.py:120
  25.7 1.6 %collective-permute-start.4 = (f32[16,512]{1,0:T(8,128)S(1)}, f32[16,512]{1,0:T(8,128)S(1)}, u32[]{:S(2)}, u32[]{:S(2)}) collective-permute-start(f32[16,512]{1,0:T(8,128)S(1)} %get-tuple-element.11), channel_id=1, source_target_pairs={{0,2},{1,3},{2,0},{3,1},{4,6},{5,7},{6,4},{7,5},{8,10},{9,11},{10,... | collective-permute-start | bytes 98312 | tf_op jit(solution)/shard_map/ppermute | solution.py:120
  27.3 2.5 %collective-permute-start.6 = (f32[16,512]{1,0:T(8,128)S(1)}, f32[16,512]{1,0:T(8,128)S(1)}, u32[]{:S(2)}, u32[]{:S(2)}) collective-permute-start(f32[16,512]{1,0:T(8,128)S(1)} %get-tuple-element.12), channel_id=1, source_target_pairs={{0,6},{1,7},{2,4},{3,5},{4,2},{5,3},{6,0},{7,1},{8,14},{9,15},{10,... | collective-permute-start | bytes 98312 | tf_op jit(solution)/shard_map/ppermute | solution.py:120
  29.9 3.1 %collective-permute-done.6 = f32[16,512]{1,0:T(8,128)S(1)} collective-permute-done((f32[16,512]{1,0:T(8,128)S(1)}, f32[16,512]{1,0:T(8,128)S(1)}, u32[]{:S(2)}, u32[]{:S(2)}) %collective-permute-start.6) | collective-permute-done | bytes 32800 | tf_op jit(solution)/shard_map/ppermute | solution.py:120
  33.0 1.9 %collective-permute-done.5 = f32[16,512]{1,0:T(8,128)S(1)} collective-permute-done((f32[16,512]{1,0:T(8,128)S(1)}, f32[16,512]{1,0:T(8,128)S(1)}, u32[]{:S(2)}, u32[]{:S(2)}) %collective-permute-start.5) | collective-permute-done | bytes 32800 | tf_op jit(solution)/shard_map/ppermute | solution.py:120
  35.5 1.4 %collective-permute-start.8 = (f32[16,512]{1,0:T(8,128)S(1)}, f32[16,512]{1,0:T(8,128)S(1)}, u32[]{:S(2)}, u32[]{:S(2)}) collective-permute-start(f32[16,512]{1,0:T(8,128)S(1)} %get-tuple-element.7), channel_id=1, source_target_pairs={{0,4},{1,5},{2,6},{3,7},{4,0},{5,1},{6,2},{7,3},{8,12},{9,13},{10,... | collective-permute-start | bytes 98312 | tf_op jit(solution)/shard_map/ppermute | solution.py:120
  36.9 2.6 %collective-permute-start.9 = (f32[16,512]{1,0:T(8,128)S(1)}, f32[16,512]{1,0:T(8,128)S(1)}, u32[]{:S(2)}, u32[]{:S(2)}) collective-permute-start(f32[16,512]{1,0:T(8,128)S(1)} %get-tuple-element.7), channel_id=1, source_target_pairs={{0,6},{1,7},{2,4},{3,5},{4,2},{5,3},{6,0},{7,1},{8,14},{9,15},{10,... | collective-permute-start | bytes 98312 | tf_op jit(solution)/shard_map/ppermute | solution.py:120
  39.4 0.8 collective-permute-done.8
  40.3 2.3 %collective-permute-done.9 = f32[16,512]{1,0:T(8,128)S(1)} collective-permute-done((f32[16,512]{1,0:T(8,128)S(1)}, f32[16,512]{1,0:T(8,128)S(1)}, u32[]{:S(2)}, u32[]{:S(2)}) %collective-permute-start.9) | collective-permute-done | bytes 32800 | tf_op jit(solution)/shard_map/ppermute | solution.py:120
  42.6 1.5 %collective-permute-start.10 = (f32[64,512]{1,0:T(8,128)S(1)}, f32[64,512]{1,0:T(8,128)S(1)}, u32[]{:S(2)}, u32[]{:S(2)}) collective-permute-start(f32[64,512]{1,0:T(8,128)S(1)} %constant_dynamic-update-slice_fusion.6), channel_id=1, source_target_pairs={{0,8},{8,0},{16,24},{24,16},{1,9},{9,1},{17,25},{25,17},{2,10},{10... | collective-permute-start | bytes 393224 | tf_op jit(solution)/shard_map/ppermute | solution.py:120
  44.5 1.5 %collective-permute-start.11 = (f32[64,512]{1,0:T(8,128)S(1)}, f32[64,512]{1,0:T(8,128)S(1)}, u32[]{:S(2)}, u32[]{:S(2)}) collective-permute-start(f32[64,512]{1,0:T(8,128)S(1)} %constant_dynamic-update-slice_fusion.6), channel_id=1, source_target_pairs={{0,16},{8,24},{16,0},{24,8},{1,17},{9,25},{17,1},{25,9},{2,18},{10... | collective-permute-start | bytes 393224 | tf_op jit(solution)/shard_map/ppermute | solution.py:120
  46.1 1.4 %collective-permute-done.10 = f32[64,512]{1,0:T(8,128)S(1)} collective-permute-done((f32[64,512]{1,0:T(8,128)S(1)}, f32[64,512]{1,0:T(8,128)S(1)}, u32[]{:S(2)}, u32[]{:S(2)}) %collective-permute-start.10) | collective-permute-done | bytes 131104 | tf_op jit(solution)/shard_map/ppermute | solution.py:120
  47.6 3.4 %collective-permute-done.11 = f32[64,512]{1,0:T(8,128)S(1)} collective-permute-done((f32[64,512]{1,0:T(8,128)S(1)}, f32[64,512]{1,0:T(8,128)S(1)}, u32[]{:S(2)}, u32[]{:S(2)}) %collective-permute-start.11) | collective-permute-done | bytes 131104 | tf_op jit(solution)/shard_map/ppermute | solution.py:120
  51.2 1.7 %collective-permute-done.13 = f32[256,512]{1,0:T(8,128)S(1)} collective-permute-done((f32[256,512]{1,0:T(8,128)S(1)}, f32[256,512]{1,0:T(8,128)S(1)}, u32[]{:S(2)}, u32[]{:S(2)}) %collective-permute-start.13) | collective-permute-done | bytes 524320 | tf_op jit(solution)/shard_map/ppermute | solution.py:120
  53.0 1.0 copy-done
  54.0 48.0 %shard_map.30 = (f32[512,512]{1,0:T(8,128)}, f32[512,512]{1,0:T(8,128)}) custom-call(f32[512,512]{1,0:T(8,128)} %copy-done), custom_call_target="tpu_custom_call" | custom-call | tf_op jit(solution)/shard_map/pallas_call | solution.py:68
  101.9 8.5 %shard_map.31 = f32[2048,512]{1,0:T(8,128)} custom-call(f32[2048,512]{1,0:T(8,128)} %a_ref.1, f32[512,512]{1,0:T(8,128)} %get-tuple-element.5.w_ref), custom_call_target="tpu_custom_call" | custom-call | tf_op jit(solution)/shard_map/pallas_call | solution.py:87
  (27 shorter events, 1.8 us)
Async XLA Ops:
  11.2 2.1 %collective-permute-start = (f32[256,512]{1,0:T(8,128)S(1)}, f32[256,512]{1,0:T(8,128)S(1)}, u32[]{:S(2)}, u32[]{:S(2)}) collective-permute-start(f32[256,512]{1,0:T(8,128)S(1)} %constant_dynamic-slice_fusion.6), channel_id=1, source_target_pairs={{0,1},{1,0},{2,3},{3,2},{4,5},{5,4},{6,7},{7,6},{8,9},{9,8},{10,11... | collective-permute-start | bytes 1572872 | tf_op jit(solution)/shard_map/ppermute | solution.py:120
  13.4 7.0 %collective-permute-start.1 = (f32[64,512]{1,0:T(8,128)S(1)}, f32[64,512]{1,0:T(8,128)S(1)}, u32[]{:S(2)}, u32[]{:S(2)}) collective-permute-start(f32[64,512]{1,0:T(8,128)S(1)} %get-tuple-element.8), channel_id=1, source_target_pairs={{0,8},{8,0},{16,24},{24,16},{1,9},{9,1},{17,25},{25,17},{2,10},{10... | collective-permute-start | bytes 393224 | tf_op jit(solution)/shard_map/ppermute | solution.py:120
  16.3 7.9 %collective-permute-start.3 = (f32[64,512]{1,0:T(8,128)S(1)}, f32[64,512]{1,0:T(8,128)S(1)}, u32[]{:S(2)}, u32[]{:S(2)}) collective-permute-start(f32[64,512]{1,0:T(8,128)S(1)} %get-tuple-element.9), channel_id=1, source_target_pairs={{0,24},{8,16},{16,8},{24,0},{1,25},{9,17},{17,9},{25,1},{2,26},{10... | collective-permute-start | bytes 393224 | tf_op jit(solution)/shard_map/ppermute | solution.py:120
  17.8 7.8 %collective-permute-start.2 = (f32[64,512]{1,0:T(8,128)S(1)}, f32[64,512]{1,0:T(8,128)S(1)}, u32[]{:S(2)}, u32[]{:S(2)}) collective-permute-start(f32[64,512]{1,0:T(8,128)S(1)} %get-tuple-element.10), channel_id=1, source_target_pairs={{0,16},{8,24},{16,0},{24,8},{1,17},{9,25},{17,1},{25,9},{2,18},{10... | collective-permute-start | bytes 393224 | tf_op jit(solution)/shard_map/ppermute | solution.py:120
  25.7 4.2 %collective-permute-start.4 = (f32[16,512]{1,0:T(8,128)S(1)}, f32[16,512]{1,0:T(8,128)S(1)}, u32[]{:S(2)}, u32[]{:S(2)}) collective-permute-start(f32[16,512]{1,0:T(8,128)S(1)} %get-tuple-element.11), channel_id=1, source_target_pairs={{0,2},{1,3},{2,0},{3,1},{4,6},{5,7},{6,4},{7,5},{8,10},{9,11},{10,... | collective-permute-start | bytes 98312 | tf_op jit(solution)/shard_map/ppermute | solution.py:120
  27.3 5.7 %collective-permute-start.6 = (f32[16,512]{1,0:T(8,128)S(1)}, f32[16,512]{1,0:T(8,128)S(1)}, u32[]{:S(2)}, u32[]{:S(2)}) collective-permute-start(f32[16,512]{1,0:T(8,128)S(1)} %get-tuple-element.12), channel_id=1, source_target_pairs={{0,6},{1,7},{2,4},{3,5},{4,2},{5,3},{6,0},{7,1},{8,14},{9,15},{10,... | collective-permute-start | bytes 98312 | tf_op jit(solution)/shard_map/ppermute | solution.py:120
  29.8 5.2 %collective-permute-start.5 = (f32[16,512]{1,0:T(8,128)S(1)}, f32[16,512]{1,0:T(8,128)S(1)}, u32[]{:S(2)}, u32[]{:S(2)}) collective-permute-start(f32[16,512]{1,0:T(8,128)S(1)} %get-tuple-element.13), channel_id=1, source_target_pairs={{0,4},{1,5},{2,6},{3,7},{4,0},{5,1},{6,2},{7,3},{8,12},{9,13},{10,... | collective-permute-start | bytes 98312 | tf_op jit(solution)/shard_map/ppermute | solution.py:120
  35.0 4.5 %collective-permute-start.7 = (f32[16,512]{1,0:T(8,128)S(1)}, f32[16,512]{1,0:T(8,128)S(1)}, u32[]{:S(2)}, u32[]{:S(2)}) collective-permute-start(f32[16,512]{1,0:T(8,128)S(1)} %get-tuple-element.7), channel_id=1, source_target_pairs={{0,2},{1,3},{2,0},{3,1},{4,6},{5,7},{6,4},{7,5},{8,10},{9,11},{10,... | collective-permute-start | bytes 98312 | tf_op jit(solution)/shard_map/ppermute | solution.py:120
  35.5 4.8 %collective-permute-start.8 = (f32[16,512]{1,0:T(8,128)S(1)}, f32[16,512]{1,0:T(8,128)S(1)}, u32[]{:S(2)}, u32[]{:S(2)}) collective-permute-start(f32[16,512]{1,0:T(8,128)S(1)} %get-tuple-element.7), channel_id=1, source_target_pairs={{0,4},{1,5},{2,6},{3,7},{4,0},{5,1},{6,2},{7,3},{8,12},{9,13},{10,... | collective-permute-start | bytes 98312 | tf_op jit(solution)/shard_map/ppermute | solution.py:120
  36.9 5.7 %collective-permute-start.9 = (f32[16,512]{1,0:T(8,128)S(1)}, f32[16,512]{1,0:T(8,128)S(1)}, u32[]{:S(2)}, u32[]{:S(2)}) collective-permute-start(f32[16,512]{1,0:T(8,128)S(1)} %get-tuple-element.7), channel_id=1, source_target_pairs={{0,6},{1,7},{2,4},{3,5},{4,2},{5,3},{6,0},{7,1},{8,14},{9,15},{10,... | collective-permute-start | bytes 98312 | tf_op jit(solution)/shard_map/ppermute | solution.py:120
  42.6 5.0 %collective-permute-start.10 = (f32[64,512]{1,0:T(8,128)S(1)}, f32[64,512]{1,0:T(8,128)S(1)}, u32[]{:S(2)}, u32[]{:S(2)}) collective-permute-start(f32[64,512]{1,0:T(8,128)S(1)} %constant_dynamic-update-slice_fusion.6), channel_id=1, source_target_pairs={{0,8},{8,0},{16,24},{24,16},{1,9},{9,1},{17,25},{25,17},{2,10},{10... | collective-permute-start | bytes 393224 | tf_op jit(solution)/shard_map/ppermute | solution.py:120
  44.1 6.9 %collective-permute-start.12 = (f32[64,512]{1,0:T(8,128)S(1)}, f32[64,512]{1,0:T(8,128)S(1)}, u32[]{:S(2)}, u32[]{:S(2)}) collective-permute-start(f32[64,512]{1,0:T(8,128)S(1)} %constant_dynamic-update-slice_fusion.6), channel_id=1, source_target_pairs={{0,24},{8,16},{16,8},{24,0},{1,25},{9,17},{17,9},{25,1},{2,26},{10... | collective-permute-start | bytes 393224 | tf_op jit(solution)/shard_map/ppermute | solution.py:120
  44.5 6.4 %collective-permute-start.11 = (f32[64,512]{1,0:T(8,128)S(1)}, f32[64,512]{1,0:T(8,128)S(1)}, u32[]{:S(2)}, u32[]{:S(2)}) collective-permute-start(f32[64,512]{1,0:T(8,128)S(1)} %constant_dynamic-update-slice_fusion.6), channel_id=1, source_target_pairs={{0,16},{8,24},{16,0},{24,8},{1,17},{9,25},{17,1},{25,9},{2,18},{10... | collective-permute-start | bytes 393224 | tf_op jit(solution)/shard_map/ppermute | solution.py:120
  51.0 2.0 %collective-permute-start.13 = (f32[256,512]{1,0:T(8,128)S(1)}, f32[256,512]{1,0:T(8,128)S(1)}, u32[]{:S(2)}, u32[]{:S(2)}) collective-permute-start(f32[256,512]{1,0:T(8,128)S(1)} %constant_dynamic-update-slice_fusion.2), channel_id=1, source_target_pairs={{0,1},{1,0},{2,3},{3,2},{4,5},{5,4},{6,7},{7,6},{8,9},{9,8},{10,11... | collective-permute-start | bytes 1572872 | tf_op jit(solution)/shard_map/ppermute | solution.py:120
  53.0 1.0 copy-start

commit v4 on v3

--- a/solution.py
+++ b/solution.py
@@ -1,3 +1,5 @@
+import functools
+
 import jax
 import jax.numpy as jnp
 from jax import lax
@@ -100,14 +102,44 @@
     return jnp.dot(left, right, precision=lax.Precision.HIGHEST, preferred_element_type=jnp.float32)
 
 
-def gram_of(matrix):
+def cross(left, right):
     return lax.dot_general(
-        matrix,
-        matrix,
+        left,
+        right,
         (((0,), (0,)), ((), ())),
         precision=lax.Precision.HIGHEST,
         preferred_element_type=jnp.float32,
     )
+
+
+def gram_kernel(row_count, a_ref, o_ref):
+    step = pl.program_id(0)
+    half = a_ref.shape[1] // 2
+
+    @pl.when(step == 0)
+    def _():
+        o_ref[...] = jnp.zeros_like(o_ref)
+
+    a = a_ref[...]
+    o_ref[:, 0:half] += cross(a, a[:, 0:half])
+    o_ref[half:, half:] += cross(a[:, half:], a[:, half:])
+
+    @pl.when(step == pl.num_programs(0) - 1)
+    def _():
+        o_ref[0:half, half:] = o_ref[half:, 0:half].T
+        o_ref[...] = o_ref[...] / row_count
+
+
+def gram_of(matrix, row_count):
+    rows, width = matrix.shape
+    tile = min(rows, 512)
+    return pl.pallas_call(
+        functools.partial(gram_kernel, row_count),
+        out_shape=jax.ShapeDtypeStruct((width, width), jnp.float32),
+        grid=(rows // tile,),
+        in_specs=[pl.BlockSpec((tile, width), lambda i: (i, 0))],
+        out_specs=pl.BlockSpec((width, width), lambda i: (0, 0)),
+    )(matrix)
 
 
 def group_index(axis, shift, size):
@@ -163,7 +195,7 @@
 
 def on_device(response):
     row_count = response.shape[0] * lax.axis_size("inner") * lax.axis_size("wide")
-    gram_matrix = gram_of(response) / row_count
+    gram_matrix = gram_of(response, row_count)
     gram_matrix = all_sum(gram_matrix)
     upper_factor, inverse_upper = cholesky_and_inverse(gram_matrix)
     q_rows = rows_times(response, inverse_upper)

time: 111 us -> 111 us (level)
  matrix products: 10.5 us -> 0 us
  Pallas kernels: 56.4 us -> 64.8 us
    dot_general x1 -> x0, matrix products: 10.5 us -> none  [gram_of(): lax.dot_general(matrix, matrix, (((0,), (0,)), ((), ())), precision=lax.P...]
    pallas_call x0 -> x1, Pallas kernels: none -> 8.41 us  [gram_of(): pl.pallas_call(functools.partial(gram_kernel, row_count), out_shape=jax.S...]
where the time goes in v4:
time: 111 us; the launch traced here: 110 us
  Pallas kernels  64.8 us (58%)
  waiting for transfers between devices  23.9 us (22%)
  starting transfers between devices  17.2 us (15%)
  local copies, waits for them, and re-layouts  2.43 us (2%)
  other arithmetic  1.18 us (1%)
    pallas_call x1, Pallas kernels, cholesky_and_inverse(): pl.pallas_call(chol_kernel, out_shape=(jax.ShapeDtypeStruct((n, n), jnp.f...  47.9 us
    ppermute x14, waiting for transfers between devices, partner_xor(): return lax.ppermute(value, axis, pairs)  23.9 us
    ppermute x14, starting transfers between devices, partner_xor(): return lax.ppermute(value, axis, pairs)  17.2 us
    pallas_call x1, Pallas kernels, rows_times(): pl.pallas_call(rows_kernel, out_shape=jax.ShapeDtypeStruct((rows, weights...  8.46 us
    pallas_call x1, Pallas kernels, gram_of(): pl.pallas_call(functools.partial(gram_kernel, row_count), out_shape=jax.S...  8.41 us
  transfers between devices with their start and end apart: 14, of which 11 were waited for; matrix products, arithmetic and copies ran while one was open for 0% of the time, Pallas kernels for 0%

profile of v4, /device:TPU:0, one launch (start us, length us, event | category | flops | bytes accessed | tf_op | source)
XLA Modules:
  0.0 110.3 jit_solution(15920731418338279437)
XLA Ops:
  0.6 8.4 %shard_map.30 = f32[512,512]{1,0:T(8,128)} custom-call(f32[2048,512]{1,0:T(8,128)} %a_ref.3), custom_call_target="tpu_custom_call" | custom-call | tf_op jit(solution)/shard_map/pallas_call | solution.py:136
  9.1 1.1 constant_dynamic-slice_fusion.6
  10.6 1.5 %collective-permute-done = f32[256,512]{1,0:T(8,128)S(1)} collective-permute-done((f32[256,512]{1,0:T(8,128)S(1)}, f32[256,512]{1,0:T(8,128)S(1)}, u32[]{:S(2)}, u32[]{:S(2)}) %collective-permute-start) | collective-permute-done | bytes 524320 | tf_op jit(solution)/shard_map/ppermute | solution.py:152
  12.2 1.1 %dynamic-slice_add_fusion = f32[256,512]{1,0:T(8,128)S(1)} fusion(f32[256,512]{1,0:T(8,128)S(1)} %collective-permute-done, f32[512,512]{1,0:T(8,128)} %shard_map.30, s32[]{:T(128)S(6)} %select_n.40), kind=kLoop, calls=%fused_computation | loop fusion | flops 131072 | bytes 1572868 | tf_op jit(solution)/shard_map/add | solution.py:161
  13.4 2.9 %collective-permute-start.1 = (f32[64,512]{1,0:T(8,128)S(1)}, f32[64,512]{1,0:T(8,128)S(1)}, u32[]{:S(2)}, u32[]{:S(2)}) collective-permute-start(f32[64,512]{1,0:T(8,128)S(1)} %get-tuple-element.8), channel_id=1, source_target_pairs={{0,8},{8,0},{16,24},{24,16},{1,9},{9,1},{17,25},{25,17},{2,10},{10... | collective-permute-start | bytes 393224 | tf_op jit(solution)/shard_map/ppermute | solution.py:152
  16.3 1.5 %collective-permute-start.3 = (f32[64,512]{1,0:T(8,128)S(1)}, f32[64,512]{1,0:T(8,128)S(1)}, u32[]{:S(2)}, u32[]{:S(2)}) collective-permute-start(f32[64,512]{1,0:T(8,128)S(1)} %get-tuple-element.9), channel_id=1, source_target_pairs={{0,24},{8,16},{16,8},{24,0},{1,25},{9,17},{17,9},{25,1},{2,26},{10... | collective-permute-start | bytes 393224 | tf_op jit(solution)/shard_map/ppermute | solution.py:152
  17.8 2.6 %collective-permute-done.1 = f32[64,512]{1,0:T(8,128)S(1)} collective-permute-done((f32[64,512]{1,0:T(8,128)S(1)}, f32[64,512]{1,0:T(8,128)S(1)}, u32[]{:S(2)}, u32[]{:S(2)}) %collective-permute-start.1) | collective-permute-done | bytes 131104 | tf_op jit(solution)/shard_map/ppermute | solution.py:152
  20.4 3.8 %collective-permute-done.3 = f32[64,512]{1,0:T(8,128)S(1)} collective-permute-done((f32[64,512]{1,0:T(8,128)S(1)}, f32[64,512]{1,0:T(8,128)S(1)}, u32[]{:S(2)}, u32[]{:S(2)}) %collective-permute-start.3) | collective-permute-done | bytes 131104 | tf_op jit(solution)/shard_map/ppermute | solution.py:152
  24.2 1.4 %collective-permute-done.2 = f32[64,512]{1,0:T(8,128)S(1)} collective-permute-done((f32[64,512]{1,0:T(8,128)S(1)}, f32[64,512]{1,0:T(8,128)S(1)}, u32[]{:S(2)}, u32[]{:S(2)}) %collective-permute-start.2) | collective-permute-done | bytes 131104 | tf_op jit(solution)/shard_map/ppermute | solution.py:152
  25.6 1.6 %collective-permute-start.4 = (f32[16,512]{1,0:T(8,128)S(1)}, f32[16,512]{1,0:T(8,128)S(1)}, u32[]{:S(2)}, u32[]{:S(2)}) collective-permute-start(f32[16,512]{1,0:T(8,128)S(1)} %get-tuple-element.11), channel_id=1, source_target_pairs={{0,2},{1,3},{2,0},{3,1},{4,6},{5,7},{6,4},{7,5},{8,10},{9,11},{10,... | collective-permute-start | bytes 98312 | tf_op jit(solution)/shard_map/ppermute | solution.py:152
  27.3 2.5 %collective-permute-start.6 = (f32[16,512]{1,0:T(8,128)S(1)}, f32[16,512]{1,0:T(8,128)S(1)}, u32[]{:S(2)}, u32[]{:S(2)}) collective-permute-start(f32[16,512]{1,0:T(8,128)S(1)} %get-tuple-element.12), channel_id=1, source_target_pairs={{0,6},{1,7},{2,4},{3,5},{4,2},{5,3},{6,0},{7,1},{8,14},{9,15},{10,... | collective-permute-start | bytes 98312 | tf_op jit(solution)/shard_map/ppermute | solution.py:152
  29.9 3.1 %collective-permute-done.6 = f32[16,512]{1,0:T(8,128)S(1)} collective-permute-done((f32[16,512]{1,0:T(8,128)S(1)}, f32[16,512]{1,0:T(8,128)S(1)}, u32[]{:S(2)}, u32[]{:S(2)}) %collective-permute-start.6) | collective-permute-done | bytes 32800 | tf_op jit(solution)/shard_map/ppermute | solution.py:152
  33.0 1.9 %collective-permute-done.5 = f32[16,512]{1,0:T(8,128)S(1)} collective-permute-done((f32[16,512]{1,0:T(8,128)S(1)}, f32[16,512]{1,0:T(8,128)S(1)}, u32[]{:S(2)}, u32[]{:S(2)}) %collective-permute-start.5) | collective-permute-done | bytes 32800 | tf_op jit(solution)/shard_map/ppermute | solution.py:152
  35.4 1.4 %collective-permute-start.8 = (f32[16,512]{1,0:T(8,128)S(1)}, f32[16,512]{1,0:T(8,128)S(1)}, u32[]{:S(2)}, u32[]{:S(2)}) collective-permute-start(f32[16,512]{1,0:T(8,128)S(1)} %get-tuple-element.7), channel_id=1, source_target_pairs={{0,4},{1,5},{2,6},{3,7},{4,0},{5,1},{6,2},{7,3},{8,12},{9,13},{10,... | collective-permute-start | bytes 98312 | tf_op jit(solution)/shard_map/ppermute | solution.py:152
  36.8 2.6 %collective-permute-start.9 = (f32[16,512]{1,0:T(8,128)S(1)}, f32[16,512]{1,0:T(8,128)S(1)}, u32[]{:S(2)}, u32[]{:S(2)}) collective-permute-start(f32[16,512]{1,0:T(8,128)S(1)} %get-tuple-element.7), channel_id=1, source_target_pairs={{0,6},{1,7},{2,4},{3,5},{4,2},{5,3},{6,0},{7,1},{8,14},{9,15},{10,... | collective-permute-start | bytes 98312 | tf_op jit(solution)/shard_map/ppermute | solution.py:152
  40.3 2.3 %collective-permute-done.9 = f32[16,512]{1,0:T(8,128)S(1)} collective-permute-done((f32[16,512]{1,0:T(8,128)S(1)}, f32[16,512]{1,0:T(8,128)S(1)}, u32[]{:S(2)}, u32[]{:S(2)}) %collective-permute-start.9) | collective-permute-done | bytes 32800 | tf_op jit(solution)/shard_map/ppermute | solution.py:152
  42.5 1.5 %collective-permute-start.10 = (f32[64,512]{1,0:T(8,128)S(1)}, f32[64,512]{1,0:T(8,128)S(1)}, u32[]{:S(2)}, u32[]{:S(2)}) collective-permute-start(f32[64,512]{1,0:T(8,128)S(1)} %constant_dynamic-update-slice_fusion.6), channel_id=1, source_target_pairs={{0,8},{8,0},{16,24},{24,16},{1,9},{9,1},{17,25},{25,17},{2,10},{10... | collective-permute-start | bytes 393224 | tf_op jit(solution)/shard_map/ppermute | solution.py:152
  44.5 1.5 %collective-permute-start.11 = (f32[64,512]{1,0:T(8,128)S(1)}, f32[64,512]{1,0:T(8,128)S(1)}, u32[]{:S(2)}, u32[]{:S(2)}) collective-permute-start(f32[64,512]{1,0:T(8,128)S(1)} %constant_dynamic-update-slice_fusion.6), channel_id=1, source_target_pairs={{0,16},{8,24},{16,0},{24,8},{1,17},{9,25},{17,1},{25,9},{2,18},{10... | collective-permute-start | bytes 393224 | tf_op jit(solution)/shard_map/ppermute | solution.py:152
  46.1 1.4 %collective-permute-done.10 = f32[64,512]{1,0:T(8,128)S(1)} collective-permute-done((f32[64,512]{1,0:T(8,128)S(1)}, f32[64,512]{1,0:T(8,128)S(1)}, u32[]{:S(2)}, u32[]{:S(2)}) %collective-permute-start.10) | collective-permute-done | bytes 131104 | tf_op jit(solution)/shard_map/ppermute | solution.py:152
  47.5 3.4 %collective-permute-done.11 = f32[64,512]{1,0:T(8,128)S(1)} collective-permute-done((f32[64,512]{1,0:T(8,128)S(1)}, f32[64,512]{1,0:T(8,128)S(1)}, u32[]{:S(2)}, u32[]{:S(2)}) %collective-permute-start.11) | collective-permute-done | bytes 131104 | tf_op jit(solution)/shard_map/ppermute | solution.py:152
  51.2 1.7 %collective-permute-done.13 = f32[256,512]{1,0:T(8,128)S(1)} collective-permute-done((f32[256,512]{1,0:T(8,128)S(1)}, f32[256,512]{1,0:T(8,128)S(1)}, u32[]{:S(2)}, u32[]{:S(2)}) %collective-permute-start.13) | collective-permute-done | bytes 524320 | tf_op jit(solution)/shard_map/ppermute | solution.py:152
  53.0 1.0 copy-done
  53.9 47.9 %shard_map.31 = (f32[512,512]{1,0:T(8,128)}, f32[512,512]{1,0:T(8,128)}) custom-call(f32[512,512]{1,0:T(8,128)} %copy-done), custom_call_target="tpu_custom_call" | custom-call | tf_op jit(solution)/shard_map/pallas_call | solution.py:70
  101.9 8.5 %shard_map.32 = f32[2048,512]{1,0:T(8,128)} custom-call(f32[2048,512]{1,0:T(8,128)} %a_ref.3, f32[512,512]{1,0:T(8,128)} %get-tuple-element.5.w_ref), custom_call_target="tpu_custom_call" | custom-call | tf_op jit(solution)/shard_map/pallas_call | solution.py:89
  (27 shorter events, 3.0 us)
Async XLA Ops:
  10.1 2.1 %collective-permute-start = (f32[256,512]{1,0:T(8,128)S(1)}, f32[256,512]{1,0:T(8,128)S(1)}, u32[]{:S(2)}, u32[]{:S(2)}) collective-permute-start(f32[256,512]{1,0:T(8,128)S(1)} %constant_dynamic-slice_fusion.6), channel_id=1, source_target_pairs={{0,1},{1,0},{2,3},{3,2},{4,5},{5,4},{6,7},{7,6},{8,9},{9,8},{10,11... | collective-permute-start | bytes 1572872 | tf_op jit(solution)/shard_map/ppermute | solution.py:152
  13.4 7.0 %collective-permute-start.1 = (f32[64,512]{1,0:T(8,128)S(1)}, f32[64,512]{1,0:T(8,128)S(1)}, u32[]{:S(2)}, u32[]{:S(2)}) collective-permute-start(f32[64,512]{1,0:T(8,128)S(1)} %get-tuple-element.8), channel_id=1, source_target_pairs={{0,8},{8,0},{16,24},{24,16},{1,9},{9,1},{17,25},{25,17},{2,10},{10... | collective-permute-start | bytes 393224 | tf_op jit(solution)/shard_map/ppermute | solution.py:152
  16.3 7.9 %collective-permute-start.3 = (f32[64,512]{1,0:T(8,128)S(1)}, f32[64,512]{1,0:T(8,128)S(1)}, u32[]{:S(2)}, u32[]{:S(2)}) collective-permute-start(f32[64,512]{1,0:T(8,128)S(1)} %get-tuple-element.9), channel_id=1, source_target_pairs={{0,24},{8,16},{16,8},{24,0},{1,25},{9,17},{17,9},{25,1},{2,26},{10... | collective-permute-start | bytes 393224 | tf_op jit(solution)/shard_map/ppermute | solution.py:152
  17.8 7.8 %collective-permute-start.2 = (f32[64,512]{1,0:T(8,128)S(1)}, f32[64,512]{1,0:T(8,128)S(1)}, u32[]{:S(2)}, u32[]{:S(2)}) collective-permute-start(f32[64,512]{1,0:T(8,128)S(1)} %get-tuple-element.10), channel_id=1, source_target_pairs={{0,16},{8,24},{16,0},{24,8},{1,17},{9,25},{17,1},{25,9},{2,18},{10... | collective-permute-start | bytes 393224 | tf_op jit(solution)/shard_map/ppermute | solution.py:152
  25.6 4.2 %collective-permute-start.4 = (f32[16,512]{1,0:T(8,128)S(1)}, f32[16,512]{1,0:T(8,128)S(1)}, u32[]{:S(2)}, u32[]{:S(2)}) collective-permute-start(f32[16,512]{1,0:T(8,128)S(1)} %get-tuple-element.11), channel_id=1, source_target_pairs={{0,2},{1,3},{2,0},{3,1},{4,6},{5,7},{6,4},{7,5},{8,10},{9,11},{10,... | collective-permute-start | bytes 98312 | tf_op jit(solution)/shard_map/ppermute | solution.py:152
  27.3 5.7 %collective-permute-start.6 = (f32[16,512]{1,0:T(8,128)S(1)}, f32[16,512]{1,0:T(8,128)S(1)}, u32[]{:S(2)}, u32[]{:S(2)}) collective-permute-start(f32[16,512]{1,0:T(8,128)S(1)} %get-tuple-element.12), channel_id=1, source_target_pairs={{0,6},{1,7},{2,4},{3,5},{4,2},{5,3},{6,0},{7,1},{8,14},{9,15},{10,... | collective-permute-start | bytes 98312 | tf_op jit(solution)/shard_map/ppermute | solution.py:152
  29.7 5.2 %collective-permute-start.5 = (f32[16,512]{1,0:T(8,128)S(1)}, f32[16,512]{1,0:T(8,128)S(1)}, u32[]{:S(2)}, u32[]{:S(2)}) collective-permute-start(f32[16,512]{1,0:T(8,128)S(1)} %get-tuple-element.13), channel_id=1, source_target_pairs={{0,4},{1,5},{2,6},{3,7},{4,0},{5,1},{6,2},{7,3},{8,12},{9,13},{10,... | collective-permute-start | bytes 98312 | tf_op jit(solution)/shard_map/ppermute | solution.py:152
  34.9 4.5 %collective-permute-start.7 = (f32[16,512]{1,0:T(8,128)S(1)}, f32[16,512]{1,0:T(8,128)S(1)}, u32[]{:S(2)}, u32[]{:S(2)}) collective-permute-start(f32[16,512]{1,0:T(8,128)S(1)} %get-tuple-element.7), channel_id=1, source_target_pairs={{0,2},{1,3},{2,0},{3,1},{4,6},{5,7},{6,4},{7,5},{8,10},{9,11},{10,... | collective-permute-start | bytes 98312 | tf_op jit(solution)/shard_map/ppermute | solution.py:152
  35.4 4.8 %collective-permute-start.8 = (f32[16,512]{1,0:T(8,128)S(1)}, f32[16,512]{1,0:T(8,128)S(1)}, u32[]{:S(2)}, u32[]{:S(2)}) collective-permute-start(f32[16,512]{1,0:T(8,128)S(1)} %get-tuple-element.7), channel_id=1, source_target_pairs={{0,4},{1,5},{2,6},{3,7},{4,0},{5,1},{6,2},{7,3},{8,12},{9,13},{10,... | collective-permute-start | bytes 98312 | tf_op jit(solution)/shard_map/ppermute | solution.py:152
  36.8 5.7 %collective-permute-start.9 = (f32[16,512]{1,0:T(8,128)S(1)}, f32[16,512]{1,0:T(8,128)S(1)}, u32[]{:S(2)}, u32[]{:S(2)}) collective-permute-start(f32[16,512]{1,0:T(8,128)S(1)} %get-tuple-element.7), channel_id=1, source_target_pairs={{0,6},{1,7},{2,4},{3,5},{4,2},{5,3},{6,0},{7,1},{8,14},{9,15},{10,... | collective-permute-start | bytes 98312 | tf_op jit(solution)/shard_map/ppermute | solution.py:152
  42.5 5.0 %collective-permute-start.10 = (f32[64,512]{1,0:T(8,128)S(1)}, f32[64,512]{1,0:T(8,128)S(1)}, u32[]{:S(2)}, u32[]{:S(2)}) collective-permute-start(f32[64,512]{1,0:T(8,128)S(1)} %constant_dynamic-update-slice_fusion.6), channel_id=1, source_target_pairs={{0,8},{8,0},{16,24},{24,16},{1,9},{9,1},{17,25},{25,17},{2,10},{10... | collective-permute-start | bytes 393224 | tf_op jit(solution)/shard_map/ppermute | solution.py:152
  44.0 6.9 %collective-permute-start.12 = (f32[64,512]{1,0:T(8,128)S(1)}, f32[64,512]{1,0:T(8,128)S(1)}, u32[]{:S(2)}, u32[]{:S(2)}) collective-permute-start(f32[64,512]{1,0:T(8,128)S(1)} %constant_dynamic-update-slice_fusion.6), channel_id=1, source_target_pairs={{0,24},{8,16},{16,8},{24,0},{1,25},{9,17},{17,9},{25,1},{2,26},{10... | collective-permute-start | bytes 393224 | tf_op jit(solution)/shard_map/ppermute | solution.py:152
  44.5 6.4 %collective-permute-start.11 = (f32[64,512]{1,0:T(8,128)S(1)}, f32[64,512]{1,0:T(8,128)S(1)}, u32[]{:S(2)}, u32[]{:S(2)}) collective-permute-start(f32[64,512]{1,0:T(8,128)S(1)} %constant_dynamic-update-slice_fusion.6), channel_id=1, source_target_pairs={{0,16},{8,24},{16,0},{24,8},{1,17},{9,25},{17,1},{25,9},{2,18},{10... | collective-permute-start | bytes 393224 | tf_op jit(solution)/shard_map/ppermute | solution.py:152
  50.9 2.0 %collective-permute-start.13 = (f32[256,512]{1,0:T(8,128)S(1)}, f32[256,512]{1,0:T(8,128)S(1)}, u32[]{:S(2)}, u32[]{:S(2)}) collective-permute-start(f32[256,512]{1,0:T(8,128)S(1)} %constant_dynamic-update-slice_fusion.2), channel_id=1, source_target_pairs={{0,1},{1,0},{2,3},{3,2},{4,5},{5,4},{6,7},{7,6},{8,9},{9,8},{10,11... | collective-permute-start | bytes 1572872 | tf_op jit(solution)/shard_map/ppermute | solution.py:152
  53.0 1.0 copy-start

commit v5 on v4

--- a/solution.py
+++ b/solution.py
@@ -37,9 +37,21 @@
     return jnp.where(c >= r, joined[:, :size], 0.0), joined[:, size:]
 
 
-def chol_kernel(g_ref, u_ref, uinv_ref, work_ref, aug_ref, inv_ref):
-    n = g_ref.shape[0]
-    g = g_ref[...]
+def chol_kernel(bit_ref, mine_ref, got_ref, u_ref, uinv_ref, work_ref, aug_ref, inv_ref):
+    n = u_ref.shape[0]
+    half = n // 2
+
+    @pl.when(bit_ref[0] == 0)
+    def _():
+        work_ref[0:half, :] = mine_ref[...]
+        work_ref[half:n, :] = got_ref[...]
+
+    @pl.when(bit_ref[0] != 0)
+    def _():
+        work_ref[0:half, :] = got_ref[...]
+        work_ref[half:n, :] = mine_ref[...]
+
+    g = work_ref[...]
     work_ref[...] = (g + g.T) * 0.5
     aug_ref[...] = jnp.zeros_like(aug_ref)
     u_ref[...] = jnp.zeros_like(u_ref)
@@ -64,16 +76,16 @@
             aug_ref[hi:n, 0:hi] = aug_ref[hi:n, 0:hi] - hdot(u_off_t, inv_ref[lo:hi, 0:hi])
 
 
-def cholesky_and_inverse(gram_matrix):
-    n = gram_matrix.shape[0]
+def cholesky_and_inverse(bit, mine, got):
+    n = mine.shape[1]
     spec = pl.BlockSpec(memory_space=pltpu.VMEM)
     return pl.pallas_call(
         chol_kernel,
         out_shape=(jax.ShapeDtypeStruct((n, n), jnp.float32), jax.ShapeDtypeStruct((n, n), jnp.float32)),
-        in_specs=[spec],
+        in_specs=[pl.BlockSpec(memory_space=pltpu.SMEM), spec, spec],
         out_specs=(spec, spec),
         scratch_shapes=[pltpu.VMEM((n, n), jnp.float32) for _ in range(3)],
-    )(gram_matrix)
+    )(bit, mine, got)
 
 
 def rows_kernel(a_ref, w_ref, o_ref):
@@ -112,34 +124,53 @@
     )
 
 
-def gram_kernel(row_count, a_ref, o_ref):
+def gram_kernel(row_count, bit_ref, a_ref, keep_ref, send_ref, acc_ref):
     step = pl.program_id(0)
     half = a_ref.shape[1] // 2
 
     @pl.when(step == 0)
     def _():
-        o_ref[...] = jnp.zeros_like(o_ref)
+        acc_ref[...] = jnp.zeros_like(acc_ref)
 
     a = a_ref[...]
-    o_ref[:, 0:half] += cross(a, a[:, 0:half])
-    o_ref[half:, half:] += cross(a[:, half:], a[:, half:])
+    acc_ref[:, 0:half] += cross(a, a[:, 0:half])
+    acc_ref[half:, half:] += cross(a[:, half:], a[:, half:])
 
     @pl.when(step == pl.num_programs(0) - 1)
     def _():
-        o_ref[0:half, half:] = o_ref[half:, 0:half].T
-        o_ref[...] = o_ref[...] / row_count
-
-
-def gram_of(matrix, row_count):
+        acc_ref[0:half, half:] = acc_ref[half:, 0:half].T
+        top = acc_ref[0:half, :] / row_count
+        bottom = acc_ref[half:, :] / row_count
+
+        @pl.when(bit_ref[0] == 0)
+        def _():
+            keep_ref[...] = top
+            send_ref[...] = bottom
+
+        @pl.when(bit_ref[0] != 0)
+        def _():
+            keep_ref[...] = bottom
+            send_ref[...] = top
+
+
+def gram_halves(matrix, row_count, bit):
     rows, width = matrix.shape
     tile = min(rows, 512)
+    half = jax.ShapeDtypeStruct((width // 2, width), jnp.float32)
     return pl.pallas_call(
         functools.partial(gram_kernel, row_count),
-        out_shape=jax.ShapeDtypeStruct((width, width), jnp.float32),
+        out_shape=(half, half),
         grid=(rows // tile,),
-        in_specs=[pl.BlockSpec((tile, width), lambda i: (i, 0))],
-        out_specs=pl.BlockSpec((width, width), lambda i: (0, 0)),
-    )(matrix)
+        in_specs=[
+            pl.BlockSpec(memory_space=pltpu.SMEM),
+            pl.BlockSpec((tile, width), lambda i: (i, 0)),
+        ],
+        out_specs=(
+            pl.BlockSpec((width // 2, width), lambda i: (0, 0)),
+            pl.BlockSpec((width // 2, width), lambda i: (0, 0)),
+        ),
+        scratch_shapes=[pltpu.VMEM((width, width), jnp.float32)],
+    )(bit, matrix)
 
 
 def group_index(axis, shift, size):
@@ -184,20 +215,18 @@
     return groups
 
 
-def all_sum(gram_matrix):
-    groups = [("wide", 0, 2)] + axis_groups("inner", 0) + axis_groups("wide", 1)
-    for group in groups:
-        gram_matrix = scatter_sum(gram_matrix, *group)
-    for group in reversed(groups):
-        gram_matrix = gather_all(gram_matrix, *group)
-    return gram_matrix
-
-
 def on_device(response):
     row_count = response.shape[0] * lax.axis_size("inner") * lax.axis_size("wide")
-    gram_matrix = gram_of(response, row_count)
-    gram_matrix = all_sum(gram_matrix)
-    upper_factor, inverse_upper = cholesky_and_inverse(gram_matrix)
+    bit = jnp.reshape(lax.axis_index("wide") & 1, (1,)).astype(jnp.int32)
+    keep, send = gram_halves(response, row_count, bit)
+    partial_sum = keep + partner_xor(send, "wide", 0, 1)
+    groups = axis_groups("inner", 0) + axis_groups("wide", 1)
+    for group in groups:
+        partial_sum = scatter_sum(partial_sum, *group)
+    for group in reversed(groups):
+        partial_sum = gather_all(partial_sum, *group)
+    got = partner_xor(partial_sum, "wide", 0, 1)
+    upper_factor, inverse_upper = cholesky_and_inverse(bit, partial_sum, got)
     q_rows = rows_times(response, inverse_upper)
     return (upper_factor, q_rows)
 

time: 111 us -> 110 us (level)
  local copies, waits for them, and re-layouts: 2.43 us -> 1.01 us
    add x0 -> x1, other arithmetic: none -> 1.12 us  [on_device(): partial_sum = keep + partner_xor(send, 'wide', 0, 1)]
    add x2 -> x1, other arithmetic: 1.16 us -> 0.04 us  [scatter_sum(): total = total + partner_xor(chunk(index ^ offset), axis, shift, offset)]
where the time goes in v5:
time: 110 us
  Pallas kernels  65.2 us (59%)
  waiting for transfers between devices  24.3 us (22%)
  starting transfers between devices  17.2 us (16%)
  other arithmetic  1.18 us (1%)
    pallas_call x1, Pallas kernels, cholesky_and_inverse(): pl.pallas_call(chol_kernel, out_shape=(jax.ShapeDtypeStruct((n, n), jnp.f...  48.2 us
    ppermute x14, waiting for transfers between devices, partner_xor(): return lax.ppermute(value, axis, pairs)  24.3 us
    ppermute x14, starting transfers between devices, partner_xor(): return lax.ppermute(value, axis, pairs)  17.2 us
    pallas_call x1, Pallas kernels, rows_times(): pl.pallas_call(rows_kernel, out_shape=jax.ShapeDtypeStruct((rows, weights...  8.46 us
    pallas_call x1, Pallas kernels, gram_halves(): pl.pallas_call(functools.partial(gram_kernel, row_count), out_shape=(half...  8.46 us
  transfers between devices with their start and end apart: 14, of which 11 were waited for; matrix products, arithmetic and copies ran while one was open for 0% of the time, Pallas kernels for 0%

profile of v5, /device:TPU:0, one launch (start us, length us, event | category | flops | bytes accessed | tf_op | source)
XLA Modules:
  0.0 109.6 jit_solution(5150892694888846230)
XLA Ops:
  0.6 8.5 %shard_map.30 = (f32[256,512]{1,0:T(8,128)}, f32[256,512]{1,0:T(8,128)}) custom-call(s32[1]{0:T(128)} %bitcast.bit_ref, f32[2048,512]{1,0:T(8,128)} %a_ref.3), custom_call_target="tpu_custom_call" | custom-call | tf_op jit(solution)/shard_map/pallas_call | solution.py:160
  9.6 1.7 %collective-permute-done = f32[256,512]{1,0:T(8,128)S(1)} collective-permute-done((f32[256,512]{1,0:T(8,128)}, f32[256,512]{1,0:T(8,128)S(1)}, u32[]{:S(2)}, u32[]{:S(2)}) %collective-permute-start) | collective-permute-done | bytes 524320 | tf_op jit(solution)/shard_map/ppermute | solution.py:183
  11.3 1.1 %add.53 = f32[256,512]{1,0:T(8,128)S(1)} add(f32[256,512]{1,0:T(8,128)} %get-tuple-element.6, f32[256,512]{1,0:T(8,128)S(1)} %collective-permute-done) | non-fusion elementwise | flops 131072 | bytes 1572864 | tf_op jit(solution)/shard_map/add | solution.py:222
  12.5 2.9 %collective-permute-start.1 = (f32[64,512]{1,0:T(8,128)S(1)}, f32[64,512]{1,0:T(8,128)S(1)}, u32[]{:S(2)}, u32[]{:S(2)}) collective-permute-start(f32[64,512]{1,0:T(8,128)S(1)} %get-tuple-element.12), channel_id=1, source_target_pairs={{0,8},{8,0},{16,24},{24,16},{1,9},{9,1},{17,25},{25,17},{2,10},{10... | collective-permute-start | bytes 393224 | tf_op jit(solution)/shard_map/ppermute | solution.py:183
  15.4 1.5 %collective-permute-start.3 = (f32[64,512]{1,0:T(8,128)S(1)}, f32[64,512]{1,0:T(8,128)S(1)}, u32[]{:S(2)}, u32[]{:S(2)}) collective-permute-start(f32[64,512]{1,0:T(8,128)S(1)} %get-tuple-element.13), channel_id=1, source_target_pairs={{0,24},{8,16},{16,8},{24,0},{1,25},{9,17},{17,9},{25,1},{2,26},{10... | collective-permute-start | bytes 393224 | tf_op jit(solution)/shard_map/ppermute | solution.py:183
  16.9 2.6 %collective-permute-done.1 = f32[64,512]{1,0:T(8,128)S(1)} collective-permute-done((f32[64,512]{1,0:T(8,128)S(1)}, f32[64,512]{1,0:T(8,128)S(1)}, u32[]{:S(2)}, u32[]{:S(2)}) %collective-permute-start.1) | collective-permute-done | bytes 131104 | tf_op jit(solution)/shard_map/ppermute | solution.py:183
  19.5 3.8 %collective-permute-done.3 = f32[64,512]{1,0:T(8,128)S(1)} collective-permute-done((f32[64,512]{1,0:T(8,128)S(1)}, f32[64,512]{1,0:T(8,128)S(1)}, u32[]{:S(2)}, u32[]{:S(2)}) %collective-permute-start.3) | collective-permute-done | bytes 131104 | tf_op jit(solution)/shard_map/ppermute | solution.py:183
  23.3 1.4 %collective-permute-done.2 = f32[64,512]{1,0:T(8,128)S(1)} collective-permute-done((f32[64,512]{1,0:T(8,128)S(1)}, f32[64,512]{1,0:T(8,128)S(1)}, u32[]{:S(2)}, u32[]{:S(2)}) %collective-permute-start.2) | collective-permute-done | bytes 131104 | tf_op jit(solution)/shard_map/ppermute | solution.py:183
  24.7 1.6 %collective-permute-start.4 = (f32[16,512]{1,0:T(8,128)S(1)}, f32[16,512]{1,0:T(8,128)S(1)}, u32[]{:S(2)}, u32[]{:S(2)}) collective-permute-start(f32[16,512]{1,0:T(8,128)S(1)} %get-tuple-element.15), channel_id=1, source_target_pairs={{0,2},{1,3},{2,0},{3,1},{4,6},{5,7},{6,4},{7,5},{8,10},{9,11},{10,... | collective-permute-start | bytes 98312 | tf_op jit(solution)/shard_map/ppermute | solution.py:183
  26.4 2.5 %collective-permute-start.6 = (f32[16,512]{1,0:T(8,128)S(1)}, f32[16,512]{1,0:T(8,128)S(1)}, u32[]{:S(2)}, u32[]{:S(2)}) collective-permute-start(f32[16,512]{1,0:T(8,128)S(1)} %get-tuple-element.16), channel_id=1, source_target_pairs={{0,6},{1,7},{2,4},{3,5},{4,2},{5,3},{6,0},{7,1},{8,14},{9,15},{10,... | collective-permute-start | bytes 98312 | tf_op jit(solution)/shard_map/ppermute | solution.py:183
  29.0 3.1 %collective-permute-done.6 = f32[16,512]{1,0:T(8,128)S(1)} collective-permute-done((f32[16,512]{1,0:T(8,128)S(1)}, f32[16,512]{1,0:T(8,128)S(1)}, u32[]{:S(2)}, u32[]{:S(2)}) %collective-permute-start.6) | collective-permute-done | bytes 32800 | tf_op jit(solution)/shard_map/ppermute | solution.py:183
  32.1 1.9 %collective-permute-done.5 = f32[16,512]{1,0:T(8,128)S(1)} collective-permute-done((f32[16,512]{1,0:T(8,128)S(1)}, f32[16,512]{1,0:T(8,128)S(1)}, u32[]{:S(2)}, u32[]{:S(2)}) %collective-permute-start.5) | collective-permute-done | bytes 32800 | tf_op jit(solution)/shard_map/ppermute | solution.py:183
  34.5 1.4 %collective-permute-start.8 = (f32[16,512]{1,0:T(8,128)S(1)}, f32[16,512]{1,0:T(8,128)S(1)}, u32[]{:S(2)}, u32[]{:S(2)}) collective-permute-start(f32[16,512]{1,0:T(8,128)S(1)} %get-tuple-element.11), channel_id=1, source_target_pairs={{0,4},{1,5},{2,6},{3,7},{4,0},{5,1},{6,2},{7,3},{8,12},{9,13},{10,... | collective-permute-start | bytes 98312 | tf_op jit(solution)/shard_map/ppermute | solution.py:183
  35.9 2.6 %collective-permute-start.9 = (f32[16,512]{1,0:T(8,128)S(1)}, f32[16,512]{1,0:T(8,128)S(1)}, u32[]{:S(2)}, u32[]{:S(2)}) collective-permute-start(f32[16,512]{1,0:T(8,128)S(1)} %get-tuple-element.11), channel_id=1, source_target_pairs={{0,6},{1,7},{2,4},{3,5},{4,2},{5,3},{6,0},{7,1},{8,14},{9,15},{10,... | collective-permute-start | bytes 98312 | tf_op jit(solution)/shard_map/ppermute | solution.py:183
  38.5 0.8 collective-permute-done.8
  39.4 2.3 %collective-permute-done.9 = f32[16,512]{1,0:T(8,128)S(1)} collective-permute-done((f32[16,512]{1,0:T(8,128)S(1)}, f32[16,512]{1,0:T(8,128)S(1)}, u32[]{:S(2)}, u32[]{:S(2)}) %collective-permute-start.9) | collective-permute-done | bytes 32800 | tf_op jit(solution)/shard_map/ppermute | solution.py:183
  41.7 1.5 %collective-permute-start.10 = (f32[64,512]{1,0:T(8,128)S(1)}, f32[64,512]{1,0:T(8,128)S(1)}, u32[]{:S(2)}, u32[]{:S(2)}) collective-permute-start(f32[64,512]{1,0:T(8,128)S(1)} %constant_dynamic-update-slice_fusion.4), channel_id=1, source_target_pairs={{0,8},{8,0},{16,24},{24,16},{1,9},{9,1},{17,25},{25,17},{2,10},{10... | collective-permute-start | bytes 393224 | tf_op jit(solution)/shard_map/ppermute | solution.py:183
  43.6 1.5 %collective-permute-start.11 = (f32[64,512]{1,0:T(8,128)S(1)}, f32[64,512]{1,0:T(8,128)S(1)}, u32[]{:S(2)}, u32[]{:S(2)}) collective-permute-start(f32[64,512]{1,0:T(8,128)S(1)} %constant_dynamic-update-slice_fusion.4), channel_id=1, source_target_pairs={{0,16},{8,24},{16,0},{24,8},{1,17},{9,25},{17,1},{25,9},{2,18},{10... | collective-permute-start | bytes 393224 | tf_op jit(solution)/shard_map/ppermute | solution.py:183
  45.2 1.4 %collective-permute-done.10 = f32[64,512]{1,0:T(8,128)S(1)} collective-permute-done((f32[64,512]{1,0:T(8,128)S(1)}, f32[64,512]{1,0:T(8,128)S(1)}, u32[]{:S(2)}, u32[]{:S(2)}) %collective-permute-start.10) | collective-permute-done | bytes 131104 | tf_op jit(solution)/shard_map/ppermute | solution.py:183
  46.6 3.4 %collective-permute-done.11 = f32[64,512]{1,0:T(8,128)S(1)} collective-permute-done((f32[64,512]{1,0:T(8,128)S(1)}, f32[64,512]{1,0:T(8,128)S(1)}, u32[]{:S(2)}, u32[]{:S(2)}) %collective-permute-start.11) | collective-permute-done | bytes 131104 | tf_op jit(solution)/shard_map/ppermute | solution.py:183
  50.1 1.9 %collective-permute-done.13.got_ref = f32[256,512]{1,0:T(8,128)S(1)} collective-permute-done((f32[256,512]{1,0:T(8,128)S(1)}, f32[256,512]{1,0:T(8,128)S(1)}, u32[]{:S(2)}, u32[]{:S(2)}) %collective-permute-start.13) | collective-permute-done | bytes 524320 | tf_op jit(solution)/shard_map/ppermute | solution.py:183
  52.0 0.8 copy-done.1
  52.9 48.2 %shard_map.31 = (f32[512,512]{1,0:T(8,128)}, f32[512,512]{1,0:T(8,128)}) custom-call(s32[1]{0:T(128)} %bitcast.bit_ref, f32[256,512]{1,0:T(8,128)} %copy-done, f32[256,512]{1,0:T(8,128)} %copy-done.1), custom_call_target="tpu_custom_call" | custom-call | tf_op jit(solution)/shard_map/pallas_call | solution.py:82
  101.1 8.5 %shard_map.32 = f32[2048,512]{1,0:T(8,128)} custom-call(f32[2048,512]{1,0:T(8,128)} %a_ref.3, f32[512,512]{1,0:T(8,128)} %get-tuple-element.9.w_ref), custom_call_target="tpu_custom_call" | custom-call | tf_op jit(solution)/shard_map/pallas_call | solution.py:101
  (25 shorter events, 1.9 us)
Async XLA Ops:
  9.1 2.2 %collective-permute-start = (f32[256,512]{1,0:T(8,128)}, f32[256,512]{1,0:T(8,128)S(1)}, u32[]{:S(2)}, u32[]{:S(2)}) collective-permute-start(f32[256,512]{1,0:T(8,128)} %get-tuple-element.7), channel_id=1, source_target_pairs={{0,1},{1,0},{2,3},{3,2},{4,5},{5,4},{6,7},{7,6},{8,9},{9,8},{10,11... | collective-permute-start | bytes 1572872 | tf_op jit(solution)/shard_map/ppermute | solution.py:183
  12.5 7.0 %collective-permute-start.1 = (f32[64,512]{1,0:T(8,128)S(1)}, f32[64,512]{1,0:T(8,128)S(1)}, u32[]{:S(2)}, u32[]{:S(2)}) collective-permute-start(f32[64,512]{1,0:T(8,128)S(1)} %get-tuple-element.12), channel_id=1, source_target_pairs={{0,8},{8,0},{16,24},{24,16},{1,9},{9,1},{17,25},{25,17},{2,10},{10... | collective-permute-start | bytes 393224 | tf_op jit(solution)/shard_map/ppermute | solution.py:183
  15.4 7.9 %collective-permute-start.3 = (f32[64,512]{1,0:T(8,128)S(1)}, f32[64,512]{1,0:T(8,128)S(1)}, u32[]{:S(2)}, u32[]{:S(2)}) collective-permute-start(f32[64,512]{1,0:T(8,128)S(1)} %get-tuple-element.13), channel_id=1, source_target_pairs={{0,24},{8,16},{16,8},{24,0},{1,25},{9,17},{17,9},{25,1},{2,26},{10... | collective-permute-start | bytes 393224 | tf_op jit(solution)/shard_map/ppermute | solution.py:183
  16.9 7.8 %collective-permute-start.2 = (f32[64,512]{1,0:T(8,128)S(1)}, f32[64,512]{1,0:T(8,128)S(1)}, u32[]{:S(2)}, u32[]{:S(2)}) collective-permute-start(f32[64,512]{1,0:T(8,128)S(1)} %get-tuple-element.14), channel_id=1, source_target_pairs={{0,16},{8,24},{16,0},{24,8},{1,17},{9,25},{17,1},{25,9},{2,18},{10... | collective-permute-start | bytes 393224 | tf_op jit(solution)/shard_map/ppermute | solution.py:183
  24.7 4.2 %collective-permute-start.4 = (f32[16,512]{1,0:T(8,128)S(1)}, f32[16,512]{1,0:T(8,128)S(1)}, u32[]{:S(2)}, u32[]{:S(2)}) collective-permute-start(f32[16,512]{1,0:T(8,128)S(1)} %get-tuple-element.15), channel_id=1, source_target_pairs={{0,2},{1,3},{2,0},{3,1},{4,6},{5,7},{6,4},{7,5},{8,10},{9,11},{10,... | collective-permute-start | bytes 98312 | tf_op jit(solution)/shard_map/ppermute | solution.py:183
  26.4 5.7 %collective-permute-start.6 = (f32[16,512]{1,0:T(8,128)S(1)}, f32[16,512]{1,0:T(8,128)S(1)}, u32[]{:S(2)}, u32[]{:S(2)}) collective-permute-start(f32[16,512]{1,0:T(8,128)S(1)} %get-tuple-element.16), channel_id=1, source_target_pairs={{0,6},{1,7},{2,4},{3,5},{4,2},{5,3},{6,0},{7,1},{8,14},{9,15},{10,... | collective-permute-start | bytes 98312 | tf_op jit(solution)/shard_map/ppermute | solution.py:183
  28.9 5.2 %collective-permute-start.5 = (f32[16,512]{1,0:T(8,128)S(1)}, f32[16,512]{1,0:T(8,128)S(1)}, u32[]{:S(2)}, u32[]{:S(2)}) collective-permute-start(f32[16,512]{1,0:T(8,128)S(1)} %get-tuple-element.17), channel_id=1, source_target_pairs={{0,4},{1,5},{2,6},{3,7},{4,0},{5,1},{6,2},{7,3},{8,12},{9,13},{10,... | collective-permute-start | bytes 98312 | tf_op jit(solution)/shard_map/ppermute | solution.py:183
  34.1 4.5 %collective-permute-start.7 = (f32[16,512]{1,0:T(8,128)S(1)}, f32[16,512]{1,0:T(8,128)S(1)}, u32[]{:S(2)}, u32[]{:S(2)}) collective-permute-start(f32[16,512]{1,0:T(8,128)S(1)} %get-tuple-element.11), channel_id=1, source_target_pairs={{0,2},{1,3},{2,0},{3,1},{4,6},{5,7},{6,4},{7,5},{8,10},{9,11},{10,... | collective-permute-start | bytes 98312 | tf_op jit(solution)/shard_map/ppermute | solution.py:183
  34.5 4.8 %collective-permute-start.8 = (f32[16,512]{1,0:T(8,128)S(1)}, f32[16,512]{1,0:T(8,128)S(1)}, u32[]{:S(2)}, u32[]{:S(2)}) collective-permute-start(f32[16,512]{1,0:T(8,128)S(1)} %get-tuple-element.11), channel_id=1, source_target_pairs={{0,4},{1,5},{2,6},{3,7},{4,0},{5,1},{6,2},{7,3},{8,12},{9,13},{10,... | collective-permute-start | bytes 98312 | tf_op jit(solution)/shard_map/ppermute | solution.py:183
  35.9 5.7 %collective-permute-start.9 = (f32[16,512]{1,0:T(8,128)S(1)}, f32[16,512]{1,0:T(8,128)S(1)}, u32[]{:S(2)}, u32[]{:S(2)}) collective-permute-start(f32[16,512]{1,0:T(8,128)S(1)} %get-tuple-element.11), channel_id=1, source_target_pairs={{0,6},{1,7},{2,4},{3,5},{4,2},{5,3},{6,0},{7,1},{8,14},{9,15},{10,... | collective-permute-start | bytes 98312 | tf_op jit(solution)/shard_map/ppermute | solution.py:183
  41.7 5.0 %collective-permute-start.10 = (f32[64,512]{1,0:T(8,128)S(1)}, f32[64,512]{1,0:T(8,128)S(1)}, u32[]{:S(2)}, u32[]{:S(2)}) collective-permute-start(f32[64,512]{1,0:T(8,128)S(1)} %constant_dynamic-update-slice_fusion.4), channel_id=1, source_target_pairs={{0,8},{8,0},{16,24},{24,16},{1,9},{9,1},{17,25},{25,17},{2,10},{10... | collective-permute-start | bytes 393224 | tf_op jit(solution)/shard_map/ppermute | solution.py:183
  43.1 6.9 %collective-permute-start.12 = (f32[64,512]{1,0:T(8,128)S(1)}, f32[64,512]{1,0:T(8,128)S(1)}, u32[]{:S(2)}, u32[]{:S(2)}) collective-permute-start(f32[64,512]{1,0:T(8,128)S(1)} %constant_dynamic-update-slice_fusion.4), channel_id=1, source_target_pairs={{0,24},{8,16},{16,8},{24,0},{1,25},{9,17},{17,9},{25,1},{2,26},{10... | collective-permute-start | bytes 393224 | tf_op jit(solution)/shard_map/ppermute | solution.py:183
  43.6 6.4 %collective-permute-start.11 = (f32[64,512]{1,0:T(8,128)S(1)}, f32[64,512]{1,0:T(8,128)S(1)}, u32[]{:S(2)}, u32[]{:S(2)}) collective-permute-start(f32[64,512]{1,0:T(8,128)S(1)} %constant_dynamic-update-slice_fusion.4), channel_id=1, source_target_pairs={{0,16},{8,24},{16,0},{24,8},{1,17},{9,25},{17,1},{25,9},{2,18},{10... | collective-permute-start | bytes 393224 | tf_op jit(solution)/shard_map/ppermute | solution.py:183
  50.0 2.0 %copy-start = (f32[256,512]{1,0:T(8,128)}, f32[256,512]{1,0:T(8,128)S(1)}, u32[]{:S(2)}) copy-start(f32[256,512]{1,0:T(8,128)S(1)} %constant_dynamic-update-slice_fusion.mine_ref) | copy-start | bytes 1572868
  50.1 2.0 %collective-permute-start.13 = (f32[256,512]{1,0:T(8,128)S(1)}, f32[256,512]{1,0:T(8,128)S(1)}, u32[]{:S(2)}, u32[]{:S(2)}) collective-permute-start(f32[256,512]{1,0:T(8,128)S(1)} %constant_dynamic-update-slice_fusion.mine_ref), channel_id=1, source_target_pairs={{0,1},{1,0},{2,3},{3,2},{4,5},{5,4},{6,7},{7,6},{8,9},{9,8},{10,11... | collective-permute-start | bytes 1572872 | tf_op jit(solution)/shard_map/ppermute | solution.py:183
  52.0 0.8 copy-start.1

commit v6 on v5

--- a/solution.py
+++ b/solution.py
@@ -183,10 +183,14 @@
     return lax.ppermute(value, axis, pairs)
 
 
-def scatter_sum(value, axis, shift, size):
-    height = value.shape[0] // size
+def scatter_sum(addends, axis, shift, size):
+    height = addends[0].shape[0] // size
     index = group_index(axis, shift, size)
-    chunk = lambda j: lax.dynamic_slice_in_dim(value, j * height, height, 0)
+
+    def chunk(j):
+        parts = [lax.dynamic_slice_in_dim(part, j * height, height, 0) for part in addends]
+        return functools.reduce(jnp.add, parts)
+
     total = chunk(index)
     for offset in range(1, size):
         total = total + partner_xor(chunk(index ^ offset), axis, shift, offset)
@@ -219,10 +223,11 @@
     row_count = response.shape[0] * lax.axis_size("inner") * lax.axis_size("wide")
     bit = jnp.reshape(lax.axis_index("wide") & 1, (1,)).astype(jnp.int32)
     keep, send = gram_halves(response, row_count, bit)
-    partial_sum = keep + partner_xor(send, "wide", 0, 1)
+    addends = [keep, partner_xor(send, "wide", 0, 1)]
     groups = axis_groups("inner", 0) + axis_groups("wide", 1)
     for group in groups:
-        partial_sum = scatter_sum(partial_sum, *group)
+        partial_sum = scatter_sum(addends, *group)
+        addends = [partial_sum]
     for group in reversed(groups):
         partial_sum = gather_all(partial_sum, *group)
     got = partner_xor(partial_sum, "wide", 0, 1)

time: 110 us -> 111 us (level)
  no operation moved by 1% of the time
where the time goes in v6:
time: 111 us; the launch traced here: 110 us
  Pallas kernels  65.1 us (59%)
  waiting for transfers between devices  24.3 us (22%)
  starting transfers between devices  17.2 us (15%)
  other arithmetic  2.05 us (2%)
    pallas_call x1, Pallas kernels, cholesky_and_inverse(): pl.pallas_call(chol_kernel, out_shape=(jax.ShapeDtypeStruct((n, n), jnp.f...  48.2 us
    ppermute x14, waiting for transfers between devices, partner_xor(): return lax.ppermute(value, axis, pairs)  24.3 us
    ppermute x14, starting transfers between devices, partner_xor(): return lax.ppermute(value, axis, pairs)  17.2 us
    pallas_call x1, Pallas kernels, rows_times(): pl.pallas_call(rows_kernel, out_shape=jax.ShapeDtypeStruct((rows, weights...  8.46 us
    pallas_call x1, Pallas kernels, gram_halves(): pl.pallas_call(functools.partial(gram_kernel, row_count), out_shape=(half...  8.46 us
  transfers between devices with their start and end apart: 14, of which 11 were waited for; matrix products, arithmetic and copies ran while one was open for 0% of the time, Pallas kernels for 0%

profile of v6, /device:TPU:0, one launch (start us, length us, event | category | flops | bytes accessed | tf_op | source)
XLA Modules:
  0.0 110.4 jit_solution(6279444249784248205)
XLA Ops:
  0.6 8.5 %shard_map.30 = (f32[256,512]{1,0:T(8,128)}, f32[256,512]{1,0:T(8,128)}) custom-call(s32[1]{0:T(128)} %bitcast.bit_ref, f32[2048,512]{1,0:T(8,128)} %a_ref.3), custom_call_target="tpu_custom_call" | custom-call | tf_op jit(solution)/shard_map/pallas_call | solution.py:160
  9.6 1.7 %collective-permute-done = f32[256,512]{1,0:T(8,128)S(1)} collective-permute-done((f32[256,512]{1,0:T(8,128)}, f32[256,512]{1,0:T(8,128)S(1)}, u32[]{:S(2)}, u32[]{:S(2)}) %collective-permute-start) | collective-permute-done | bytes 524320 | tf_op jit(solution)/shard_map/ppermute | solution.py:183
  11.3 1.1 dynamic-slice_add_fusion.2
  12.4 2.9 %collective-permute-start.1 = (f32[64,512]{1,0:T(8,128)S(1)}, f32[64,512]{1,0:T(8,128)S(1)}, u32[]{:S(2)}, u32[]{:S(2)}) collective-permute-start(f32[64,512]{1,0:T(8,128)S(1)} %get-tuple-element.12), channel_id=1, source_target_pairs={{0,8},{8,0},{16,24},{24,16},{1,9},{9,1},{17,25},{25,17},{2,10},{10... | collective-permute-start | bytes 393224 | tf_op jit(solution)/shard_map/ppermute | solution.py:183
  15.3 1.5 %collective-permute-start.3 = (f32[64,512]{1,0:T(8,128)S(1)}, f32[64,512]{1,0:T(8,128)S(1)}, u32[]{:S(2)}, u32[]{:S(2)}) collective-permute-start(f32[64,512]{1,0:T(8,128)S(1)} %get-tuple-element.13), channel_id=1, source_target_pairs={{0,24},{8,16},{16,8},{24,0},{1,25},{9,17},{17,9},{25,1},{2,26},{10... | collective-permute-start | bytes 393224 | tf_op jit(solution)/shard_map/ppermute | solution.py:183
  16.8 2.6 %collective-permute-done.1 = f32[64,512]{1,0:T(8,128)S(1)} collective-permute-done((f32[64,512]{1,0:T(8,128)S(1)}, f32[64,512]{1,0:T(8,128)S(1)}, u32[]{:S(2)}, u32[]{:S(2)}) %collective-permute-start.1) | collective-permute-done | bytes 131104 | tf_op jit(solution)/shard_map/ppermute | solution.py:183
  19.4 3.8 %collective-permute-done.3 = f32[64,512]{1,0:T(8,128)S(1)} collective-permute-done((f32[64,512]{1,0:T(8,128)S(1)}, f32[64,512]{1,0:T(8,128)S(1)}, u32[]{:S(2)}, u32[]{:S(2)}) %collective-permute-start.3) | collective-permute-done | bytes 131104 | tf_op jit(solution)/shard_map/ppermute | solution.py:183
  23.2 1.4 %collective-permute-done.2 = f32[64,512]{1,0:T(8,128)S(1)} collective-permute-done((f32[64,512]{1,0:T(8,128)S(1)}, f32[64,512]{1,0:T(8,128)S(1)}, u32[]{:S(2)}, u32[]{:S(2)}) %collective-permute-start.2) | collective-permute-done | bytes 131104 | tf_op jit(solution)/shard_map/ppermute | solution.py:183
  24.6 0.9 add_add_fusion
  25.6 1.6 %collective-permute-start.4 = (f32[16,512]{1,0:T(8,128)S(1)}, f32[16,512]{1,0:T(8,128)S(1)}, u32[]{:S(2)}, u32[]{:S(2)}) collective-permute-start(f32[16,512]{1,0:T(8,128)S(1)} %get-tuple-element.15), channel_id=1, source_target_pairs={{0,2},{1,3},{2,0},{3,1},{4,6},{5,7},{6,4},{7,5},{8,10},{9,11},{10,... | collective-permute-start | bytes 98312 | tf_op jit(solution)/shard_map/ppermute | solution.py:183
  27.2 2.5 %collective-permute-start.6 = (f32[16,512]{1,0:T(8,128)S(1)}, f32[16,512]{1,0:T(8,128)S(1)}, u32[]{:S(2)}, u32[]{:S(2)}) collective-permute-start(f32[16,512]{1,0:T(8,128)S(1)} %get-tuple-element.16), channel_id=1, source_target_pairs={{0,6},{1,7},{2,4},{3,5},{4,2},{5,3},{6,0},{7,1},{8,14},{9,15},{10,... | collective-permute-start | bytes 98312 | tf_op jit(solution)/shard_map/ppermute | solution.py:183
  29.8 3.1 %collective-permute-done.6 = f32[16,512]{1,0:T(8,128)S(1)} collective-permute-done((f32[16,512]{1,0:T(8,128)S(1)}, f32[16,512]{1,0:T(8,128)S(1)}, u32[]{:S(2)}, u32[]{:S(2)}) %collective-permute-start.6) | collective-permute-done | bytes 32800 | tf_op jit(solution)/shard_map/ppermute | solution.py:183
  32.9 1.9 %collective-permute-done.5 = f32[16,512]{1,0:T(8,128)S(1)} collective-permute-done((f32[16,512]{1,0:T(8,128)S(1)}, f32[16,512]{1,0:T(8,128)S(1)}, u32[]{:S(2)}, u32[]{:S(2)}) %collective-permute-start.5) | collective-permute-done | bytes 32800 | tf_op jit(solution)/shard_map/ppermute | solution.py:183
  35.4 1.4 %collective-permute-start.8 = (f32[16,512]{1,0:T(8,128)S(1)}, f32[16,512]{1,0:T(8,128)S(1)}, u32[]{:S(2)}, u32[]{:S(2)}) collective-permute-start(f32[16,512]{1,0:T(8,128)S(1)} %get-tuple-element.11), channel_id=1, source_target_pairs={{0,4},{1,5},{2,6},{3,7},{4,0},{5,1},{6,2},{7,3},{8,12},{9,13},{10,... | collective-permute-start | bytes 98312 | tf_op jit(solution)/shard_map/ppermute | solution.py:183
  36.8 2.6 %collective-permute-start.9 = (f32[16,512]{1,0:T(8,128)S(1)}, f32[16,512]{1,0:T(8,128)S(1)}, u32[]{:S(2)}, u32[]{:S(2)}) collective-permute-start(f32[16,512]{1,0:T(8,128)S(1)} %get-tuple-element.11), channel_id=1, source_target_pairs={{0,6},{1,7},{2,4},{3,5},{4,2},{5,3},{6,0},{7,1},{8,14},{9,15},{10,... | collective-permute-start | bytes 98312 | tf_op jit(solution)/shard_map/ppermute | solution.py:183
  39.4 0.8 collective-permute-done.8
  40.2 2.3 %collective-permute-done.9 = f32[16,512]{1,0:T(8,128)S(1)} collective-permute-done((f32[16,512]{1,0:T(8,128)S(1)}, f32[16,512]{1,0:T(8,128)S(1)}, u32[]{:S(2)}, u32[]{:S(2)}) %collective-permute-start.9) | collective-permute-done | bytes 32800 | tf_op jit(solution)/shard_map/ppermute | solution.py:183
  42.5 1.5 %collective-permute-start.10 = (f32[64,512]{1,0:T(8,128)S(1)}, f32[64,512]{1,0:T(8,128)S(1)}, u32[]{:S(2)}, u32[]{:S(2)}) collective-permute-start(f32[64,512]{1,0:T(8,128)S(1)} %constant_dynamic-update-slice_fusion), channel_id=1, source_target_pairs={{0,8},{8,0},{16,24},{24,16},{1,9},{9,1},{17,25},{25,17},{2,10},{10... | collective-permute-start | bytes 393224 | tf_op jit(solution)/shard_map/ppermute | solution.py:183
  44.5 1.5 %collective-permute-start.11 = (f32[64,512]{1,0:T(8,128)S(1)}, f32[64,512]{1,0:T(8,128)S(1)}, u32[]{:S(2)}, u32[]{:S(2)}) collective-permute-start(f32[64,512]{1,0:T(8,128)S(1)} %constant_dynamic-update-slice_fusion), channel_id=1, source_target_pairs={{0,16},{8,24},{16,0},{24,8},{1,17},{9,25},{17,1},{25,9},{2,18},{10... | collective-permute-start | bytes 393224 | tf_op jit(solution)/shard_map/ppermute | solution.py:183
  46.1 1.4 %collective-permute-done.10 = f32[64,512]{1,0:T(8,128)S(1)} collective-permute-done((f32[64,512]{1,0:T(8,128)S(1)}, f32[64,512]{1,0:T(8,128)S(1)}, u32[]{:S(2)}, u32[]{:S(2)}) %collective-permute-start.10) | collective-permute-done | bytes 131104 | tf_op jit(solution)/shard_map/ppermute | solution.py:183
  47.5 3.4 %collective-permute-done.11 = f32[64,512]{1,0:T(8,128)S(1)} collective-permute-done((f32[64,512]{1,0:T(8,128)S(1)}, f32[64,512]{1,0:T(8,128)S(1)}, u32[]{:S(2)}, u32[]{:S(2)}) %collective-permute-start.11) | collective-permute-done | bytes 131104 | tf_op jit(solution)/shard_map/ppermute | solution.py:183
  51.0 1.9 %collective-permute-done.13.got_ref = f32[256,512]{1,0:T(8,128)S(1)} collective-permute-done((f32[256,512]{1,0:T(8,128)S(1)}, f32[256,512]{1,0:T(8,128)S(1)}, u32[]{:S(2)}, u32[]{:S(2)}) %collective-permute-start.13) | collective-permute-done | bytes 524320 | tf_op jit(solution)/shard_map/ppermute | solution.py:183
  53.7 48.2 %shard_map.31 = (f32[512,512]{1,0:T(8,128)}, f32[512,512]{1,0:T(8,128)}) custom-call(s32[1]{0:T(128)} %bitcast.bit_ref, f32[256,512]{1,0:T(8,128)} %copy-done, f32[256,512]{1,0:T(8,128)} %copy-done.1), custom_call_target="tpu_custom_call" | custom-call | tf_op jit(solution)/shard_map/pallas_call | solution.py:82
  101.9 8.5 %shard_map.32 = f32[2048,512]{1,0:T(8,128)} custom-call(f32[2048,512]{1,0:T(8,128)} %a_ref.3, f32[512,512]{1,0:T(8,128)} %get-tuple-element.9.w_ref), custom_call_target="tpu_custom_call" | custom-call | tf_op jit(solution)/shard_map/pallas_call | solution.py:101
  (24 shorter events, 2.7 us)
Async XLA Ops:
  9.1 2.2 %collective-permute-start = (f32[256,512]{1,0:T(8,128)}, f32[256,512]{1,0:T(8,128)S(1)}, u32[]{:S(2)}, u32[]{:S(2)}) collective-permute-start(f32[256,512]{1,0:T(8,128)} %get-tuple-element.7), channel_id=1, source_target_pairs={{0,1},{1,0},{2,3},{3,2},{4,5},{5,4},{6,7},{7,6},{8,9},{9,8},{10,11... | collective-permute-start | bytes 1572872 | tf_op jit(solution)/shard_map/ppermute | solution.py:183
  12.4 7.0 %collective-permute-start.1 = (f32[64,512]{1,0:T(8,128)S(1)}, f32[64,512]{1,0:T(8,128)S(1)}, u32[]{:S(2)}, u32[]{:S(2)}) collective-permute-start(f32[64,512]{1,0:T(8,128)S(1)} %get-tuple-element.12), channel_id=1, source_target_pairs={{0,8},{8,0},{16,24},{24,16},{1,9},{9,1},{17,25},{25,17},{2,10},{10... | collective-permute-start | bytes 393224 | tf_op jit(solution)/shard_map/ppermute | solution.py:183
  15.3 7.9 %collective-permute-start.3 = (f32[64,512]{1,0:T(8,128)S(1)}, f32[64,512]{1,0:T(8,128)S(1)}, u32[]{:S(2)}, u32[]{:S(2)}) collective-permute-start(f32[64,512]{1,0:T(8,128)S(1)} %get-tuple-element.13), channel_id=1, source_target_pairs={{0,24},{8,16},{16,8},{24,0},{1,25},{9,17},{17,9},{25,1},{2,26},{10... | collective-permute-start | bytes 393224 | tf_op jit(solution)/shard_map/ppermute | solution.py:183
  16.8 7.8 %collective-permute-start.2 = (f32[64,512]{1,0:T(8,128)S(1)}, f32[64,512]{1,0:T(8,128)S(1)}, u32[]{:S(2)}, u32[]{:S(2)}) collective-permute-start(f32[64,512]{1,0:T(8,128)S(1)} %get-tuple-element.14), channel_id=1, source_target_pairs={{0,16},{8,24},{16,0},{24,8},{1,17},{9,25},{17,1},{25,9},{2,18},{10... | collective-permute-start | bytes 393224 | tf_op jit(solution)/shard_map/ppermute | solution.py:183
  25.6 4.2 %collective-permute-start.4 = (f32[16,512]{1,0:T(8,128)S(1)}, f32[16,512]{1,0:T(8,128)S(1)}, u32[]{:S(2)}, u32[]{:S(2)}) collective-permute-start(f32[16,512]{1,0:T(8,128)S(1)} %get-tuple-element.15), channel_id=1, source_target_pairs={{0,2},{1,3},{2,0},{3,1},{4,6},{5,7},{6,4},{7,5},{8,10},{9,11},{10,... | collective-permute-start | bytes 98312 | tf_op jit(solution)/shard_map/ppermute | solution.py:183
  27.2 5.7 %collective-permute-start.6 = (f32[16,512]{1,0:T(8,128)S(1)}, f32[16,512]{1,0:T(8,128)S(1)}, u32[]{:S(2)}, u32[]{:S(2)}) collective-permute-start(f32[16,512]{1,0:T(8,128)S(1)} %get-tuple-element.16), channel_id=1, source_target_pairs={{0,6},{1,7},{2,4},{3,5},{4,2},{5,3},{6,0},{7,1},{8,14},{9,15},{10,... | collective-permute-start | bytes 98312 | tf_op jit(solution)/shard_map/ppermute | solution.py:183
  29.7 5.2 %collective-permute-start.5 = (f32[16,512]{1,0:T(8,128)S(1)}, f32[16,512]{1,0:T(8,128)S(1)}, u32[]{:S(2)}, u32[]{:S(2)}) collective-permute-start(f32[16,512]{1,0:T(8,128)S(1)} %get-tuple-element.17), channel_id=1, source_target_pairs={{0,4},{1,5},{2,6},{3,7},{4,0},{5,1},{6,2},{7,3},{8,12},{9,13},{10,... | collective-permute-start | bytes 98312 | tf_op jit(solution)/shard_map/ppermute | solution.py:183
  34.9 4.5 %collective-permute-start.7 = (f32[16,512]{1,0:T(8,128)S(1)}, f32[16,512]{1,0:T(8,128)S(1)}, u32[]{:S(2)}, u32[]{:S(2)}) collective-permute-start(f32[16,512]{1,0:T(8,128)S(1)} %get-tuple-element.11), channel_id=1, source_target_pairs={{0,2},{1,3},{2,0},{3,1},{4,6},{5,7},{6,4},{7,5},{8,10},{9,11},{10,... | collective-permute-start | bytes 98312 | tf_op jit(solution)/shard_map/ppermute | solution.py:183
  35.4 4.8 %collective-permute-start.8 = (f32[16,512]{1,0:T(8,128)S(1)}, f32[16,512]{1,0:T(8,128)S(1)}, u32[]{:S(2)}, u32[]{:S(2)}) collective-permute-start(f32[16,512]{1,0:T(8,128)S(1)} %get-tuple-element.11), channel_id=1, source_target_pairs={{0,4},{1,5},{2,6},{3,7},{4,0},{5,1},{6,2},{7,3},{8,12},{9,13},{10,... | collective-permute-start | bytes 98312 | tf_op jit(solution)/shard_map/ppermute | solution.py:183
  36.8 5.7 %collective-permute-start.9 = (f32[16,512]{1,0:T(8,128)S(1)}, f32[16,512]{1,0:T(8,128)S(1)}, u32[]{:S(2)}, u32[]{:S(2)}) collective-permute-start(f32[16,512]{1,0:T(8,128)S(1)} %get-tuple-element.11), channel_id=1, source_target_pairs={{0,6},{1,7},{2,4},{3,5},{4,2},{5,3},{6,0},{7,1},{8,14},{9,15},{10,... | collective-permute-start | bytes 98312 | tf_op jit(solution)/shard_map/ppermute | solution.py:183
  42.5 5.0 %collective-permute-start.10 = (f32[64,512]{1,0:T(8,128)S(1)}, f32[64,512]{1,0:T(8,128)S(1)}, u32[]{:S(2)}, u32[]{:S(2)}) collective-permute-start(f32[64,512]{1,0:T(8,128)S(1)} %constant_dynamic-update-slice_fusion), channel_id=1, source_target_pairs={{0,8},{8,0},{16,24},{24,16},{1,9},{9,1},{17,25},{25,17},{2,10},{10... | collective-permute-start | bytes 393224 | tf_op jit(solution)/shard_map/ppermute | solution.py:183
  44.0 6.9 %collective-permute-start.12 = (f32[64,512]{1,0:T(8,128)S(1)}, f32[64,512]{1,0:T(8,128)S(1)}, u32[]{:S(2)}, u32[]{:S(2)}) collective-permute-start(f32[64,512]{1,0:T(8,128)S(1)} %constant_dynamic-update-slice_fusion), channel_id=1, source_target_pairs={{0,24},{8,16},{16,8},{24,0},{1,25},{9,17},{17,9},{25,1},{2,26},{10... | collective-permute-start | bytes 393224 | tf_op jit(solution)/shard_map/ppermute | solution.py:183
  44.5 6.4 %collective-permute-start.11 = (f32[64,512]{1,0:T(8,128)S(1)}, f32[64,512]{1,0:T(8,128)S(1)}, u32[]{:S(2)}, u32[]{:S(2)}) collective-permute-start(f32[64,512]{1,0:T(8,128)S(1)} %constant_dynamic-update-slice_fusion), channel_id=1, source_target_pairs={{0,16},{8,24},{16,0},{24,8},{1,17},{9,25},{17,1},{25,9},{2,18},{10... | collective-permute-start | bytes 393224 | tf_op jit(solution)/shard_map/ppermute | solution.py:183
  50.9 2.0 %copy-start = (f32[256,512]{1,0:T(8,128)}, f32[256,512]{1,0:T(8,128)S(1)}, u32[]{:S(2)}) copy-start(f32[256,512]{1,0:T(8,128)S(1)} %constant_dynamic-update-slice_fusion.4.mine_ref) | copy-start | bytes 1572868
  50.9 2.0 %collective-permute-start.13 = (f32[256,512]{1,0:T(8,128)S(1)}, f32[256,512]{1,0:T(8,128)S(1)}, u32[]{:S(2)}, u32[]{:S(2)}) collective-permute-start(f32[256,512]{1,0:T(8,128)S(1)} %constant_dynamic-update-slice_fusion.4.mine_ref), channel_id=1, source_target_pairs={{0,1},{1,0},{2,3},{3,2},{4,5},{5,4},{6,7},{7,6},{8,9},{9,8},{10,11... | collective-permute-start | bytes 1572872 | tf_op jit(solution)/shard_map/ppermute | solution.py:183
  52.9 0.8 copy-start.1

commit v7 on v3

--- a/solution.py
+++ b/solution.py
@@ -153,9 +153,10 @@
 
 
 def all_sum(gram_matrix):
-    groups = [("wide", 0, 2)] + axis_groups("inner", 0) + axis_groups("wide", 1)
+    groups = axis_groups("inner", 0) + axis_groups("wide", 1)
     for group in groups:
         gram_matrix = scatter_sum(gram_matrix, *group)
+    gram_matrix = gram_matrix + partner_xor(gram_matrix, "wide", 0, 1)
     for group in reversed(groups):
         gram_matrix = gather_all(gram_matrix, *group)
     return gram_matrix

time: 111 us -> 120 us (1.081)
  waiting for transfers between devices: 23.9 us -> 34.1 us
    ppermute x14 -> x13, waiting for transfers between devices: 23.9 us -> 34.1 us  [partner_xor(): return lax.ppermute(value, axis, pairs)]
    ppermute x14 -> x13, starting transfers between devices: 17.2 us -> 16.9 us  [partner_xor(): return lax.ppermute(value, axis, pairs)]
  transfers between devices with their start and end apart: 14 -> 13, of which waited for: 11 -> 11; matrix products, arithmetic and copies ran while one was open for 0% -> 0% of each run, Pallas kernels for 0% -> 0%
where the time goes in v7:
time: 120 us
  Pallas kernels  56.5 us (47%)
  waiting for transfers between devices  34.1 us (28%)
  starting transfers between devices  16.9 us (14%)
  matrix products  10.5 us (9%)
  local copies, waits for them, and re-layouts  1.31 us (1%)
    pallas_call x1, Pallas kernels, cholesky_and_inverse(): pl.pallas_call(chol_kernel, out_shape=(jax.ShapeDtypeStruct((n, n), jnp.f...  48 us
    ppermute x13, waiting for transfers between devices, partner_xor(): return lax.ppermute(value, axis, pairs)  34.1 us
    ppermute x13, starting transfers between devices, partner_xor(): return lax.ppermute(value, axis, pairs)  16.9 us
    dot_general x1, matrix products, gram_of(): lax.dot_general(matrix, matrix, (((0,), (0,)), ((), ())), precision=lax.P...  10.5 us
    pallas_call x1, Pallas kernels, rows_times(): pl.pallas_call(rows_kernel, out_shape=jax.ShapeDtypeStruct((rows, weights...  8.46 us
  transfers between devices with their start and end apart: 13, of which 11 were waited for; matrix products, arithmetic and copies ran while one was open for 0% of the time, Pallas kernels for 0%

profile of v7, /device:TPU:0, one launch (start us, length us, event | category | flops | bytes accessed | tf_op | source)
XLA Modules:
  0.0 120.2 jit_solution(14066928760573737166)
XLA Ops:
  0.6 10.5 %convolution_multiply_fusion = f32[512,512]{1,0:T(8,128)S(1)} fusion(f32[2048,512]{1,0:T(8,128)} %a_ref.1), kind=kOutput, calls=%fused_computation | convolution fusion | flops 6442713088 | bytes 5242880 | tf_op jit(solution)/shard_map/dot_general | solution.py:104
  11.2 3.0 %collective-permute-start = (f32[128,512]{1,0:T(8,128)S(1)}, f32[128,512]{1,0:T(8,128)S(1)}, u32[]{:S(2)}, u32[]{:S(2)}) collective-permute-start(f32[128,512]{1,0:T(8,128)S(1)} %get-tuple-element.8), channel_id=1, source_target_pairs={{0,8},{8,0},{16,24},{24,16},{1,9},{9,1},{17,25},{25,17},{2,10},{10... | collective-permute-start | bytes 786440 | tf_op jit(solution)/shard_map/ppermute | solution.py:120
  14.2 1.5 %collective-permute-start.2 = (f32[128,512]{1,0:T(8,128)S(1)}, f32[128,512]{1,0:T(8,128)S(1)}, u32[]{:S(2)}, u32[]{:S(2)}) collective-permute-start(f32[128,512]{1,0:T(8,128)S(1)} %get-tuple-element.9), channel_id=1, source_target_pairs={{0,24},{8,16},{16,8},{24,0},{1,25},{9,17},{17,9},{25,1},{2,26},{10... | collective-permute-start | bytes 786440 | tf_op jit(solution)/shard_map/ppermute | solution.py:120
  15.8 5.6 %collective-permute-done = f32[128,512]{1,0:T(8,128)S(1)} collective-permute-done((f32[128,512]{1,0:T(8,128)S(1)}, f32[128,512]{1,0:T(8,128)S(1)}, u32[]{:S(2)}, u32[]{:S(2)}) %collective-permute-start) | collective-permute-done | bytes 262176 | tf_op jit(solution)/shard_map/ppermute | solution.py:120
  21.4 6.1 %collective-permute-done.2 = f32[128,512]{1,0:T(8,128)S(1)} collective-permute-done((f32[128,512]{1,0:T(8,128)S(1)}, f32[128,512]{1,0:T(8,128)S(1)}, u32[]{:S(2)}, u32[]{:S(2)}) %collective-permute-start.2) | collective-permute-done | bytes 262176 | tf_op jit(solution)/shard_map/ppermute | solution.py:120
  27.5 1.4 %collective-permute-done.1 = f32[128,512]{1,0:T(8,128)S(1)} collective-permute-done((f32[128,512]{1,0:T(8,128)S(1)}, f32[128,512]{1,0:T(8,128)S(1)}, u32[]{:S(2)}, u32[]{:S(2)}) %collective-permute-start.1) | collective-permute-done | bytes 262176 | tf_op jit(solution)/shard_map/ppermute | solution.py:120
  29.0 1.6 %collective-permute-start.3 = (f32[32,512]{1,0:T(8,128)S(1)}, f32[32,512]{1,0:T(8,128)S(1)}, u32[]{:S(2)}, u32[]{:S(2)}) collective-permute-start(f32[32,512]{1,0:T(8,128)S(1)} %get-tuple-element.11), channel_id=1, source_target_pairs={{0,2},{1,3},{2,0},{3,1},{4,6},{5,7},{6,4},{7,5},{8,10},{9,11},{10,... | collective-permute-start | bytes 196616 | tf_op jit(solution)/shard_map/ppermute | solution.py:120
  30.6 2.5 %collective-permute-start.5 = (f32[32,512]{1,0:T(8,128)S(1)}, f32[32,512]{1,0:T(8,128)S(1)}, u32[]{:S(2)}, u32[]{:S(2)}) collective-permute-start(f32[32,512]{1,0:T(8,128)S(1)} %get-tuple-element.12), channel_id=1, source_target_pairs={{0,6},{1,7},{2,4},{3,5},{4,2},{5,3},{6,0},{7,1},{8,14},{9,15},{10,... | collective-permute-start | bytes 196616 | tf_op jit(solution)/shard_map/ppermute | solution.py:120
  33.2 0.5 collective-permute-done.3
  33.7 3.0 %collective-permute-done.5 = f32[32,512]{1,0:T(8,128)S(1)} collective-permute-done((f32[32,512]{1,0:T(8,128)S(1)}, f32[32,512]{1,0:T(8,128)S(1)}, u32[]{:S(2)}, u32[]{:S(2)}) %collective-permute-start.5) | collective-permute-done | bytes 65568 | tf_op jit(solution)/shard_map/ppermute | solution.py:120
  36.7 2.3 %collective-permute-done.4 = f32[32,512]{1,0:T(8,128)S(1)} collective-permute-done((f32[32,512]{1,0:T(8,128)S(1)}, f32[32,512]{1,0:T(8,128)S(1)}, u32[]{:S(2)}, u32[]{:S(2)}) %collective-permute-start.4) | collective-permute-done | bytes 65568 | tf_op jit(solution)/shard_map/ppermute | solution.py:120
  39.0 1.2 %collective-permute-done.6 = f32[32,512]{1,0:T(8,128)S(1)} collective-permute-done((f32[32,512]{1,0:T(8,128)S(1)}, f32[32,512]{1,0:T(8,128)S(1)}, u32[]{:S(2)}, u32[]{:S(2)}) %collective-permute-start.6) | collective-permute-done | bytes 65568 | tf_op jit(solution)/shard_map/ppermute | solution.py:120
  40.5 2.1 %collective-permute-start.8 = (f32[32,512]{1,0:T(8,128)S(1)}, f32[32,512]{1,0:T(8,128)S(1)}, u32[]{:S(2)}, u32[]{:S(2)}) collective-permute-start(f32[32,512]{1,0:T(8,128)S(1)} %get-tuple-element.7), channel_id=1, source_target_pairs={{0,4},{1,5},{2,6},{3,7},{4,0},{5,1},{6,2},{7,3},{8,12},{9,13},{10,... | collective-permute-start | bytes 196616 | tf_op jit(solution)/shard_map/ppermute | solution.py:120
  42.6 2.2 %collective-permute-start.9 = (f32[32,512]{1,0:T(8,128)S(1)}, f32[32,512]{1,0:T(8,128)S(1)}, u32[]{:S(2)}, u32[]{:S(2)}) collective-permute-start(f32[32,512]{1,0:T(8,128)S(1)} %get-tuple-element.7), channel_id=1, source_target_pairs={{0,6},{1,7},{2,4},{3,5},{4,2},{5,3},{6,0},{7,1},{8,14},{9,15},{10,... | collective-permute-start | bytes 196616 | tf_op jit(solution)/shard_map/ppermute | solution.py:120
  44.8 0.8 collective-permute-done.7
  45.6 3.5 %collective-permute-done.8 = f32[32,512]{1,0:T(8,128)S(1)} collective-permute-done((f32[32,512]{1,0:T(8,128)S(1)}, f32[32,512]{1,0:T(8,128)S(1)}, u32[]{:S(2)}, u32[]{:S(2)}) %collective-permute-start.8) | collective-permute-done | bytes 65568 | tf_op jit(solution)/shard_map/ppermute | solution.py:120
  49.1 1.6 %collective-permute-start.10 = (f32[128,512]{1,0:T(8,128)S(1)}, f32[128,512]{1,0:T(8,128)S(1)}, u32[]{:S(2)}, u32[]{:S(2)}) collective-permute-start(f32[128,512]{1,0:T(8,128)S(1)} %constant_dynamic-update-slice_fusion.4), channel_id=1, source_target_pairs={{0,8},{8,0},{16,24},{24,16},{1,9},{9,1},{17,25},{25,17},{2,10},{10... | collective-permute-start | bytes 786440 | tf_op jit(solution)/shard_map/ppermute | solution.py:120
  50.6 0.5 collective-permute-start.11
  51.2 1.5 %collective-permute-start.12 = (f32[128,512]{1,0:T(8,128)S(1)}, f32[128,512]{1,0:T(8,128)S(1)}, u32[]{:S(2)}, u32[]{:S(2)}) collective-permute-start(f32[128,512]{1,0:T(8,128)S(1)} %constant_dynamic-update-slice_fusion.4), channel_id=1, source_target_pairs={{0,24},{8,16},{16,8},{24,0},{1,25},{9,17},{17,9},{25,1},{2,26},{10... | collective-permute-start | bytes 786440 | tf_op jit(solution)/shard_map/ppermute | solution.py:120
  52.8 5.6 %collective-permute-done.10 = f32[128,512]{1,0:T(8,128)S(1)} collective-permute-done((f32[128,512]{1,0:T(8,128)S(1)}, f32[128,512]{1,0:T(8,128)S(1)}, u32[]{:S(2)}, u32[]{:S(2)}) %collective-permute-start.10) | collective-permute-done | bytes 262176 | tf_op jit(solution)/shard_map/ppermute | solution.py:120
  58.4 4.2 %collective-permute-done.11 = f32[128,512]{1,0:T(8,128)S(1)} collective-permute-done((f32[128,512]{1,0:T(8,128)S(1)}, f32[128,512]{1,0:T(8,128)S(1)}, u32[]{:S(2)}, u32[]{:S(2)}) %collective-permute-start.11) | collective-permute-done | bytes 262176 | tf_op jit(solution)/shard_map/ppermute | solution.py:120
  62.8 1.0 copy-done
  63.7 48.0 %shard_map.30 = (f32[512,512]{1,0:T(8,128)}, f32[512,512]{1,0:T(8,128)}) custom-call(f32[512,512]{1,0:T(8,128)} %copy-done), custom_call_target="tpu_custom_call" | custom-call | tf_op jit(solution)/shard_map/pallas_call | solution.py:68
  111.7 8.5 %shard_map.31 = f32[2048,512]{1,0:T(8,128)} custom-call(f32[2048,512]{1,0:T(8,128)} %a_ref.1, f32[512,512]{1,0:T(8,128)} %get-tuple-element.5.w_ref), custom_call_target="tpu_custom_call" | custom-call | tf_op jit(solution)/shard_map/pallas_call | solution.py:87
  (21 shorter events, 0.9 us)
Async XLA Ops:
  11.2 10.1 %collective-permute-start = (f32[128,512]{1,0:T(8,128)S(1)}, f32[128,512]{1,0:T(8,128)S(1)}, u32[]{:S(2)}, u32[]{:S(2)}) collective-permute-start(f32[128,512]{1,0:T(8,128)S(1)} %get-tuple-element.8), channel_id=1, source_target_pairs={{0,8},{8,0},{16,24},{24,16},{1,9},{9,1},{17,25},{25,17},{2,10},{10... | collective-permute-start | bytes 786440 | tf_op jit(solution)/shard_map/ppermute | solution.py:120
  14.2 13.2 %collective-permute-start.2 = (f32[128,512]{1,0:T(8,128)S(1)}, f32[128,512]{1,0:T(8,128)S(1)}, u32[]{:S(2)}, u32[]{:S(2)}) collective-permute-start(f32[128,512]{1,0:T(8,128)S(1)} %get-tuple-element.9), channel_id=1, source_target_pairs={{0,24},{8,16},{16,8},{24,0},{1,25},{9,17},{17,9},{25,1},{2,26},{10... | collective-permute-start | bytes 786440 | tf_op jit(solution)/shard_map/ppermute | solution.py:120
  15.7 13.1 %collective-permute-start.1 = (f32[128,512]{1,0:T(8,128)S(1)}, f32[128,512]{1,0:T(8,128)S(1)}, u32[]{:S(2)}, u32[]{:S(2)}) collective-permute-start(f32[128,512]{1,0:T(8,128)S(1)} %get-tuple-element.10), channel_id=1, source_target_pairs={{0,16},{8,24},{16,0},{24,8},{1,17},{9,25},{17,1},{25,9},{2,18},{10... | collective-permute-start | bytes 786440 | tf_op jit(solution)/shard_map/ppermute | solution.py:120
  29.0 4.7 %collective-permute-start.3 = (f32[32,512]{1,0:T(8,128)S(1)}, f32[32,512]{1,0:T(8,128)S(1)}, u32[]{:S(2)}, u32[]{:S(2)}) collective-permute-start(f32[32,512]{1,0:T(8,128)S(1)} %get-tuple-element.11), channel_id=1, source_target_pairs={{0,2},{1,3},{2,0},{3,1},{4,6},{5,7},{6,4},{7,5},{8,10},{9,11},{10,... | collective-permute-start | bytes 196616 | tf_op jit(solution)/shard_map/ppermute | solution.py:120
  30.6 6.1 %collective-permute-start.5 = (f32[32,512]{1,0:T(8,128)S(1)}, f32[32,512]{1,0:T(8,128)S(1)}, u32[]{:S(2)}, u32[]{:S(2)}) collective-permute-start(f32[32,512]{1,0:T(8,128)S(1)} %get-tuple-element.12), channel_id=1, source_target_pairs={{0,6},{1,7},{2,4},{3,5},{4,2},{5,3},{6,0},{7,1},{8,14},{9,15},{10,... | collective-permute-start | bytes 196616 | tf_op jit(solution)/shard_map/ppermute | solution.py:120
  33.1 5.9 %collective-permute-start.4 = (f32[32,512]{1,0:T(8,128)S(1)}, f32[32,512]{1,0:T(8,128)S(1)}, u32[]{:S(2)}, u32[]{:S(2)}) collective-permute-start(f32[32,512]{1,0:T(8,128)S(1)} %get-tuple-element.13), channel_id=1, source_target_pairs={{0,4},{1,5},{2,6},{3,7},{4,0},{5,1},{6,2},{7,3},{8,12},{9,13},{10,... | collective-permute-start | bytes 196616 | tf_op jit(solution)/shard_map/ppermute | solution.py:120
  39.0 1.3 %collective-permute-start.6 = (f32[32,512]{1,0:T(8,128)S(1)}, f32[32,512]{1,0:T(8,128)S(1)}, u32[]{:S(2)}, u32[]{:S(2)}) collective-permute-start(f32[32,512]{1,0:T(8,128)S(1)} %add_add_fusion.1), channel_id=1, source_target_pairs={{0,1},{1,0},{2,3},{3,2},{4,5},{5,4},{6,7},{7,6},{8,9},{9,8},{10,11... | collective-permute-start | bytes 196616 | tf_op jit(solution)/shard_map/ppermute | solution.py:120
  40.3 5.2 %collective-permute-start.7 = (f32[32,512]{1,0:T(8,128)S(1)}, f32[32,512]{1,0:T(8,128)S(1)}, u32[]{:S(2)}, u32[]{:S(2)}) collective-permute-start(f32[32,512]{1,0:T(8,128)S(1)} %get-tuple-element.7), channel_id=1, source_target_pairs={{0,2},{1,3},{2,0},{3,1},{4,6},{5,7},{6,4},{7,5},{8,10},{9,11},{10,... | collective-permute-start | bytes 196616 | tf_op jit(solution)/shard_map/ppermute | solution.py:120
  40.5 8.6 %collective-permute-start.8 = (f32[32,512]{1,0:T(8,128)S(1)}, f32[32,512]{1,0:T(8,128)S(1)}, u32[]{:S(2)}, u32[]{:S(2)}) collective-permute-start(f32[32,512]{1,0:T(8,128)S(1)} %get-tuple-element.7), channel_id=1, source_target_pairs={{0,4},{1,5},{2,6},{3,7},{4,0},{5,1},{6,2},{7,3},{8,12},{9,13},{10,... | collective-permute-start | bytes 196616 | tf_op jit(solution)/shard_map/ppermute | solution.py:120
  42.6 6.5 %collective-permute-start.9 = (f32[32,512]{1,0:T(8,128)S(1)}, f32[32,512]{1,0:T(8,128)S(1)}, u32[]{:S(2)}, u32[]{:S(2)}) collective-permute-start(f32[32,512]{1,0:T(8,128)S(1)} %get-tuple-element.7), channel_id=1, source_target_pairs={{0,6},{1,7},{2,4},{3,5},{4,2},{5,3},{6,0},{7,1},{8,14},{9,15},{10,... | collective-permute-start | bytes 196616 | tf_op jit(solution)/shard_map/ppermute | solution.py:120
  49.1 9.3 %collective-permute-start.10 = (f32[128,512]{1,0:T(8,128)S(1)}, f32[128,512]{1,0:T(8,128)S(1)}, u32[]{:S(2)}, u32[]{:S(2)}) collective-permute-start(f32[128,512]{1,0:T(8,128)S(1)} %constant_dynamic-update-slice_fusion.4), channel_id=1, source_target_pairs={{0,8},{8,0},{16,24},{24,16},{1,9},{9,1},{17,25},{25,17},{2,10},{10... | collective-permute-start | bytes 786440 | tf_op jit(solution)/shard_map/ppermute | solution.py:120
  50.6 12.0 %collective-permute-start.11 = (f32[128,512]{1,0:T(8,128)S(1)}, f32[128,512]{1,0:T(8,128)S(1)}, u32[]{:S(2)}, u32[]{:S(2)}) collective-permute-start(f32[128,512]{1,0:T(8,128)S(1)} %constant_dynamic-update-slice_fusion.4), channel_id=1, source_target_pairs={{0,16},{8,24},{16,0},{24,8},{1,17},{9,25},{17,1},{25,9},{2,18},{10... | collective-permute-start | bytes 786440 | tf_op jit(solution)/shard_map/ppermute | solution.py:120
  51.2 11.6 %collective-permute-start.12 = (f32[128,512]{1,0:T(8,128)S(1)}, f32[128,512]{1,0:T(8,128)S(1)}, u32[]{:S(2)}, u32[]{:S(2)}) collective-permute-start(f32[128,512]{1,0:T(8,128)S(1)} %constant_dynamic-update-slice_fusion.4), channel_id=1, source_target_pairs={{0,24},{8,16},{16,8},{24,0},{1,25},{9,17},{17,9},{25,1},{2,26},{10... | collective-permute-start | bytes 786440 | tf_op jit(solution)/shard_map/ppermute | solution.py:120
  62.7 1.0 copy-start

commit v8 on v5

--- a/solution.py
+++ b/solution.py
@@ -51,15 +51,13 @@
         work_ref[0:half, :] = got_ref[...]
         work_ref[half:n, :] = mine_ref[...]
 
-    g = work_ref[...]
-    work_ref[...] = (g + g.T) * 0.5
     aug_ref[...] = jnp.zeros_like(aug_ref)
-    u_ref[...] = jnp.zeros_like(u_ref)
-    uinv_ref[...] = jnp.zeros_like(uinv_ref)
-    inv_ref[...] = jnp.zeros_like(inv_ref)
     blocks = n // BLOCK
     for k in range(blocks):
         lo, hi = k * BLOCK, (k + 1) * BLOCK
+        if hi < n:
+            u_ref[hi:n, lo:hi] = jnp.zeros((n - hi, BLOCK), jnp.float32)
+            uinv_ref[hi:n, lo:hi] = jnp.zeros((n - hi, BLOCK), jnp.float32)
         u_kk, inv_kk = sweep_block(work_ref[lo:hi, lo:hi])
         u_ref[lo:hi, lo:hi] = u_kk
         if k > 0:

time: 110 us -> 110 us (level)
  no operation moved by 1% of the time
where the time goes in v8:
time: 110 us
  Pallas kernels  65.1 us (59%)
  waiting for transfers between devices  24.3 us (22%)
  starting transfers between devices  17.2 us (16%)
  other arithmetic  1.18 us (1%)
    pallas_call x1, Pallas kernels, cholesky_and_inverse(): pl.pallas_call(chol_kernel, out_shape=(jax.ShapeDtypeStruct((n, n), jnp.f...  48.2 us
    ppermute x14, waiting for transfers between devices, partner_xor(): return lax.ppermute(value, axis, pairs)  24.3 us
    ppermute x14, starting transfers between devices, partner_xor(): return lax.ppermute(value, axis, pairs)  17.2 us
    pallas_call x1, Pallas kernels, rows_times(): pl.pallas_call(rows_kernel, out_shape=jax.ShapeDtypeStruct((rows, weights...  8.46 us
    pallas_call x1, Pallas kernels, gram_halves(): pl.pallas_call(functools.partial(gram_kernel, row_count), out_shape=(half...  8.46 us
  transfers between devices with their start and end apart: 14, of which 11 were waited for; matrix products, arithmetic and copies ran while one was open for 0% of the time, Pallas kernels for 0%

profile of v8, /device:TPU:0, one launch (start us, length us, event | category | flops | bytes accessed | tf_op | source)
XLA Modules:
  0.0 109.5 jit_solution(11735083953528394836)
XLA Ops:
  0.6 8.5 %shard_map.30 = (f32[256,512]{1,0:T(8,128)}, f32[256,512]{1,0:T(8,128)}) custom-call(s32[1]{0:T(128)} %bitcast.bit_ref, f32[2048,512]{1,0:T(8,128)} %a_ref.3), custom_call_target="tpu_custom_call" | custom-call | tf_op jit(solution)/shard_map/pallas_call | solution.py:158
  9.6 1.7 %collective-permute-done = f32[256,512]{1,0:T(8,128)S(1)} collective-permute-done((f32[256,512]{1,0:T(8,128)}, f32[256,512]{1,0:T(8,128)S(1)}, u32[]{:S(2)}, u32[]{:S(2)}) %collective-permute-start) | collective-permute-done | bytes 524320 | tf_op jit(solution)/shard_map/ppermute | solution.py:181
  11.3 1.1 %add.53 = f32[256,512]{1,0:T(8,128)S(1)} add(f32[256,512]{1,0:T(8,128)} %get-tuple-element.6, f32[256,512]{1,0:T(8,128)S(1)} %collective-permute-done) | non-fusion elementwise | flops 131072 | bytes 1572864 | tf_op jit(solution)/shard_map/add | solution.py:220
  12.5 2.9 %collective-permute-start.1 = (f32[64,512]{1,0:T(8,128)S(1)}, f32[64,512]{1,0:T(8,128)S(1)}, u32[]{:S(2)}, u32[]{:S(2)}) collective-permute-start(f32[64,512]{1,0:T(8,128)S(1)} %get-tuple-element.12), channel_id=1, source_target_pairs={{0,8},{8,0},{16,24},{24,16},{1,9},{9,1},{17,25},{25,17},{2,10},{10... | collective-permute-start | bytes 393224 | tf_op jit(solution)/shard_map/ppermute | solution.py:181
  15.4 1.5 %collective-permute-start.3 = (f32[64,512]{1,0:T(8,128)S(1)}, f32[64,512]{1,0:T(8,128)S(1)}, u32[]{:S(2)}, u32[]{:S(2)}) collective-permute-start(f32[64,512]{1,0:T(8,128)S(1)} %get-tuple-element.13), channel_id=1, source_target_pairs={{0,24},{8,16},{16,8},{24,0},{1,25},{9,17},{17,9},{25,1},{2,26},{10... | collective-permute-start | bytes 393224 | tf_op jit(solution)/shard_map/ppermute | solution.py:181
  16.9 2.6 %collective-permute-done.1 = f32[64,512]{1,0:T(8,128)S(1)} collective-permute-done((f32[64,512]{1,0:T(8,128)S(1)}, f32[64,512]{1,0:T(8,128)S(1)}, u32[]{:S(2)}, u32[]{:S(2)}) %collective-permute-start.1) | collective-permute-done | bytes 131104 | tf_op jit(solution)/shard_map/ppermute | solution.py:181
  19.5 3.8 %collective-permute-done.3 = f32[64,512]{1,0:T(8,128)S(1)} collective-permute-done((f32[64,512]{1,0:T(8,128)S(1)}, f32[64,512]{1,0:T(8,128)S(1)}, u32[]{:S(2)}, u32[]{:S(2)}) %collective-permute-start.3) | collective-permute-done | bytes 131104 | tf_op jit(solution)/shard_map/ppermute | solution.py:181
  23.3 1.4 %collective-permute-done.2 = f32[64,512]{1,0:T(8,128)S(1)} collective-permute-done((f32[64,512]{1,0:T(8,128)S(1)}, f32[64,512]{1,0:T(8,128)S(1)}, u32[]{:S(2)}, u32[]{:S(2)}) %collective-permute-start.2) | collective-permute-done | bytes 131104 | tf_op jit(solution)/shard_map/ppermute | solution.py:181
  24.7 1.6 %collective-permute-start.4 = (f32[16,512]{1,0:T(8,128)S(1)}, f32[16,512]{1,0:T(8,128)S(1)}, u32[]{:S(2)}, u32[]{:S(2)}) collective-permute-start(f32[16,512]{1,0:T(8,128)S(1)} %get-tuple-element.15), channel_id=1, source_target_pairs={{0,2},{1,3},{2,0},{3,1},{4,6},{5,7},{6,4},{7,5},{8,10},{9,11},{10,... | collective-permute-start | bytes 98312 | tf_op jit(solution)/shard_map/ppermute | solution.py:181
  26.4 2.5 %collective-permute-start.6 = (f32[16,512]{1,0:T(8,128)S(1)}, f32[16,512]{1,0:T(8,128)S(1)}, u32[]{:S(2)}, u32[]{:S(2)}) collective-permute-start(f32[16,512]{1,0:T(8,128)S(1)} %get-tuple-element.16), channel_id=1, source_target_pairs={{0,6},{1,7},{2,4},{3,5},{4,2},{5,3},{6,0},{7,1},{8,14},{9,15},{10,... | collective-permute-start | bytes 98312 | tf_op jit(solution)/shard_map/ppermute | solution.py:181
  29.0 3.1 %collective-permute-done.6 = f32[16,512]{1,0:T(8,128)S(1)} collective-permute-done((f32[16,512]{1,0:T(8,128)S(1)}, f32[16,512]{1,0:T(8,128)S(1)}, u32[]{:S(2)}, u32[]{:S(2)}) %collective-permute-start.6) | collective-permute-done | bytes 32800 | tf_op jit(solution)/shard_map/ppermute | solution.py:181
  32.1 1.9 %collective-permute-done.5 = f32[16,512]{1,0:T(8,128)S(1)} collective-permute-done((f32[16,512]{1,0:T(8,128)S(1)}, f32[16,512]{1,0:T(8,128)S(1)}, u32[]{:S(2)}, u32[]{:S(2)}) %collective-permute-start.5) | collective-permute-done | bytes 32800 | tf_op jit(solution)/shard_map/ppermute | solution.py:181
  34.5 1.4 %collective-permute-start.8 = (f32[16,512]{1,0:T(8,128)S(1)}, f32[16,512]{1,0:T(8,128)S(1)}, u32[]{:S(2)}, u32[]{:S(2)}) collective-permute-start(f32[16,512]{1,0:T(8,128)S(1)} %get-tuple-element.11), channel_id=1, source_target_pairs={{0,4},{1,5},{2,6},{3,7},{4,0},{5,1},{6,2},{7,3},{8,12},{9,13},{10,... | collective-permute-start | bytes 98312 | tf_op jit(solution)/shard_map/ppermute | solution.py:181
  35.9 2.6 %collective-permute-start.9 = (f32[16,512]{1,0:T(8,128)S(1)}, f32[16,512]{1,0:T(8,128)S(1)}, u32[]{:S(2)}, u32[]{:S(2)}) collective-permute-start(f32[16,512]{1,0:T(8,128)S(1)} %get-tuple-element.11), channel_id=1, source_target_pairs={{0,6},{1,7},{2,4},{3,5},{4,2},{5,3},{6,0},{7,1},{8,14},{9,15},{10,... | collective-permute-start | bytes 98312 | tf_op jit(solution)/shard_map/ppermute | solution.py:181
  38.5 0.8 collective-permute-done.8
  39.4 2.3 %collective-permute-done.9 = f32[16,512]{1,0:T(8,128)S(1)} collective-permute-done((f32[16,512]{1,0:T(8,128)S(1)}, f32[16,512]{1,0:T(8,128)S(1)}, u32[]{:S(2)}, u32[]{:S(2)}) %collective-permute-start.9) | collective-permute-done | bytes 32800 | tf_op jit(solution)/shard_map/ppermute | solution.py:181
  41.7 1.5 %collective-permute-start.10 = (f32[64,512]{1,0:T(8,128)S(1)}, f32[64,512]{1,0:T(8,128)S(1)}, u32[]{:S(2)}, u32[]{:S(2)}) collective-permute-start(f32[64,512]{1,0:T(8,128)S(1)} %constant_dynamic-update-slice_fusion.4), channel_id=1, source_target_pairs={{0,8},{8,0},{16,24},{24,16},{1,9},{9,1},{17,25},{25,17},{2,10},{10... | collective-permute-start | bytes 393224 | tf_op jit(solution)/shard_map/ppermute | solution.py:181
  43.6 1.5 %collective-permute-start.11 = (f32[64,512]{1,0:T(8,128)S(1)}, f32[64,512]{1,0:T(8,128)S(1)}, u32[]{:S(2)}, u32[]{:S(2)}) collective-permute-start(f32[64,512]{1,0:T(8,128)S(1)} %constant_dynamic-update-slice_fusion.4), channel_id=1, source_target_pairs={{0,16},{8,24},{16,0},{24,8},{1,17},{9,25},{17,1},{25,9},{2,18},{10... | collective-permute-start | bytes 393224 | tf_op jit(solution)/shard_map/ppermute | solution.py:181
  45.2 1.4 %collective-permute-done.10 = f32[64,512]{1,0:T(8,128)S(1)} collective-permute-done((f32[64,512]{1,0:T(8,128)S(1)}, f32[64,512]{1,0:T(8,128)S(1)}, u32[]{:S(2)}, u32[]{:S(2)}) %collective-permute-start.10) | collective-permute-done | bytes 131104 | tf_op jit(solution)/shard_map/ppermute | solution.py:181
  46.6 3.4 %collective-permute-done.11 = f32[64,512]{1,0:T(8,128)S(1)} collective-permute-done((f32[64,512]{1,0:T(8,128)S(1)}, f32[64,512]{1,0:T(8,128)S(1)}, u32[]{:S(2)}, u32[]{:S(2)}) %collective-permute-start.11) | collective-permute-done | bytes 131104 | tf_op jit(solution)/shard_map/ppermute | solution.py:181
  50.1 1.9 %collective-permute-done.13.got_ref = f32[256,512]{1,0:T(8,128)S(1)} collective-permute-done((f32[256,512]{1,0:T(8,128)S(1)}, f32[256,512]{1,0:T(8,128)S(1)}, u32[]{:S(2)}, u32[]{:S(2)}) %collective-permute-start.13) | collective-permute-done | bytes 524320 | tf_op jit(solution)/shard_map/ppermute | solution.py:181
  52.0 0.8 copy-done.1
  52.9 48.2 %shard_map.31 = (f32[512,512]{1,0:T(8,128)}, f32[512,512]{1,0:T(8,128)}) custom-call(s32[1]{0:T(128)} %bitcast.bit_ref, f32[256,512]{1,0:T(8,128)} %copy-done, f32[256,512]{1,0:T(8,128)} %copy-done.1), custom_call_target="tpu_custom_call" | custom-call | tf_op jit(solution)/shard_map/pallas_call | solution.py:80
  101.1 8.5 %shard_map.32 = f32[2048,512]{1,0:T(8,128)} custom-call(f32[2048,512]{1,0:T(8,128)} %a_ref.3, f32[512,512]{1,0:T(8,128)} %get-tuple-element.9.w_ref), custom_call_target="tpu_custom_call" | custom-call | tf_op jit(solution)/shard_map/pallas_call | solution.py:99
  (25 shorter events, 1.9 us)
Async XLA Ops:
  9.1 2.2 %collective-permute-start = (f32[256,512]{1,0:T(8,128)}, f32[256,512]{1,0:T(8,128)S(1)}, u32[]{:S(2)}, u32[]{:S(2)}) collective-permute-start(f32[256,512]{1,0:T(8,128)} %get-tuple-element.7), channel_id=1, source_target_pairs={{0,1},{1,0},{2,3},{3,2},{4,5},{5,4},{6,7},{7,6},{8,9},{9,8},{10,11... | collective-permute-start | bytes 1572872 | tf_op jit(solution)/shard_map/ppermute | solution.py:181
  12.5 7.0 %collective-permute-start.1 = (f32[64,512]{1,0:T(8,128)S(1)}, f32[64,512]{1,0:T(8,128)S(1)}, u32[]{:S(2)}, u32[]{:S(2)}) collective-permute-start(f32[64,512]{1,0:T(8,128)S(1)} %get-tuple-element.12), channel_id=1, source_target_pairs={{0,8},{8,0},{16,24},{24,16},{1,9},{9,1},{17,25},{25,17},{2,10},{10... | collective-permute-start | bytes 393224 | tf_op jit(solution)/shard_map/ppermute | solution.py:181
  15.4 7.9 %collective-permute-start.3 = (f32[64,512]{1,0:T(8,128)S(1)}, f32[64,512]{1,0:T(8,128)S(1)}, u32[]{:S(2)}, u32[]{:S(2)}) collective-permute-start(f32[64,512]{1,0:T(8,128)S(1)} %get-tuple-element.13), channel_id=1, source_target_pairs={{0,24},{8,16},{16,8},{24,0},{1,25},{9,17},{17,9},{25,1},{2,26},{10... | collective-permute-start | bytes 393224 | tf_op jit(solution)/shard_map/ppermute | solution.py:181
  16.9 7.8 %collective-permute-start.2 = (f32[64,512]{1,0:T(8,128)S(1)}, f32[64,512]{1,0:T(8,128)S(1)}, u32[]{:S(2)}, u32[]{:S(2)}) collective-permute-start(f32[64,512]{1,0:T(8,128)S(1)} %get-tuple-element.14), channel_id=1, source_target_pairs={{0,16},{8,24},{16,0},{24,8},{1,17},{9,25},{17,1},{25,9},{2,18},{10... | collective-permute-start | bytes 393224 | tf_op jit(solution)/shard_map/ppermute | solution.py:181
  24.7 4.2 %collective-permute-start.4 = (f32[16,512]{1,0:T(8,128)S(1)}, f32[16,512]{1,0:T(8,128)S(1)}, u32[]{:S(2)}, u32[]{:S(2)}) collective-permute-start(f32[16,512]{1,0:T(8,128)S(1)} %get-tuple-element.15), channel_id=1, source_target_pairs={{0,2},{1,3},{2,0},{3,1},{4,6},{5,7},{6,4},{7,5},{8,10},{9,11},{10,... | collective-permute-start | bytes 98312 | tf_op jit(solution)/shard_map/ppermute | solution.py:181
  26.4 5.7 %collective-permute-start.6 = (f32[16,512]{1,0:T(8,128)S(1)}, f32[16,512]{1,0:T(8,128)S(1)}, u32[]{:S(2)}, u32[]{:S(2)}) collective-permute-start(f32[16,512]{1,0:T(8,128)S(1)} %get-tuple-element.16), channel_id=1, source_target_pairs={{0,6},{1,7},{2,4},{3,5},{4,2},{5,3},{6,0},{7,1},{8,14},{9,15},{10,... | collective-permute-start | bytes 98312 | tf_op jit(solution)/shard_map/ppermute | solution.py:181
  28.9 5.2 %collective-permute-start.5 = (f32[16,512]{1,0:T(8,128)S(1)}, f32[16,512]{1,0:T(8,128)S(1)}, u32[]{:S(2)}, u32[]{:S(2)}) collective-permute-start(f32[16,512]{1,0:T(8,128)S(1)} %get-tuple-element.17), channel_id=1, source_target_pairs={{0,4},{1,5},{2,6},{3,7},{4,0},{5,1},{6,2},{7,3},{8,12},{9,13},{10,... | collective-permute-start | bytes 98312 | tf_op jit(solution)/shard_map/ppermute | solution.py:181
  34.1 4.5 %collective-permute-start.7 = (f32[16,512]{1,0:T(8,128)S(1)}, f32[16,512]{1,0:T(8,128)S(1)}, u32[]{:S(2)}, u32[]{:S(2)}) collective-permute-start(f32[16,512]{1,0:T(8,128)S(1)} %get-tuple-element.11), channel_id=1, source_target_pairs={{0,2},{1,3},{2,0},{3,1},{4,6},{5,7},{6,4},{7,5},{8,10},{9,11},{10,... | collective-permute-start | bytes 98312 | tf_op jit(solution)/shard_map/ppermute | solution.py:181
  34.5 4.8 %collective-permute-start.8 = (f32[16,512]{1,0:T(8,128)S(1)}, f32[16,512]{1,0:T(8,128)S(1)}, u32[]{:S(2)}, u32[]{:S(2)}) collective-permute-start(f32[16,512]{1,0:T(8,128)S(1)} %get-tuple-element.11), channel_id=1, source_target_pairs={{0,4},{1,5},{2,6},{3,7},{4,0},{5,1},{6,2},{7,3},{8,12},{9,13},{10,... | collective-permute-start | bytes 98312 | tf_op jit(solution)/shard_map/ppermute | solution.py:181
  35.9 5.7 %collective-permute-start.9 = (f32[16,512]{1,0:T(8,128)S(1)}, f32[16,512]{1,0:T(8,128)S(1)}, u32[]{:S(2)}, u32[]{:S(2)}) collective-permute-start(f32[16,512]{1,0:T(8,128)S(1)} %get-tuple-element.11), channel_id=1, source_target_pairs={{0,6},{1,7},{2,4},{3,5},{4,2},{5,3},{6,0},{7,1},{8,14},{9,15},{10,... | collective-permute-start | bytes 98312 | tf_op jit(solution)/shard_map/ppermute | solution.py:181
  41.7 5.0 %collective-permute-start.10 = (f32[64,512]{1,0:T(8,128)S(1)}, f32[64,512]{1,0:T(8,128)S(1)}, u32[]{:S(2)}, u32[]{:S(2)}) collective-permute-start(f32[64,512]{1,0:T(8,128)S(1)} %constant_dynamic-update-slice_fusion.4), channel_id=1, source_target_pairs={{0,8},{8,0},{16,24},{24,16},{1,9},{9,1},{17,25},{25,17},{2,10},{10... | collective-permute-start | bytes 393224 | tf_op jit(solution)/shard_map/ppermute | solution.py:181
  43.1 6.9 %collective-permute-start.12 = (f32[64,512]{1,0:T(8,128)S(1)}, f32[64,512]{1,0:T(8,128)S(1)}, u32[]{:S(2)}, u32[]{:S(2)}) collective-permute-start(f32[64,512]{1,0:T(8,128)S(1)} %constant_dynamic-update-slice_fusion.4), channel_id=1, source_target_pairs={{0,24},{8,16},{16,8},{24,0},{1,25},{9,17},{17,9},{25,1},{2,26},{10... | collective-permute-start | bytes 393224 | tf_op jit(solution)/shard_map/ppermute | solution.py:181
  43.6 6.4 %collective-permute-start.11 = (f32[64,512]{1,0:T(8,128)S(1)}, f32[64,512]{1,0:T(8,128)S(1)}, u32[]{:S(2)}, u32[]{:S(2)}) collective-permute-start(f32[64,512]{1,0:T(8,128)S(1)} %constant_dynamic-update-slice_fusion.4), channel_id=1, source_target_pairs={{0,16},{8,24},{16,0},{24,8},{1,17},{9,25},{17,1},{25,9},{2,18},{10... | collective-permute-start | bytes 393224 | tf_op jit(solution)/shard_map/ppermute | solution.py:181
  50.0 2.0 %copy-start = (f32[256,512]{1,0:T(8,128)}, f32[256,512]{1,0:T(8,128)S(1)}, u32[]{:S(2)}) copy-start(f32[256,512]{1,0:T(8,128)S(1)} %constant_dynamic-update-slice_fusion.mine_ref) | copy-start | bytes 1572868
  50.1 2.0 %collective-permute-start.13 = (f32[256,512]{1,0:T(8,128)S(1)}, f32[256,512]{1,0:T(8,128)S(1)}, u32[]{:S(2)}, u32[]{:S(2)}) collective-permute-start(f32[256,512]{1,0:T(8,128)S(1)} %constant_dynamic-update-slice_fusion.mine_ref), channel_id=1, source_target_pairs={{0,1},{1,0},{2,3},{3,2},{4,5},{5,4},{6,7},{7,6},{8,9},{9,8},{10,11... | collective-permute-start | bytes 1572872 | tf_op jit(solution)/shard_map/ppermute | solution.py:181
  52.0 0.8 copy-start.1

commit v9 on v8

--- a/solution.py
+++ b/solution.py
@@ -10,6 +10,30 @@
 
 BLOCK = 128
 SLAB = 8
+
+
+STACK = 5 * BLOCK
+
+
+def lower_stacks(acc_ref):
+    b = BLOCK
+    first = jnp.concatenate([acc_ref[:, 0:b], acc_ref[b:2 * b, b:2 * b]], axis=0)
+    second = jnp.concatenate(
+        [acc_ref[2 * b:4 * b, b:2 * b], acc_ref[2 * b:4 * b, 2 * b:3 * b], acc_ref[3 * b:4 * b, 3 * b:4 * b]], axis=0
+    )
+    return first, second
+
+
+def fill_gram(work_ref, first_ref, second_ref):
+    b = BLOCK
+    work_ref[:, 0:b] = first_ref[0:4 * b, :]
+    work_ref[b:2 * b, b:2 * b] = first_ref[4 * b:5 * b, :]
+    work_ref[2 * b:4 * b, b:2 * b] = second_ref[0:2 * b, :]
+    work_ref[2 * b:4 * b, 2 * b:3 * b] = second_ref[2 * b:4 * b, :]
+    work_ref[3 * b:4 * b, 3 * b:4 * b] = second_ref[4 * b:5 * b, :]
+    for i in range(4):
+        for j in range(i + 1, 4):
+            work_ref[i * b:(i + 1) * b, j * b:(j + 1) * b] = work_ref[j * b:(j + 1) * b, i * b:(i + 1) * b].T
 
 
 def hdot(left, right):
@@ -39,17 +63,14 @@
 
 def chol_kernel(bit_ref, mine_ref, got_ref, u_ref, uinv_ref, work_ref, aug_ref, inv_ref):
     n = u_ref.shape[0]
-    half = n // 2
 
     @pl.when(bit_ref[0] == 0)
     def _():
-        work_ref[0:half, :] = mine_ref[...]
-        work_ref[half:n, :] = got_ref[...]
+        fill_gram(work_ref, mine_ref, got_ref)
 
     @pl.when(bit_ref[0] != 0)
     def _():
-        work_ref[0:half, :] = got_ref[...]
-        work_ref[half:n, :] = mine_ref[...]
+        fill_gram(work_ref, got_ref, mine_ref)
 
     aug_ref[...] = jnp.zeros_like(aug_ref)
     blocks = n // BLOCK
@@ -75,7 +96,7 @@
 
 
 def cholesky_and_inverse(bit, mine, got):
-    n = mine.shape[1]
+    n = 4 * BLOCK
     spec = pl.BlockSpec(memory_space=pltpu.VMEM)
     return pl.pallas_call(
         chol_kernel,
@@ -136,25 +157,25 @@
 
     @pl.when(step == pl.num_programs(0) - 1)
     def _():
-        acc_ref[0:half, half:] = acc_ref[half:, 0:half].T
-        top = acc_ref[0:half, :] / row_count
-        bottom = acc_ref[half:, :] / row_count
+        first, second = lower_stacks(acc_ref)
+        first = first / row_count
+        second = second / row_count
 
         @pl.when(bit_ref[0] == 0)
         def _():
-            keep_ref[...] = top
-            send_ref[...] = bottom
+            keep_ref[...] = first
+            send_ref[...] = second
 
         @pl.when(bit_ref[0] != 0)
         def _():
-            keep_ref[...] = bottom
-            send_ref[...] = top
+            keep_ref[...] = second
+            send_ref[...] = first
 
 
 def gram_halves(matrix, row_count, bit):
     rows, width = matrix.shape
     tile = min(rows, 512)
-    half = jax.ShapeDtypeStruct((width // 2, width), jnp.float32)
+    half = jax.ShapeDtypeStruct((STACK, BLOCK), jnp.float32)
     return pl.pallas_call(
         functools.partial(gram_kernel, row_count),
         out_shape=(half, half),
@@ -164,8 +185,8 @@
             pl.BlockSpec((tile, width), lambda i: (i, 0)),
         ],
         out_specs=(
-            pl.BlockSpec((width // 2, width), lambda i: (0, 0)),
-            pl.BlockSpec((width // 2, width), lambda i: (0, 0)),
+            pl.BlockSpec((STACK, BLOCK), lambda i: (0, 0)),
+            pl.BlockSpec((STACK, BLOCK), lambda i: (0, 0)),
         ),
         scratch_shapes=[pltpu.VMEM((width, width), jnp.float32)],
     )(bit, matrix)

time: 110 us -> 105 us (0.955)
  waiting for transfers between devices: 24.3 us -> 20 us
    ppermute x14, waiting for transfers between devices: 24.3 us -> 20 us  [partner_xor(): return lax.ppermute(value, axis, pairs)]
  transfers between devices with their start and end apart: 14 -> 14, of which waited for: 11 -> 10; matrix products, arithmetic and copies ran while one was open for 0% -> 0% of each run, Pallas kernels for 0% -> 0%
where the time goes in v9:
time: 105 us
  Pallas kernels  64.9 us (62%)
  waiting for transfers between devices  20 us (19%)
  starting transfers between devices  17.2 us (16%)
    pallas_call x1, Pallas kernels, cholesky_and_inverse(): pl.pallas_call(chol_kernel, out_shape=(jax.ShapeDtypeStruct((n, n), jnp.f...  48.2 us
    ppermute x14, waiting for transfers between devices, partner_xor(): return lax.ppermute(value, axis, pairs)  20 us
    ppermute x14, starting transfers between devices, partner_xor(): return lax.ppermute(value, axis, pairs)  17.2 us
    pallas_call x1, Pallas kernels, rows_times(): pl.pallas_call(rows_kernel, out_shape=jax.ShapeDtypeStruct((rows, weights...  8.46 us
    pallas_call x1, Pallas kernels, gram_halves(): pl.pallas_call(functools.partial(gram_kernel, row_count), out_shape=(half...  8.23 us
  transfers between devices with their start and end apart: 14, of which 10 were waited for; matrix products, arithmetic and copies ran while one was open for 0% of the time, Pallas kernels for 0%

profile of v9, /device:TPU:0, one launch (start us, length us, event | category | flops | bytes accessed | tf_op | source)
XLA Modules:
  0.0 104.7 jit_solution(16935277175347979845)
XLA Ops:
  0.6 8.2 %shard_map.30 = (f32[640,128]{1,0:T(8,128)}, f32[640,128]{1,0:T(8,128)}) custom-call(s32[1]{0:T(128)} %bitcast.bit_ref, f32[2048,512]{1,0:T(8,128)} %a_ref.3), custom_call_target="tpu_custom_call" | custom-call | tf_op jit(solution)/shard_map/pallas_call | solution.py:179
  9.3 1.5 %collective-permute-done = f32[640,128]{1,0:T(8,128)S(1)} collective-permute-done((f32[640,128]{1,0:T(8,128)}, f32[640,128]{1,0:T(8,128)S(1)}, u32[]{:S(2)}, u32[]{:S(2)}) %collective-permute-start) | collective-permute-done | bytes 327712 | tf_op jit(solution)/shard_map/ppermute | solution.py:202
  10.8 1.0 add.53
  11.8 2.9 %collective-permute-start.1 = (f32[160,128]{1,0:T(8,128)S(1)}, f32[160,128]{1,0:T(8,128)S(1)}, u32[]{:S(2)}, u32[]{:S(2)}) collective-permute-start(f32[160,128]{1,0:T(8,128)S(1)} %get-tuple-element.12), channel_id=1, source_target_pairs={{0,8},{8,0},{16,24},{24,16},{1,9},{9,1},{17,25},{25,17},{2,10},{10... | collective-permute-start | bytes 245768 | tf_op jit(solution)/shard_map/ppermute | solution.py:202
  14.8 1.5 %collective-permute-start.3 = (f32[160,128]{1,0:T(8,128)S(1)}, f32[160,128]{1,0:T(8,128)S(1)}, u32[]{:S(2)}, u32[]{:S(2)}) collective-permute-start(f32[160,128]{1,0:T(8,128)S(1)} %get-tuple-element.13), channel_id=1, source_target_pairs={{0,24},{8,16},{16,8},{24,0},{1,25},{9,17},{17,9},{25,1},{2,26},{10... | collective-permute-start | bytes 245768 | tf_op jit(solution)/shard_map/ppermute | solution.py:202
  16.3 1.2 %collective-permute-done.1 = f32[160,128]{1,0:T(8,128)S(1)} collective-permute-done((f32[160,128]{1,0:T(8,128)S(1)}, f32[160,128]{1,0:T(8,128)S(1)}, u32[]{:S(2)}, u32[]{:S(2)}) %collective-permute-start.1) | collective-permute-done | bytes 81952 | tf_op jit(solution)/shard_map/ppermute | solution.py:202
  17.5 3.1 %collective-permute-done.3 = f32[160,128]{1,0:T(8,128)S(1)} collective-permute-done((f32[160,128]{1,0:T(8,128)S(1)}, f32[160,128]{1,0:T(8,128)S(1)}, u32[]{:S(2)}, u32[]{:S(2)}) %collective-permute-start.3) | collective-permute-done | bytes 81952 | tf_op jit(solution)/shard_map/ppermute | solution.py:202
  20.6 1.2 %collective-permute-done.2 = f32[160,128]{1,0:T(8,128)S(1)} collective-permute-done((f32[160,128]{1,0:T(8,128)S(1)}, f32[160,128]{1,0:T(8,128)S(1)}, u32[]{:S(2)}, u32[]{:S(2)}) %collective-permute-start.2) | collective-permute-done | bytes 81952 | tf_op jit(solution)/shard_map/ppermute | solution.py:202
  21.8 1.6 %collective-permute-start.4 = (f32[40,128]{1,0:T(8,128)S(1)}, f32[40,128]{1,0:T(8,128)S(1)}, u32[]{:S(2)}, u32[]{:S(2)}) collective-permute-start(f32[40,128]{1,0:T(8,128)S(1)} %get-tuple-element.15), channel_id=1, source_target_pairs={{0,2},{1,3},{2,0},{3,1},{4,6},{5,7},{6,4},{7,5},{8,10},{9,11},{10,... | collective-permute-start | bytes 61448 | tf_op jit(solution)/shard_map/ppermute | solution.py:202
  23.5 2.5 %collective-permute-start.6 = (f32[40,128]{1,0:T(8,128)S(1)}, f32[40,128]{1,0:T(8,128)S(1)}, u32[]{:S(2)}, u32[]{:S(2)}) collective-permute-start(f32[40,128]{1,0:T(8,128)S(1)} %get-tuple-element.16), channel_id=1, source_target_pairs={{0,6},{1,7},{2,4},{3,5},{4,2},{5,3},{6,0},{7,1},{8,14},{9,15},{10,... | collective-permute-start | bytes 61448 | tf_op jit(solution)/shard_map/ppermute | solution.py:202
  26.1 3.0 %collective-permute-done.6 = f32[40,128]{1,0:T(8,128)S(1)} collective-permute-done((f32[40,128]{1,0:T(8,128)S(1)}, f32[40,128]{1,0:T(8,128)S(1)}, u32[]{:S(2)}, u32[]{:S(2)}) %collective-permute-start.6) | collective-permute-done | bytes 20512 | tf_op jit(solution)/shard_map/ppermute | solution.py:202
  29.0 1.8 %collective-permute-done.5 = f32[40,128]{1,0:T(8,128)S(1)} collective-permute-done((f32[40,128]{1,0:T(8,128)S(1)}, f32[40,128]{1,0:T(8,128)S(1)}, u32[]{:S(2)}, u32[]{:S(2)}) %collective-permute-start.5) | collective-permute-done | bytes 20512 | tf_op jit(solution)/shard_map/ppermute | solution.py:202
  31.5 1.1 %collective-permute-start.8 = (f32[40,128]{1,0:T(8,128)S(1)}, f32[40,128]{1,0:T(8,128)S(1)}, u32[]{:S(2)}, u32[]{:S(2)}) collective-permute-start(f32[40,128]{1,0:T(8,128)S(1)} %get-tuple-element.11), channel_id=1, source_target_pairs={{0,4},{1,5},{2,6},{3,7},{4,0},{5,1},{6,2},{7,3},{8,12},{9,13},{10,... | collective-permute-start | bytes 61448 | tf_op jit(solution)/shard_map/ppermute | solution.py:202
  32.6 2.7 %collective-permute-start.9 = (f32[40,128]{1,0:T(8,128)S(1)}, f32[40,128]{1,0:T(8,128)S(1)}, u32[]{:S(2)}, u32[]{:S(2)}) collective-permute-start(f32[40,128]{1,0:T(8,128)S(1)} %get-tuple-element.11), channel_id=1, source_target_pairs={{0,6},{1,7},{2,4},{3,5},{4,2},{5,3},{6,0},{7,1},{8,14},{9,15},{10,... | collective-permute-start | bytes 61448 | tf_op jit(solution)/shard_map/ppermute | solution.py:202
  35.3 0.8 collective-permute-done.8
  36.2 2.0 %collective-permute-done.9 = f32[40,128]{1,0:T(8,128)S(1)} collective-permute-done((f32[40,128]{1,0:T(8,128)S(1)}, f32[40,128]{1,0:T(8,128)S(1)}, u32[]{:S(2)}, u32[]{:S(2)}) %collective-permute-start.9) | collective-permute-done | bytes 20512 | tf_op jit(solution)/shard_map/ppermute | solution.py:202
  38.2 1.5 %collective-permute-start.12 = (f32[160,128]{1,0:T(8,128)S(1)}, f32[160,128]{1,0:T(8,128)S(1)}, u32[]{:S(2)}, u32[]{:S(2)}) collective-permute-start(f32[160,128]{1,0:T(8,128)S(1)} %constant_dynamic-update-slice_fusion.4), channel_id=1, source_target_pairs={{0,24},{8,16},{16,8},{24,0},{1,25},{9,17},{17,9},{25,1},{2,26},{10... | collective-permute-start | bytes 245768 | tf_op jit(solution)/shard_map/ppermute | solution.py:202
  39.7 1.4 %collective-permute-start.11 = (f32[160,128]{1,0:T(8,128)S(1)}, f32[160,128]{1,0:T(8,128)S(1)}, u32[]{:S(2)}, u32[]{:S(2)}) collective-permute-start(f32[160,128]{1,0:T(8,128)S(1)} %constant_dynamic-update-slice_fusion.4), channel_id=1, source_target_pairs={{0,16},{8,24},{16,0},{24,8},{1,17},{9,25},{17,1},{25,9},{2,18},{10... | collective-permute-start | bytes 245768 | tf_op jit(solution)/shard_map/ppermute | solution.py:202
  41.1 0.6 collective-permute-start.10
  41.7 3.8 %collective-permute-done.10 = f32[160,128]{1,0:T(8,128)S(1)} collective-permute-done((f32[160,128]{1,0:T(8,128)S(1)}, f32[160,128]{1,0:T(8,128)S(1)}, u32[]{:S(2)}, u32[]{:S(2)}) %collective-permute-start.10) | collective-permute-done | bytes 81952 | tf_op jit(solution)/shard_map/ppermute | solution.py:202
  45.7 1.6 %collective-permute-done.13.got_ref = f32[640,128]{1,0:T(8,128)S(1)} collective-permute-done((f32[640,128]{1,0:T(8,128)S(1)}, f32[640,128]{1,0:T(8,128)S(1)}, u32[]{:S(2)}, u32[]{:S(2)}) %collective-permute-start.13) | collective-permute-done | bytes 327712 | tf_op jit(solution)/shard_map/ppermute | solution.py:202
  47.3 0.7 copy-done.1
  48.0 48.2 %shard_map.31 = (f32[512,512]{1,0:T(8,128)}, f32[512,512]{1,0:T(8,128)}) custom-call(s32[1]{0:T(128)} %bitcast.bit_ref, f32[640,128]{1,0:T(8,128)} %copy-done, f32[640,128]{1,0:T(8,128)} %copy-done.1), custom_call_target="tpu_custom_call" | custom-call | tf_op jit(solution)/shard_map/pallas_call | solution.py:101
  96.2 8.5 %shard_map.32 = f32[2048,512]{1,0:T(8,128)} custom-call(f32[2048,512]{1,0:T(8,128)} %a_ref.3, f32[512,512]{1,0:T(8,128)} %get-tuple-element.9.w_ref), custom_call_target="tpu_custom_call" | custom-call | tf_op jit(solution)/shard_map/pallas_call | solution.py:120
  (25 shorter events, 1.5 us)
Async XLA Ops:
  8.9 1.9 %collective-permute-start = (f32[640,128]{1,0:T(8,128)}, f32[640,128]{1,0:T(8,128)S(1)}, u32[]{:S(2)}, u32[]{:S(2)}) collective-permute-start(f32[640,128]{1,0:T(8,128)} %get-tuple-element.7), channel_id=1, source_target_pairs={{0,1},{1,0},{2,3},{3,2},{4,5},{5,4},{6,7},{7,6},{8,9},{9,8},{10,11... | collective-permute-start | bytes 983048 | tf_op jit(solution)/shard_map/ppermute | solution.py:202
  11.8 5.7 %collective-permute-start.1 = (f32[160,128]{1,0:T(8,128)S(1)}, f32[160,128]{1,0:T(8,128)S(1)}, u32[]{:S(2)}, u32[]{:S(2)}) collective-permute-start(f32[160,128]{1,0:T(8,128)S(1)} %get-tuple-element.12), channel_id=1, source_target_pairs={{0,8},{8,0},{16,24},{24,16},{1,9},{9,1},{17,25},{25,17},{2,10},{10... | collective-permute-start | bytes 245768 | tf_op jit(solution)/shard_map/ppermute | solution.py:202
  14.8 5.8 %collective-permute-start.3 = (f32[160,128]{1,0:T(8,128)S(1)}, f32[160,128]{1,0:T(8,128)S(1)}, u32[]{:S(2)}, u32[]{:S(2)}) collective-permute-start(f32[160,128]{1,0:T(8,128)S(1)} %get-tuple-element.13), channel_id=1, source_target_pairs={{0,24},{8,16},{16,8},{24,0},{1,25},{9,17},{17,9},{25,1},{2,26},{10... | collective-permute-start | bytes 245768 | tf_op jit(solution)/shard_map/ppermute | solution.py:202
  16.2 5.5 %collective-permute-start.2 = (f32[160,128]{1,0:T(8,128)S(1)}, f32[160,128]{1,0:T(8,128)S(1)}, u32[]{:S(2)}, u32[]{:S(2)}) collective-permute-start(f32[160,128]{1,0:T(8,128)S(1)} %get-tuple-element.14), channel_id=1, source_target_pairs={{0,16},{8,24},{16,0},{24,8},{1,17},{9,25},{17,1},{25,9},{2,18},{10... | collective-permute-start | bytes 245768 | tf_op jit(solution)/shard_map/ppermute | solution.py:202
  21.8 4.2 %collective-permute-start.4 = (f32[40,128]{1,0:T(8,128)S(1)}, f32[40,128]{1,0:T(8,128)S(1)}, u32[]{:S(2)}, u32[]{:S(2)}) collective-permute-start(f32[40,128]{1,0:T(8,128)S(1)} %get-tuple-element.15), channel_id=1, source_target_pairs={{0,2},{1,3},{2,0},{3,1},{4,6},{5,7},{6,4},{7,5},{8,10},{9,11},{10,... | collective-permute-start | bytes 61448 | tf_op jit(solution)/shard_map/ppermute | solution.py:202
  23.5 5.6 %collective-permute-start.6 = (f32[40,128]{1,0:T(8,128)S(1)}, f32[40,128]{1,0:T(8,128)S(1)}, u32[]{:S(2)}, u32[]{:S(2)}) collective-permute-start(f32[40,128]{1,0:T(8,128)S(1)} %get-tuple-element.16), channel_id=1, source_target_pairs={{0,6},{1,7},{2,4},{3,5},{4,2},{5,3},{6,0},{7,1},{8,14},{9,15},{10,... | collective-permute-start | bytes 61448 | tf_op jit(solution)/shard_map/ppermute | solution.py:202
  25.9 4.9 %collective-permute-start.5 = (f32[40,128]{1,0:T(8,128)S(1)}, f32[40,128]{1,0:T(8,128)S(1)}, u32[]{:S(2)}, u32[]{:S(2)}) collective-permute-start(f32[40,128]{1,0:T(8,128)S(1)} %get-tuple-element.17), channel_id=1, source_target_pairs={{0,4},{1,5},{2,6},{3,7},{4,0},{5,1},{6,2},{7,3},{8,12},{9,13},{10,... | collective-permute-start | bytes 61448 | tf_op jit(solution)/shard_map/ppermute | solution.py:202
  30.9 4.5 %collective-permute-start.7 = (f32[40,128]{1,0:T(8,128)S(1)}, f32[40,128]{1,0:T(8,128)S(1)}, u32[]{:S(2)}, u32[]{:S(2)}) collective-permute-start(f32[40,128]{1,0:T(8,128)S(1)} %get-tuple-element.11), channel_id=1, source_target_pairs={{0,2},{1,3},{2,0},{3,1},{4,6},{5,7},{6,4},{7,5},{8,10},{9,11},{10,... | collective-permute-start | bytes 61448 | tf_op jit(solution)/shard_map/ppermute | solution.py:202
  31.5 4.7 %collective-permute-start.8 = (f32[40,128]{1,0:T(8,128)S(1)}, f32[40,128]{1,0:T(8,128)S(1)}, u32[]{:S(2)}, u32[]{:S(2)}) collective-permute-start(f32[40,128]{1,0:T(8,128)S(1)} %get-tuple-element.11), channel_id=1, source_target_pairs={{0,4},{1,5},{2,6},{3,7},{4,0},{5,1},{6,2},{7,3},{8,12},{9,13},{10,... | collective-permute-start | bytes 61448 | tf_op jit(solution)/shard_map/ppermute | solution.py:202
  32.6 5.6 %collective-permute-start.9 = (f32[40,128]{1,0:T(8,128)S(1)}, f32[40,128]{1,0:T(8,128)S(1)}, u32[]{:S(2)}, u32[]{:S(2)}) collective-permute-start(f32[40,128]{1,0:T(8,128)S(1)} %get-tuple-element.11), channel_id=1, source_target_pairs={{0,6},{1,7},{2,4},{3,5},{4,2},{5,3},{6,0},{7,1},{8,14},{9,15},{10,... | collective-permute-start | bytes 61448 | tf_op jit(solution)/shard_map/ppermute | solution.py:202
  38.2 7.3 %collective-permute-start.12 = (f32[160,128]{1,0:T(8,128)S(1)}, f32[160,128]{1,0:T(8,128)S(1)}, u32[]{:S(2)}, u32[]{:S(2)}) collective-permute-start(f32[160,128]{1,0:T(8,128)S(1)} %constant_dynamic-update-slice_fusion.4), channel_id=1, source_target_pairs={{0,24},{8,16},{16,8},{24,0},{1,25},{9,17},{17,9},{25,1},{2,26},{10... | collective-permute-start | bytes 245768 | tf_op jit(solution)/shard_map/ppermute | solution.py:202
  39.7 5.8 %collective-permute-start.11 = (f32[160,128]{1,0:T(8,128)S(1)}, f32[160,128]{1,0:T(8,128)S(1)}, u32[]{:S(2)}, u32[]{:S(2)}) collective-permute-start(f32[160,128]{1,0:T(8,128)S(1)} %constant_dynamic-update-slice_fusion.4), channel_id=1, source_target_pairs={{0,16},{8,24},{16,0},{24,8},{1,17},{9,25},{17,1},{25,9},{2,18},{10... | collective-permute-start | bytes 245768 | tf_op jit(solution)/shard_map/ppermute | solution.py:202
  41.1 4.4 %collective-permute-start.10 = (f32[160,128]{1,0:T(8,128)S(1)}, f32[160,128]{1,0:T(8,128)S(1)}, u32[]{:S(2)}, u32[]{:S(2)}) collective-permute-start(f32[160,128]{1,0:T(8,128)S(1)} %constant_dynamic-update-slice_fusion.4), channel_id=1, source_target_pairs={{0,8},{8,0},{16,24},{24,16},{1,9},{9,1},{17,25},{25,17},{2,10},{10... | collective-permute-start | bytes 245768 | tf_op jit(solution)/shard_map/ppermute | solution.py:202
  45.6 1.7 %copy-start = (f32[640,128]{1,0:T(8,128)}, f32[640,128]{1,0:T(8,128)S(1)}, u32[]{:S(2)}) copy-start(f32[640,128]{1,0:T(8,128)S(1)} %constant_dynamic-update-slice_fusion.mine_ref) | copy-start | bytes 983044
  45.6 1.7 %collective-permute-start.13 = (f32[640,128]{1,0:T(8,128)S(1)}, f32[640,128]{1,0:T(8,128)S(1)}, u32[]{:S(2)}, u32[]{:S(2)}) collective-permute-start(f32[640,128]{1,0:T(8,128)S(1)} %constant_dynamic-update-slice_fusion.mine_ref), channel_id=1, source_target_pairs={{0,1},{1,0},{2,3},{3,2},{4,5},{5,4},{6,7},{7,6},{8,9},{9,8},{10,11... | collective-permute-start | bytes 983048 | tf_op jit(solution)/shard_map/ppermute | solution.py:202
  47.3 0.7 copy-start.1

commit v10 on v9

--- a/solution.py
+++ b/solution.py
@@ -234,15 +234,28 @@
     return groups
 
 
+def group_total(value, axis, shift, size):
+    index = group_index(axis, shift, size)
+    received = [value] + [partner_xor(value, axis, shift, offset) for offset in range(1, size)]
+    ordered = []
+    for slot in range(size):
+        pick = received[0]
+        for offset in range(1, size):
+            pick = jnp.where((index ^ offset) == slot, received[offset], pick)
+        ordered.append(pick)
+    return functools.reduce(jnp.add, ordered)
+
+
 def on_device(response):
     row_count = response.shape[0] * lax.axis_size("inner") * lax.axis_size("wide")
     bit = jnp.reshape(lax.axis_index("wide") & 1, (1,)).astype(jnp.int32)
     keep, send = gram_halves(response, row_count, bit)
     partial_sum = keep + partner_xor(send, "wide", 0, 1)
     groups = axis_groups("inner", 0) + axis_groups("wide", 1)
-    for group in groups:
+    for group in groups[:-1]:
         partial_sum = scatter_sum(partial_sum, *group)
-    for group in reversed(groups):
+    partial_sum = group_total(partial_sum, *groups[-1])
+    for group in reversed(groups[:-1]):
         partial_sum = gather_all(partial_sum, *group)
     got = partner_xor(partial_sum, "wide", 0, 1)
     upper_factor, inverse_upper = cholesky_and_inverse(bit, partial_sum, got)

time: 105 us -> 99.3 us (0.946)
  starting transfers between devices: 17.2 us -> 13 us
  waiting for transfers between devices: 20 us -> 18.5 us
    ppermute x14 -> x11, starting transfers between devices: 17.2 us -> 13 us  [partner_xor(): return lax.ppermute(value, axis, pairs)]
    ppermute x14 -> x11, waiting for transfers between devices: 20 us -> 18.5 us  [partner_xor(): return lax.ppermute(value, axis, pairs)]
  transfers between devices with their start and end apart: 14 -> 11, of which waited for: 10 -> 11; matrix products, arithmetic and copies ran while one was open for 0% -> 0% of each run, Pallas kernels for 0% -> 0%
where the time goes in v10:
time: 99.3 us; the launch traced here: 99 us
  Pallas kernels  64.9 us (65%)
  waiting for transfers between devices  18.5 us (19%)
  starting transfers between devices  13 us (13%)
  other arithmetic  1.08 us (1%)
    pallas_call x1, Pallas kernels, cholesky_and_inverse(): pl.pallas_call(chol_kernel, out_shape=(jax.ShapeDtypeStruct((n, n), jnp.f...  48.2 us
    ppermute x11, waiting for transfers between devices, partner_xor(): return lax.ppermute(value, axis, pairs)  18.5 us
    ppermute x11, starting transfers between devices, partner_xor(): return lax.ppermute(value, axis, pairs)  13 us
    pallas_call x1, Pallas kernels, rows_times(): pl.pallas_call(rows_kernel, out_shape=jax.ShapeDtypeStruct((rows, weights...  8.46 us
    pallas_call x1, Pallas kernels, gram_halves(): pl.pallas_call(functools.partial(gram_kernel, row_count), out_shape=(half...  8.23 us
  transfers between devices with their start and end apart: 11, of which 11 were waited for; matrix products, arithmetic and copies ran while one was open for 0% of the time, Pallas kernels for 0%

profile of v10, /device:TPU:0, one launch (start us, length us, event | category | flops | bytes accessed | tf_op | source)
XLA Modules:
  0.0 99.0 jit_solution(13445589092152155423)
XLA Ops:
  0.6 8.2 %shard_map.30 = (f32[640,128]{1,0:T(8,128)}, f32[640,128]{1,0:T(8,128)}) custom-call(s32[1]{0:T(128)} %bitcast.bit_ref, f32[2048,512]{1,0:T(8,128)} %a_ref.3), custom_call_target="tpu_custom_call" | custom-call | tf_op jit(solution)/shard_map/pallas_call | solution.py:179
  8.9 0.5 collective-permute-start
  9.3 1.5 %collective-permute-done = f32[640,128]{1,0:T(8,128)S(1)} collective-permute-done((f32[640,128]{1,0:T(8,128)}, f32[640,128]{1,0:T(8,128)S(1)}, u32[]{:S(2)}, u32[]{:S(2)}) %collective-permute-start) | collective-permute-done | bytes 327712 | tf_op jit(solution)/shard_map/ppermute | solution.py:202
  10.8 1.0 %add.37 = f32[640,128]{1,0:T(8,128)S(1)} add(f32[640,128]{1,0:T(8,128)} %get-tuple-element.6, f32[640,128]{1,0:T(8,128)S(1)} %collective-permute-done) | non-fusion elementwise | flops 81920 | bytes 983040 | tf_op jit(solution)/shard_map/add | solution.py:253
  11.8 2.9 %collective-permute-start.1 = (f32[160,128]{1,0:T(8,128)S(1)}, f32[160,128]{1,0:T(8,128)S(1)}, u32[]{:S(2)}, u32[]{:S(2)}) collective-permute-start(f32[160,128]{1,0:T(8,128)S(1)} %get-tuple-element.12), channel_id=1, source_target_pairs={{0,8},{8,0},{16,24},{24,16},{1,9},{9,1},{17,25},{25,17},{2,10},{10... | collective-permute-start | bytes 245768 | tf_op jit(solution)/shard_map/ppermute | solution.py:202
  14.8 1.5 %collective-permute-start.3 = (f32[160,128]{1,0:T(8,128)S(1)}, f32[160,128]{1,0:T(8,128)S(1)}, u32[]{:S(2)}, u32[]{:S(2)}) collective-permute-start(f32[160,128]{1,0:T(8,128)S(1)} %get-tuple-element.13), channel_id=1, source_target_pairs={{0,24},{8,16},{16,8},{24,0},{1,25},{9,17},{17,9},{25,1},{2,26},{10... | collective-permute-start | bytes 245768 | tf_op jit(solution)/shard_map/ppermute | solution.py:202
  16.3 1.2 %collective-permute-done.1 = f32[160,128]{1,0:T(8,128)S(1)} collective-permute-done((f32[160,128]{1,0:T(8,128)S(1)}, f32[160,128]{1,0:T(8,128)S(1)}, u32[]{:S(2)}, u32[]{:S(2)}) %collective-permute-start.1) | collective-permute-done | bytes 81952 | tf_op jit(solution)/shard_map/ppermute | solution.py:202
  17.5 3.1 %collective-permute-done.3 = f32[160,128]{1,0:T(8,128)S(1)} collective-permute-done((f32[160,128]{1,0:T(8,128)S(1)}, f32[160,128]{1,0:T(8,128)S(1)}, u32[]{:S(2)}, u32[]{:S(2)}) %collective-permute-start.3) | collective-permute-done | bytes 81952 | tf_op jit(solution)/shard_map/ppermute | solution.py:202
  20.6 1.2 %collective-permute-done.2 = f32[160,128]{1,0:T(8,128)S(1)} collective-permute-done((f32[160,128]{1,0:T(8,128)S(1)}, f32[160,128]{1,0:T(8,128)S(1)}, u32[]{:S(2)}, u32[]{:S(2)}) %collective-permute-start.2) | collective-permute-done | bytes 81952 | tf_op jit(solution)/shard_map/ppermute | solution.py:202
  21.8 1.6 %collective-permute-start.6 = (f32[160,128]{1,0:T(8,128)S(1)}, f32[160,128]{1,0:T(8,128)S(1)}, u32[]{:S(2)}, u32[]{:S(2)}) collective-permute-start(f32[160,128]{1,0:T(8,128)S(1)} %add_add_fusion), channel_id=1, source_target_pairs={{0,2},{1,3},{2,0},{3,1},{4,6},{5,7},{6,4},{7,5},{8,10},{9,11},{10,... | collective-permute-start | bytes 245768 | tf_op jit(solution)/shard_map/ppermute | solution.py:202
  23.4 2.6 %collective-permute-start.5 = (f32[160,128]{1,0:T(8,128)S(1)}, f32[160,128]{1,0:T(8,128)S(1)}, u32[]{:S(2)}, u32[]{:S(2)}) collective-permute-start(f32[160,128]{1,0:T(8,128)S(1)} %add_add_fusion), channel_id=1, source_target_pairs={{0,4},{1,5},{2,6},{3,7},{4,0},{5,1},{6,2},{7,3},{8,12},{9,13},{10,... | collective-permute-start | bytes 245768 | tf_op jit(solution)/shard_map/ppermute | solution.py:202
  26.2 0.9 collective-permute-done.6
  27.1 4.3 %collective-permute-done.5 = f32[160,128]{1,0:T(8,128)S(1)} collective-permute-done((f32[160,128]{1,0:T(8,128)S(1)}, f32[160,128]{1,0:T(8,128)S(1)}, u32[]{:S(2)}, u32[]{:S(2)}) %collective-permute-start.5) | collective-permute-done | bytes 81952 | tf_op jit(solution)/shard_map/ppermute | solution.py:202
  31.4 0.9 collective-permute-done.4
  32.5 1.5 %collective-permute-start.7 = (f32[160,128]{1,0:T(8,128)S(1)}, f32[160,128]{1,0:T(8,128)S(1)}, u32[]{:S(2)}, u32[]{:S(2)}) collective-permute-start(f32[160,128]{1,0:T(8,128)S(1)} %get-tuple-element.11), channel_id=1, source_target_pairs={{0,8},{8,0},{16,24},{24,16},{1,9},{9,1},{17,25},{25,17},{2,10},{10... | collective-permute-start | bytes 245768 | tf_op jit(solution)/shard_map/ppermute | solution.py:202
  33.9 0.6 collective-permute-start.8
  34.6 1.5 %collective-permute-start.9 = (f32[160,128]{1,0:T(8,128)S(1)}, f32[160,128]{1,0:T(8,128)S(1)}, u32[]{:S(2)}, u32[]{:S(2)}) collective-permute-start(f32[160,128]{1,0:T(8,128)S(1)} %get-tuple-element.11), channel_id=1, source_target_pairs={{0,24},{8,16},{16,8},{24,0},{1,25},{9,17},{17,9},{25,1},{2,26},{10... | collective-permute-start | bytes 245768 | tf_op jit(solution)/shard_map/ppermute | solution.py:202
  36.0 1.0 collective-permute-done.7
  37.0 1.3 %collective-permute-done.8 = f32[160,128]{1,0:T(8,128)S(1)} collective-permute-done((f32[160,128]{1,0:T(8,128)S(1)}, f32[160,128]{1,0:T(8,128)S(1)}, u32[]{:S(2)}, u32[]{:S(2)}) %collective-permute-start.8) | collective-permute-done | bytes 81952 | tf_op jit(solution)/shard_map/ppermute | solution.py:202
  38.4 1.5 %collective-permute-done.9 = f32[160,128]{1,0:T(8,128)S(1)} collective-permute-done((f32[160,128]{1,0:T(8,128)S(1)}, f32[160,128]{1,0:T(8,128)S(1)}, u32[]{:S(2)}, u32[]{:S(2)}) %collective-permute-start.9) | collective-permute-done | bytes 81952 | tf_op jit(solution)/shard_map/ppermute | solution.py:202
  40.0 1.6 %collective-permute-done.10.got_ref = f32[640,128]{1,0:T(8,128)S(1)} collective-permute-done((f32[640,128]{1,0:T(8,128)S(1)}, f32[640,128]{1,0:T(8,128)S(1)}, u32[]{:S(2)}, u32[]{:S(2)}) %collective-permute-start.10) | collective-permute-done | bytes 327712 | tf_op jit(solution)/shard_map/ppermute | solution.py:202
  41.6 0.7 copy-done.1
  42.4 48.2 %shard_map.31 = (f32[512,512]{1,0:T(8,128)}, f32[512,512]{1,0:T(8,128)}) custom-call(s32[1]{0:T(128)} %bitcast.bit_ref, f32[640,128]{1,0:T(8,128)} %copy-done, f32[640,128]{1,0:T(8,128)} %copy-done.1), custom_call_target="tpu_custom_call" | custom-call | tf_op jit(solution)/shard_map/pallas_call | solution.py:101
  90.5 8.5 %shard_map.32 = f32[2048,512]{1,0:T(8,128)} custom-call(f32[2048,512]{1,0:T(8,128)} %a_ref.3, f32[512,512]{1,0:T(8,128)} %get-tuple-element.9.w_ref), custom_call_target="tpu_custom_call" | custom-call | tf_op jit(solution)/shard_map/pallas_call | solution.py:120
  (13 shorter events, 0.5 us)
Async XLA Ops:
  8.9 1.9 %collective-permute-start = (f32[640,128]{1,0:T(8,128)}, f32[640,128]{1,0:T(8,128)S(1)}, u32[]{:S(2)}, u32[]{:S(2)}) collective-permute-start(f32[640,128]{1,0:T(8,128)} %get-tuple-element.7), channel_id=1, source_target_pairs={{0,1},{1,0},{2,3},{3,2},{4,5},{5,4},{6,7},{7,6},{8,9},{9,8},{10,11... | collective-permute-start | bytes 983048 | tf_op jit(solution)/shard_map/ppermute | solution.py:202
  11.8 5.7 %collective-permute-start.1 = (f32[160,128]{1,0:T(8,128)S(1)}, f32[160,128]{1,0:T(8,128)S(1)}, u32[]{:S(2)}, u32[]{:S(2)}) collective-permute-start(f32[160,128]{1,0:T(8,128)S(1)} %get-tuple-element.12), channel_id=1, source_target_pairs={{0,8},{8,0},{16,24},{24,16},{1,9},{9,1},{17,25},{25,17},{2,10},{10... | collective-permute-start | bytes 245768 | tf_op jit(solution)/shard_map/ppermute | solution.py:202
  14.8 5.8 %collective-permute-start.3 = (f32[160,128]{1,0:T(8,128)S(1)}, f32[160,128]{1,0:T(8,128)S(1)}, u32[]{:S(2)}, u32[]{:S(2)}) collective-permute-start(f32[160,128]{1,0:T(8,128)S(1)} %get-tuple-element.13), channel_id=1, source_target_pairs={{0,24},{8,16},{16,8},{24,0},{1,25},{9,17},{17,9},{25,1},{2,26},{10... | collective-permute-start | bytes 245768 | tf_op jit(solution)/shard_map/ppermute | solution.py:202
  16.2 5.5 %collective-permute-start.2 = (f32[160,128]{1,0:T(8,128)S(1)}, f32[160,128]{1,0:T(8,128)S(1)}, u32[]{:S(2)}, u32[]{:S(2)}) collective-permute-start(f32[160,128]{1,0:T(8,128)S(1)} %get-tuple-element.14), channel_id=1, source_target_pairs={{0,16},{8,24},{16,0},{24,8},{1,17},{9,25},{17,1},{25,9},{2,18},{10... | collective-permute-start | bytes 245768 | tf_op jit(solution)/shard_map/ppermute | solution.py:202
  21.8 5.3 %collective-permute-start.6 = (f32[160,128]{1,0:T(8,128)S(1)}, f32[160,128]{1,0:T(8,128)S(1)}, u32[]{:S(2)}, u32[]{:S(2)}) collective-permute-start(f32[160,128]{1,0:T(8,128)S(1)} %add_add_fusion), channel_id=1, source_target_pairs={{0,2},{1,3},{2,0},{3,1},{4,6},{5,7},{6,4},{7,5},{8,10},{9,11},{10,... | collective-permute-start | bytes 245768 | tf_op jit(solution)/shard_map/ppermute | solution.py:202
  23.4 8.0 %collective-permute-start.5 = (f32[160,128]{1,0:T(8,128)S(1)}, f32[160,128]{1,0:T(8,128)S(1)}, u32[]{:S(2)}, u32[]{:S(2)}) collective-permute-start(f32[160,128]{1,0:T(8,128)S(1)} %add_add_fusion), channel_id=1, source_target_pairs={{0,4},{1,5},{2,6},{3,7},{4,0},{5,1},{6,2},{7,3},{8,12},{9,13},{10,... | collective-permute-start | bytes 245768 | tf_op jit(solution)/shard_map/ppermute | solution.py:202
  26.0 6.3 %collective-permute-start.4 = (f32[160,128]{1,0:T(8,128)S(1)}, f32[160,128]{1,0:T(8,128)S(1)}, u32[]{:S(2)}, u32[]{:S(2)}) collective-permute-start(f32[160,128]{1,0:T(8,128)S(1)} %add_add_fusion), channel_id=1, source_target_pairs={{0,6},{1,7},{2,4},{3,5},{4,2},{5,3},{6,0},{7,1},{8,14},{9,15},{10,... | collective-permute-start | bytes 245768 | tf_op jit(solution)/shard_map/ppermute | solution.py:202
  32.5 4.5 %collective-permute-start.7 = (f32[160,128]{1,0:T(8,128)S(1)}, f32[160,128]{1,0:T(8,128)S(1)}, u32[]{:S(2)}, u32[]{:S(2)}) collective-permute-start(f32[160,128]{1,0:T(8,128)S(1)} %get-tuple-element.11), channel_id=1, source_target_pairs={{0,8},{8,0},{16,24},{24,16},{1,9},{9,1},{17,25},{25,17},{2,10},{10... | collective-permute-start | bytes 245768 | tf_op jit(solution)/shard_map/ppermute | solution.py:202
  33.9 4.4 %collective-permute-start.8 = (f32[160,128]{1,0:T(8,128)S(1)}, f32[160,128]{1,0:T(8,128)S(1)}, u32[]{:S(2)}, u32[]{:S(2)}) collective-permute-start(f32[160,128]{1,0:T(8,128)S(1)} %get-tuple-element.11), channel_id=1, source_target_pairs={{0,16},{8,24},{16,0},{24,8},{1,17},{9,25},{17,1},{25,9},{2,18},{10... | collective-permute-start | bytes 245768 | tf_op jit(solution)/shard_map/ppermute | solution.py:202
  34.6 5.3 %collective-permute-start.9 = (f32[160,128]{1,0:T(8,128)S(1)}, f32[160,128]{1,0:T(8,128)S(1)}, u32[]{:S(2)}, u32[]{:S(2)}) collective-permute-start(f32[160,128]{1,0:T(8,128)S(1)} %get-tuple-element.11), channel_id=1, source_target_pairs={{0,24},{8,16},{16,8},{24,0},{1,25},{9,17},{17,9},{25,1},{2,26},{10... | collective-permute-start | bytes 245768 | tf_op jit(solution)/shard_map/ppermute | solution.py:202
  39.9 1.7 %copy-start = (f32[640,128]{1,0:T(8,128)}, f32[640,128]{1,0:T(8,128)S(1)}, u32[]{:S(2)}) copy-start(f32[640,128]{1,0:T(8,128)S(1)} %constant_dynamic-update-slice_fusion.mine_ref) | copy-start | bytes 983044
  39.9 1.7 %collective-permute-start.10 = (f32[640,128]{1,0:T(8,128)S(1)}, f32[640,128]{1,0:T(8,128)S(1)}, u32[]{:S(2)}, u32[]{:S(2)}) collective-permute-start(f32[640,128]{1,0:T(8,128)S(1)} %constant_dynamic-update-slice_fusion.mine_ref), channel_id=1, source_target_pairs={{0,1},{1,0},{2,3},{3,2},{4,5},{5,4},{6,7},{7,6},{8,9},{9,8},{10,11... | collective-permute-start | bytes 983048 | tf_op jit(solution)/shard_map/ppermute | solution.py:202
  41.6 0.7 copy-start.1

commit v11 on v10

--- a/solution.py
+++ b/solution.py
@@ -13,15 +13,6 @@
 
 
 STACK = 5 * BLOCK
-
-
-def lower_stacks(acc_ref):
-    b = BLOCK
-    first = jnp.concatenate([acc_ref[:, 0:b], acc_ref[b:2 * b, b:2 * b]], axis=0)
-    second = jnp.concatenate(
-        [acc_ref[2 * b:4 * b, b:2 * b], acc_ref[2 * b:4 * b, 2 * b:3 * b], acc_ref[3 * b:4 * b, 3 * b:4 * b]], axis=0
-    )
-    return first, second
 
 
 def fill_gram(work_ref, first_ref, second_ref):
@@ -143,52 +134,51 @@
     )
 
 
-def gram_kernel(row_count, bit_ref, a_ref, keep_ref, send_ref, acc_ref):
+def stack_blocks(a, which):
+    b = BLOCK
+    if which == 0:
+        return [cross(a, a[:, 0:b]), cross(a[:, b:2 * b], a[:, b:2 * b])]
+    return [
+        cross(a[:, 2 * b:4 * b], a[:, b:2 * b]),
+        cross(a[:, 2 * b:4 * b], a[:, 2 * b:3 * b]),
+        cross(a[:, 3 * b:4 * b], a[:, 3 * b:4 * b]),
+    ]
+
+
+def stack_kernel(row_count, flip, bit_ref, a_ref, o_ref):
     step = pl.program_id(0)
-    half = a_ref.shape[1] // 2
 
     @pl.when(step == 0)
     def _():
-        acc_ref[...] = jnp.zeros_like(acc_ref)
+        o_ref[...] = jnp.zeros_like(o_ref)
 
     a = a_ref[...]
-    acc_ref[:, 0:half] += cross(a, a[:, 0:half])
-    acc_ref[half:, half:] += cross(a[:, half:], a[:, half:])
+    for which in (0, 1):
+
+        @pl.when((bit_ref[0] ^ flip) == which)
+        def _():
+            start = 0
+            for block in stack_blocks(a, which):
+                o_ref[start:start + block.shape[0], :] += block
+                start += block.shape[0]
 
     @pl.when(step == pl.num_programs(0) - 1)
     def _():
-        first, second = lower_stacks(acc_ref)
-        first = first / row_count
-        second = second / row_count
-
-        @pl.when(bit_ref[0] == 0)
-        def _():
-            keep_ref[...] = first
-            send_ref[...] = second
-
-        @pl.when(bit_ref[0] != 0)
-        def _():
-            keep_ref[...] = second
-            send_ref[...] = first
-
-
-def gram_halves(matrix, row_count, bit):
+        o_ref[...] = o_ref[...] / row_count
+
+
+def gram_stack(matrix, row_count, bit, flip):
     rows, width = matrix.shape
     tile = min(rows, 512)
-    half = jax.ShapeDtypeStruct((STACK, BLOCK), jnp.float32)
     return pl.pallas_call(
-        functools.partial(gram_kernel, row_count),
-        out_shape=(half, half),
+        functools.partial(stack_kernel, row_count, flip),
+        out_shape=jax.ShapeDtypeStruct((STACK, BLOCK), jnp.float32),
         grid=(rows // tile,),
         in_specs=[
             pl.BlockSpec(memory_space=pltpu.SMEM),
             pl.BlockSpec((tile, width), lambda i: (i, 0)),
         ],
-        out_specs=(
-            pl.BlockSpec((STACK, BLOCK), lambda i: (0, 0)),
-            pl.BlockSpec((STACK, BLOCK), lambda i: (0, 0)),
-        ),
-        scratch_shapes=[pltpu.VMEM((width, width), jnp.float32)],
+        out_specs=pl.BlockSpec((STACK, BLOCK), lambda i: (0, 0)),
     )(bit, matrix)
 
 
@@ -249,8 +239,10 @@
 def on_device(response):
     row_count = response.shape[0] * lax.axis_size("inner") * lax.axis_size("wide")
     bit = jnp.reshape(lax.axis_index("wide") & 1, (1,)).astype(jnp.int32)
-    keep, send = gram_halves(response, row_count, bit)
-    partial_sum = keep + partner_xor(send, "wide", 0, 1)
+    send = gram_stack(response, row_count, bit, 1)
+    received = partner_xor(send, "wide", 0, 1)
+    keep = gram_stack(response, row_count, bit, 0)
+    partial_sum = keep + received
     groups = axis_groups("inner", 0) + axis_groups("wide", 1)
     for group in groups[:-1]:
         partial_sum = scatter_sum(partial_sum, *group)

time: 99.3 us -> 104 us (1.047)
  Pallas kernels: 64.9 us -> 71.3 us
    pallas_call x1 -> x2, Pallas kernels: 8.23 us -> 14.6 us  [gram_stack(): pl.pallas_call(functools.partial(stack_kernel, row_count, flip), out_shap...]
  transfers between devices with their start and end apart: 11 -> 11, of which waited for: 11 -> 9; matrix products, arithmetic and copies ran while one was open for 0% -> 0% of each run, Pallas kernels for 0% -> 7%
where the time goes in v11:
time: 104 us
  Pallas kernels  71.3 us (69%)
  waiting for transfers between devices  17.5 us (17%)
  starting transfers between devices  12.6 us (12%)
  other arithmetic  1.08 us (1%)
    pallas_call x1, Pallas kernels, cholesky_and_inverse(): pl.pallas_call(chol_kernel, out_shape=(jax.ShapeDtypeStruct((n, n), jnp.f...  48.2 us
    ppermute x11, waiting for transfers between devices, partner_xor(): return lax.ppermute(value, axis, pairs)  17.5 us
    pallas_call x2, Pallas kernels, gram_stack(): pl.pallas_call(functools.partial(stack_kernel, row_count, flip), out_shap...  14.6 us
    ppermute x11, starting transfers between devices, partner_xor(): return lax.ppermute(value, axis, pairs)  12.6 us
    pallas_call x1, Pallas kernels, rows_times(): pl.pallas_call(rows_kernel, out_shape=jax.ShapeDtypeStruct((rows, weights...  8.46 us
  transfers between devices with their start and end apart: 11, of which 9 were waited for; matrix products, arithmetic and copies ran while one was open for 0% of the time, Pallas kernels for 7%

profile of v11, /device:TPU:0, one launch (start us, length us, event | category | flops | bytes accessed | tf_op | source)
XLA Modules:
  0.0 104.0 jit_solution(5049304486682840999)
XLA Ops:
  0.6 7.3 %shard_map.31 = f32[640,128]{1,0:T(8,128)} custom-call(s32[1]{0:T(128)} %bitcast.bit_ref, f32[2048,512]{1,0:T(8,128)} %a_ref.5), custom_call_target="tpu_custom_call" | custom-call | tf_op jit(solution)/shard_map/pallas_call | solution.py:173
  7.9 0.5 collective-permute-start
  8.4 7.3 %shard_map.30 = f32[640,128]{1,0:T(8,128)} custom-call(s32[1]{0:T(128)} %bitcast.bit_ref, f32[2048,512]{1,0:T(8,128)} %a_ref.5), custom_call_target="tpu_custom_call" | custom-call | tf_op jit(solution)/shard_map/pallas_call | solution.py:173
  15.7 1.0 add.37
  16.8 2.5 %collective-permute-start.1 = (f32[160,128]{1,0:T(8,128)S(1)}, f32[160,128]{1,0:T(8,128)S(1)}, u32[]{:S(2)}, u32[]{:S(2)}) collective-permute-start(f32[160,128]{1,0:T(8,128)S(1)} %get-tuple-element.8), channel_id=1, source_target_pairs={{0,8},{8,0},{16,24},{24,16},{1,9},{9,1},{17,25},{25,17},{2,10},{10... | collective-permute-start | bytes 245768 | tf_op jit(solution)/shard_map/ppermute | solution.py:192
  19.3 1.5 %collective-permute-start.3 = (f32[160,128]{1,0:T(8,128)S(1)}, f32[160,128]{1,0:T(8,128)S(1)}, u32[]{:S(2)}, u32[]{:S(2)}) collective-permute-start(f32[160,128]{1,0:T(8,128)S(1)} %get-tuple-element.9), channel_id=1, source_target_pairs={{0,24},{8,16},{16,8},{24,0},{1,25},{9,17},{17,9},{25,1},{2,26},{10... | collective-permute-start | bytes 245768 | tf_op jit(solution)/shard_map/ppermute | solution.py:192
  20.8 1.5 %collective-permute-done.1 = f32[160,128]{1,0:T(8,128)S(1)} collective-permute-done((f32[160,128]{1,0:T(8,128)S(1)}, f32[160,128]{1,0:T(8,128)S(1)}, u32[]{:S(2)}, u32[]{:S(2)}) %collective-permute-start.1) | collective-permute-done | bytes 81952 | tf_op jit(solution)/shard_map/ppermute | solution.py:192
  22.4 3.1 %collective-permute-done.3 = f32[160,128]{1,0:T(8,128)S(1)} collective-permute-done((f32[160,128]{1,0:T(8,128)S(1)}, f32[160,128]{1,0:T(8,128)S(1)}, u32[]{:S(2)}, u32[]{:S(2)}) %collective-permute-start.3) | collective-permute-done | bytes 81952 | tf_op jit(solution)/shard_map/ppermute | solution.py:192
  25.5 1.3 %collective-permute-done.2 = f32[160,128]{1,0:T(8,128)S(1)} collective-permute-done((f32[160,128]{1,0:T(8,128)S(1)}, f32[160,128]{1,0:T(8,128)S(1)}, u32[]{:S(2)}, u32[]{:S(2)}) %collective-permute-start.2) | collective-permute-done | bytes 81952 | tf_op jit(solution)/shard_map/ppermute | solution.py:192
  26.8 1.6 %collective-permute-start.6 = (f32[160,128]{1,0:T(8,128)S(1)}, f32[160,128]{1,0:T(8,128)S(1)}, u32[]{:S(2)}, u32[]{:S(2)}) collective-permute-start(f32[160,128]{1,0:T(8,128)S(1)} %add_add_fusion), channel_id=1, source_target_pairs={{0,2},{1,3},{2,0},{3,1},{4,6},{5,7},{6,4},{7,5},{8,10},{9,11},{10,... | collective-permute-start | bytes 245768 | tf_op jit(solution)/shard_map/ppermute | solution.py:192
  28.4 2.6 %collective-permute-start.5 = (f32[160,128]{1,0:T(8,128)S(1)}, f32[160,128]{1,0:T(8,128)S(1)}, u32[]{:S(2)}, u32[]{:S(2)}) collective-permute-start(f32[160,128]{1,0:T(8,128)S(1)} %add_add_fusion), channel_id=1, source_target_pairs={{0,4},{1,5},{2,6},{3,7},{4,0},{5,1},{6,2},{7,3},{8,12},{9,13},{10,... | collective-permute-start | bytes 245768 | tf_op jit(solution)/shard_map/ppermute | solution.py:192
  31.0 0.2 collective-permute-start.4
  31.3 6.1 %collective-permute-done.5 = f32[160,128]{1,0:T(8,128)S(1)} collective-permute-done((f32[160,128]{1,0:T(8,128)S(1)}, f32[160,128]{1,0:T(8,128)S(1)}, u32[]{:S(2)}, u32[]{:S(2)}) %collective-permute-start.5) | collective-permute-done | bytes 81952 | tf_op jit(solution)/shard_map/ppermute | solution.py:192
  37.5 1.6 %collective-permute-start.7 = (f32[160,128]{1,0:T(8,128)S(1)}, f32[160,128]{1,0:T(8,128)S(1)}, u32[]{:S(2)}, u32[]{:S(2)}) collective-permute-start(f32[160,128]{1,0:T(8,128)S(1)} %get-tuple-element.7), channel_id=1, source_target_pairs={{0,8},{8,0},{16,24},{24,16},{1,9},{9,1},{17,25},{25,17},{2,10},{10... | collective-permute-start | bytes 245768 | tf_op jit(solution)/shard_map/ppermute | solution.py:192
  39.1 0.5 collective-permute-start.8
  39.6 1.5 %collective-permute-start.9 = (f32[160,128]{1,0:T(8,128)S(1)}, f32[160,128]{1,0:T(8,128)S(1)}, u32[]{:S(2)}, u32[]{:S(2)}) collective-permute-start(f32[160,128]{1,0:T(8,128)S(1)} %get-tuple-element.7), channel_id=1, source_target_pairs={{0,24},{8,16},{16,8},{24,0},{1,25},{9,17},{17,9},{25,1},{2,26},{10... | collective-permute-start | bytes 245768 | tf_op jit(solution)/shard_map/ppermute | solution.py:192
  41.1 1.2 %collective-permute-done.7 = f32[160,128]{1,0:T(8,128)S(1)} collective-permute-done((f32[160,128]{1,0:T(8,128)S(1)}, f32[160,128]{1,0:T(8,128)S(1)}, u32[]{:S(2)}, u32[]{:S(2)}) %collective-permute-start.7) | collective-permute-done | bytes 81952 | tf_op jit(solution)/shard_map/ppermute | solution.py:192
  42.3 1.2 %collective-permute-done.8 = f32[160,128]{1,0:T(8,128)S(1)} collective-permute-done((f32[160,128]{1,0:T(8,128)S(1)}, f32[160,128]{1,0:T(8,128)S(1)}, u32[]{:S(2)}, u32[]{:S(2)}) %collective-permute-start.8) | collective-permute-done | bytes 81952 | tf_op jit(solution)/shard_map/ppermute | solution.py:192
  43.5 1.4 %collective-permute-done.9 = f32[160,128]{1,0:T(8,128)S(1)} collective-permute-done((f32[160,128]{1,0:T(8,128)S(1)}, f32[160,128]{1,0:T(8,128)S(1)}, u32[]{:S(2)}, u32[]{:S(2)}) %collective-permute-start.9) | collective-permute-done | bytes 81952 | tf_op jit(solution)/shard_map/ppermute | solution.py:192
  44.9 0.1 collective-permute-start.10
  45.0 1.6 %collective-permute-done.10.got_ref = f32[640,128]{1,0:T(8,128)S(1)} collective-permute-done((f32[640,128]{1,0:T(8,128)S(1)}, f32[640,128]{1,0:T(8,128)S(1)}, u32[]{:S(2)}, u32[]{:S(2)}) %collective-permute-start.10) | collective-permute-done | bytes 327712 | tf_op jit(solution)/shard_map/ppermute | solution.py:192
  46.6 0.7 copy-done.1
  47.4 48.2 %shard_map.32 = (f32[512,512]{1,0:T(8,128)}, f32[512,512]{1,0:T(8,128)}) custom-call(s32[1]{0:T(128)} %bitcast.bit_ref, f32[640,128]{1,0:T(8,128)} %copy-done, f32[640,128]{1,0:T(8,128)} %copy-done.1), custom_call_target="tpu_custom_call" | custom-call | tf_op jit(solution)/shard_map/pallas_call | solution.py:92
  95.6 8.5 %shard_map.33 = f32[2048,512]{1,0:T(8,128)} custom-call(f32[2048,512]{1,0:T(8,128)} %a_ref.5, f32[512,512]{1,0:T(8,128)} %get-tuple-element.5.w_ref), custom_call_target="tpu_custom_call" | custom-call | tf_op jit(solution)/shard_map/pallas_call | solution.py:111
  (14 shorter events, 0.3 us)
Async XLA Ops:
  7.9 7.8 %collective-permute-start = (f32[640,128]{1,0:T(8,128)}, f32[640,128]{1,0:T(8,128)S(1)}, u32[]{:S(2)}, u32[]{:S(2)}) collective-permute-start(f32[640,128]{1,0:T(8,128)} %shard_map.31), channel_id=1, source_target_pairs={{0,1},{1,0},{2,3},{3,2},{4,5},{5,4},{6,7},{7,6},{8,9},{9,8},{10,11... | collective-permute-start | bytes 983048 | tf_op jit(solution)/shard_map/ppermute | solution.py:192
  16.8 5.6 %collective-permute-start.1 = (f32[160,128]{1,0:T(8,128)S(1)}, f32[160,128]{1,0:T(8,128)S(1)}, u32[]{:S(2)}, u32[]{:S(2)}) collective-permute-start(f32[160,128]{1,0:T(8,128)S(1)} %get-tuple-element.8), channel_id=1, source_target_pairs={{0,8},{8,0},{16,24},{24,16},{1,9},{9,1},{17,25},{25,17},{2,10},{10... | collective-permute-start | bytes 245768 | tf_op jit(solution)/shard_map/ppermute | solution.py:192
  19.3 6.2 %collective-permute-start.3 = (f32[160,128]{1,0:T(8,128)S(1)}, f32[160,128]{1,0:T(8,128)S(1)}, u32[]{:S(2)}, u32[]{:S(2)}) collective-permute-start(f32[160,128]{1,0:T(8,128)S(1)} %get-tuple-element.9), channel_id=1, source_target_pairs={{0,24},{8,16},{16,8},{24,0},{1,25},{9,17},{17,9},{25,1},{2,26},{10... | collective-permute-start | bytes 245768 | tf_op jit(solution)/shard_map/ppermute | solution.py:192
  20.8 6.0 %collective-permute-start.2 = (f32[160,128]{1,0:T(8,128)S(1)}, f32[160,128]{1,0:T(8,128)S(1)}, u32[]{:S(2)}, u32[]{:S(2)}) collective-permute-start(f32[160,128]{1,0:T(8,128)S(1)} %get-tuple-element.10), channel_id=1, source_target_pairs={{0,16},{8,24},{16,0},{24,8},{1,17},{9,25},{17,1},{25,9},{2,18},{10... | collective-permute-start | bytes 245768 | tf_op jit(solution)/shard_map/ppermute | solution.py:192
  26.8 4.5 %collective-permute-start.6 = (f32[160,128]{1,0:T(8,128)S(1)}, f32[160,128]{1,0:T(8,128)S(1)}, u32[]{:S(2)}, u32[]{:S(2)}) collective-permute-start(f32[160,128]{1,0:T(8,128)S(1)} %add_add_fusion), channel_id=1, source_target_pairs={{0,2},{1,3},{2,0},{3,1},{4,6},{5,7},{6,4},{7,5},{8,10},{9,11},{10,... | collective-permute-start | bytes 245768 | tf_op jit(solution)/shard_map/ppermute | solution.py:192
  28.4 9.0 %collective-permute-start.5 = (f32[160,128]{1,0:T(8,128)S(1)}, f32[160,128]{1,0:T(8,128)S(1)}, u32[]{:S(2)}, u32[]{:S(2)}) collective-permute-start(f32[160,128]{1,0:T(8,128)S(1)} %add_add_fusion), channel_id=1, source_target_pairs={{0,4},{1,5},{2,6},{3,7},{4,0},{5,1},{6,2},{7,3},{8,12},{9,13},{10,... | collective-permute-start | bytes 245768 | tf_op jit(solution)/shard_map/ppermute | solution.py:192
  31.0 6.4 %collective-permute-start.4 = (f32[160,128]{1,0:T(8,128)S(1)}, f32[160,128]{1,0:T(8,128)S(1)}, u32[]{:S(2)}, u32[]{:S(2)}) collective-permute-start(f32[160,128]{1,0:T(8,128)S(1)} %add_add_fusion), channel_id=1, source_target_pairs={{0,6},{1,7},{2,4},{3,5},{4,2},{5,3},{6,0},{7,1},{8,14},{9,15},{10,... | collective-permute-start | bytes 245768 | tf_op jit(solution)/shard_map/ppermute | solution.py:192
  37.5 4.8 %collective-permute-start.7 = (f32[160,128]{1,0:T(8,128)S(1)}, f32[160,128]{1,0:T(8,128)S(1)}, u32[]{:S(2)}, u32[]{:S(2)}) collective-permute-start(f32[160,128]{1,0:T(8,128)S(1)} %get-tuple-element.7), channel_id=1, source_target_pairs={{0,8},{8,0},{16,24},{24,16},{1,9},{9,1},{17,25},{25,17},{2,10},{10... | collective-permute-start | bytes 245768 | tf_op jit(solution)/shard_map/ppermute | solution.py:192
  39.1 4.4 %collective-permute-start.8 = (f32[160,128]{1,0:T(8,128)S(1)}, f32[160,128]{1,0:T(8,128)S(1)}, u32[]{:S(2)}, u32[]{:S(2)}) collective-permute-start(f32[160,128]{1,0:T(8,128)S(1)} %get-tuple-element.7), channel_id=1, source_target_pairs={{0,16},{8,24},{16,0},{24,8},{1,17},{9,25},{17,1},{25,9},{2,18},{10... | collective-permute-start | bytes 245768 | tf_op jit(solution)/shard_map/ppermute | solution.py:192
  39.6 5.3 %collective-permute-start.9 = (f32[160,128]{1,0:T(8,128)S(1)}, f32[160,128]{1,0:T(8,128)S(1)}, u32[]{:S(2)}, u32[]{:S(2)}) collective-permute-start(f32[160,128]{1,0:T(8,128)S(1)} %get-tuple-element.7), channel_id=1, source_target_pairs={{0,24},{8,16},{16,8},{24,0},{1,25},{9,17},{17,9},{25,1},{2,26},{10... | collective-permute-start | bytes 245768 | tf_op jit(solution)/shard_map/ppermute | solution.py:192
  44.9 1.7 %copy-start = (f32[640,128]{1,0:T(8,128)}, f32[640,128]{1,0:T(8,128)S(1)}, u32[]{:S(2)}) copy-start(f32[640,128]{1,0:T(8,128)S(1)} %constant_dynamic-update-slice_fusion.mine_ref) | copy-start | bytes 983044
  44.9 1.7 %collective-permute-start.10 = (f32[640,128]{1,0:T(8,128)S(1)}, f32[640,128]{1,0:T(8,128)S(1)}, u32[]{:S(2)}, u32[]{:S(2)}) collective-permute-start(f32[640,128]{1,0:T(8,128)S(1)} %constant_dynamic-update-slice_fusion.mine_ref), channel_id=1, source_target_pairs={{0,1},{1,0},{2,3},{3,2},{4,5},{5,4},{6,7},{7,6},{8,9},{9,8},{10,11... | collective-permute-start | bytes 983048 | tf_op jit(solution)/shard_map/ppermute | solution.py:192
  46.6 0.7 copy-start.1

commit v12 on v10

--- a/solution.py
+++ b/solution.py
@@ -251,7 +251,7 @@
     bit = jnp.reshape(lax.axis_index("wide") & 1, (1,)).astype(jnp.int32)
     keep, send = gram_halves(response, row_count, bit)
     partial_sum = keep + partner_xor(send, "wide", 0, 1)
-    groups = axis_groups("inner", 0) + axis_groups("wide", 1)
+    groups = axis_groups("wide", 1) + axis_groups("inner", 0)
     for group in groups[:-1]:
         partial_sum = scatter_sum(partial_sum, *group)
     partial_sum = group_total(partial_sum, *groups[-1])

time: 99.3 us -> 103 us (1.037)
  waiting for transfers between devices: 18.5 us -> 20.7 us
  starting transfers between devices: 13 us -> 14.1 us
    ppermute x11, waiting for transfers between devices: 18.5 us -> 20.7 us  [partner_xor(): return lax.ppermute(value, axis, pairs)]
    ppermute x11, starting transfers between devices: 13 us -> 14.1 us  [partner_xor(): return lax.ppermute(value, axis, pairs)]
where the time goes in v12:
time: 103 us; the launch traced here: 102 us
  Pallas kernels  64.9 us (63%)
  waiting for transfers between devices  20.7 us (20%)
  starting transfers between devices  14.1 us (14%)
  other arithmetic  1.08 us (1%)
    pallas_call x1, Pallas kernels, cholesky_and_inverse(): pl.pallas_call(chol_kernel, out_shape=(jax.ShapeDtypeStruct((n, n), jnp.f...  48.2 us
    ppermute x11, waiting for transfers between devices, partner_xor(): return lax.ppermute(value, axis, pairs)  20.7 us
    ppermute x11, starting transfers between devices, partner_xor(): return lax.ppermute(value, axis, pairs)  14.1 us
    pallas_call x1, Pallas kernels, rows_times(): pl.pallas_call(rows_kernel, out_shape=jax.ShapeDtypeStruct((rows, weights...  8.46 us
    pallas_call x1, Pallas kernels, gram_halves(): pl.pallas_call(functools.partial(gram_kernel, row_count), out_shape=(half...  8.23 us
  transfers between devices with their start and end apart: 11, of which 11 were waited for; matrix products, arithmetic and copies ran while one was open for 0% of the time, Pallas kernels for 0%

profile of v12, /device:TPU:0, one launch (start us, length us, event | category | flops | bytes accessed | tf_op | source)
XLA Modules:
  0.0 102.3 jit_solution(15806041670424584424)
XLA Ops:
  0.6 8.2 %shard_map.30 = (f32[640,128]{1,0:T(8,128)}, f32[640,128]{1,0:T(8,128)}) custom-call(s32[1]{0:T(128)} %bitcast.bit_ref, f32[2048,512]{1,0:T(8,128)} %a_ref.3), custom_call_target="tpu_custom_call" | custom-call | tf_op jit(solution)/shard_map/pallas_call | solution.py:179
  8.9 0.5 collective-permute-start
  9.3 1.5 %collective-permute-done = f32[640,128]{1,0:T(8,128)S(1)} collective-permute-done((f32[640,128]{1,0:T(8,128)}, f32[640,128]{1,0:T(8,128)S(1)}, u32[]{:S(2)}, u32[]{:S(2)}) %collective-permute-start) | collective-permute-done | bytes 327712 | tf_op jit(solution)/shard_map/ppermute | solution.py:202
  10.8 1.0 add.37
  11.8 3.0 %collective-permute-start.1 = (f32[160,128]{1,0:T(8,128)S(1)}, f32[160,128]{1,0:T(8,128)S(1)}, u32[]{:S(2)}, u32[]{:S(2)}) collective-permute-start(f32[160,128]{1,0:T(8,128)S(1)} %get-tuple-element.12), channel_id=1, source_target_pairs={{0,2},{1,3},{2,0},{3,1},{4,6},{5,7},{6,4},{7,5},{8,10},{9,11},{10,... | collective-permute-start | bytes 245768 | tf_op jit(solution)/shard_map/ppermute | solution.py:202
  14.8 2.5 %collective-permute-start.3 = (f32[160,128]{1,0:T(8,128)S(1)}, f32[160,128]{1,0:T(8,128)S(1)}, u32[]{:S(2)}, u32[]{:S(2)}) collective-permute-start(f32[160,128]{1,0:T(8,128)S(1)} %get-tuple-element.13), channel_id=1, source_target_pairs={{0,6},{1,7},{2,4},{3,5},{4,2},{5,3},{6,0},{7,1},{8,14},{9,15},{10,... | collective-permute-start | bytes 245768 | tf_op jit(solution)/shard_map/ppermute | solution.py:202
  17.3 0.1 collective-permute-start.2
  17.4 0.2 collective-permute-done.1
  17.6 4.7 %collective-permute-done.3 = f32[160,128]{1,0:T(8,128)S(1)} collective-permute-done((f32[160,128]{1,0:T(8,128)S(1)}, f32[160,128]{1,0:T(8,128)S(1)}, u32[]{:S(2)}, u32[]{:S(2)}) %collective-permute-start.3) | collective-permute-done | bytes 81952 | tf_op jit(solution)/shard_map/ppermute | solution.py:202
  22.3 2.9 %collective-permute-done.2 = f32[160,128]{1,0:T(8,128)S(1)} collective-permute-done((f32[160,128]{1,0:T(8,128)S(1)}, f32[160,128]{1,0:T(8,128)S(1)}, u32[]{:S(2)}, u32[]{:S(2)}) %collective-permute-start.2) | collective-permute-done | bytes 81952 | tf_op jit(solution)/shard_map/ppermute | solution.py:202
  25.2 1.6 %collective-permute-start.6 = (f32[160,128]{1,0:T(8,128)S(1)}, f32[160,128]{1,0:T(8,128)S(1)}, u32[]{:S(2)}, u32[]{:S(2)}) collective-permute-start(f32[160,128]{1,0:T(8,128)S(1)} %add_add_fusion), channel_id=1, source_target_pairs={{0,8},{8,0},{16,24},{24,16},{1,9},{9,1},{17,25},{25,17},{2,10},{10... | collective-permute-start | bytes 245768 | tf_op jit(solution)/shard_map/ppermute | solution.py:202
  26.7 1.5 %collective-permute-start.5 = (f32[160,128]{1,0:T(8,128)S(1)}, f32[160,128]{1,0:T(8,128)S(1)}, u32[]{:S(2)}, u32[]{:S(2)}) collective-permute-start(f32[160,128]{1,0:T(8,128)S(1)} %add_add_fusion), channel_id=1, source_target_pairs={{0,16},{8,24},{16,0},{24,8},{1,17},{9,25},{17,1},{25,9},{2,18},{10... | collective-permute-start | bytes 245768 | tf_op jit(solution)/shard_map/ppermute | solution.py:202
  28.3 0.5 collective-permute-start.4
  28.7 1.0 collective-permute-done.6
  29.7 1.5 %collective-permute-done.5 = f32[160,128]{1,0:T(8,128)S(1)} collective-permute-done((f32[160,128]{1,0:T(8,128)S(1)}, f32[160,128]{1,0:T(8,128)S(1)}, u32[]{:S(2)}, u32[]{:S(2)}) %collective-permute-start.5) | collective-permute-done | bytes 81952 | tf_op jit(solution)/shard_map/ppermute | solution.py:202
  31.2 2.4 %collective-permute-done.4 = f32[160,128]{1,0:T(8,128)S(1)} collective-permute-done((f32[160,128]{1,0:T(8,128)S(1)}, f32[160,128]{1,0:T(8,128)S(1)}, u32[]{:S(2)}, u32[]{:S(2)}) %collective-permute-start.4) | collective-permute-done | bytes 81952 | tf_op jit(solution)/shard_map/ppermute | solution.py:202
  33.8 3.2 %collective-permute-start.8 = (f32[160,128]{1,0:T(8,128)S(1)}, f32[160,128]{1,0:T(8,128)S(1)}, u32[]{:S(2)}, u32[]{:S(2)}) collective-permute-start(f32[160,128]{1,0:T(8,128)S(1)} %get-tuple-element.11), channel_id=1, source_target_pairs={{0,4},{1,5},{2,6},{3,7},{4,0},{5,1},{6,2},{7,3},{8,12},{9,13},{10,... | collective-permute-start | bytes 245768 | tf_op jit(solution)/shard_map/ppermute | solution.py:202
  37.0 1.2 %collective-permute-start.9 = (f32[160,128]{1,0:T(8,128)S(1)}, f32[160,128]{1,0:T(8,128)S(1)}, u32[]{:S(2)}, u32[]{:S(2)}) collective-permute-start(f32[160,128]{1,0:T(8,128)S(1)} %get-tuple-element.11), channel_id=1, source_target_pairs={{0,6},{1,7},{2,4},{3,5},{4,2},{5,3},{6,0},{7,1},{8,14},{9,15},{10,... | collective-permute-start | bytes 245768 | tf_op jit(solution)/shard_map/ppermute | solution.py:202
  38.2 2.9 %collective-permute-done.8 = f32[160,128]{1,0:T(8,128)S(1)} collective-permute-done((f32[160,128]{1,0:T(8,128)S(1)}, f32[160,128]{1,0:T(8,128)S(1)}, u32[]{:S(2)}, u32[]{:S(2)}) %collective-permute-start.8) | collective-permute-done | bytes 81952 | tf_op jit(solution)/shard_map/ppermute | solution.py:202
  41.1 2.1 %collective-permute-done.9 = f32[160,128]{1,0:T(8,128)S(1)} collective-permute-done((f32[160,128]{1,0:T(8,128)S(1)}, f32[160,128]{1,0:T(8,128)S(1)}, u32[]{:S(2)}, u32[]{:S(2)}) %collective-permute-start.9) | collective-permute-done | bytes 81952 | tf_op jit(solution)/shard_map/ppermute | solution.py:202
  43.3 1.6 %collective-permute-done.10.got_ref = f32[640,128]{1,0:T(8,128)S(1)} collective-permute-done((f32[640,128]{1,0:T(8,128)S(1)}, f32[640,128]{1,0:T(8,128)S(1)}, u32[]{:S(2)}, u32[]{:S(2)}) %collective-permute-start.10) | collective-permute-done | bytes 327712 | tf_op jit(solution)/shard_map/ppermute | solution.py:202
  44.9 0.7 copy-done.1
  45.7 48.2 %shard_map.31 = (f32[512,512]{1,0:T(8,128)}, f32[512,512]{1,0:T(8,128)}) custom-call(s32[1]{0:T(128)} %bitcast.bit_ref, f32[640,128]{1,0:T(8,128)} %copy-done, f32[640,128]{1,0:T(8,128)} %copy-done.1), custom_call_target="tpu_custom_call" | custom-call | tf_op jit(solution)/shard_map/pallas_call | solution.py:101
  93.8 8.5 %shard_map.32 = f32[2048,512]{1,0:T(8,128)} custom-call(f32[2048,512]{1,0:T(8,128)} %a_ref.3, f32[512,512]{1,0:T(8,128)} %get-tuple-element.9.w_ref), custom_call_target="tpu_custom_call" | custom-call | tf_op jit(solution)/shard_map/pallas_call | solution.py:120
  (13 shorter events, 0.4 us)
Async XLA Ops:
  8.9 1.9 %collective-permute-start = (f32[640,128]{1,0:T(8,128)}, f32[640,128]{1,0:T(8,128)S(1)}, u32[]{:S(2)}, u32[]{:S(2)}) collective-permute-start(f32[640,128]{1,0:T(8,128)} %get-tuple-element.7), channel_id=1, source_target_pairs={{0,1},{1,0},{2,3},{3,2},{4,5},{5,4},{6,7},{7,6},{8,9},{9,8},{10,11... | collective-permute-start | bytes 983048 | tf_op jit(solution)/shard_map/ppermute | solution.py:202
  11.8 5.7 %collective-permute-start.1 = (f32[160,128]{1,0:T(8,128)S(1)}, f32[160,128]{1,0:T(8,128)S(1)}, u32[]{:S(2)}, u32[]{:S(2)}) collective-permute-start(f32[160,128]{1,0:T(8,128)S(1)} %get-tuple-element.12), channel_id=1, source_target_pairs={{0,2},{1,3},{2,0},{3,1},{4,6},{5,7},{6,4},{7,5},{8,10},{9,11},{10,... | collective-permute-start | bytes 245768 | tf_op jit(solution)/shard_map/ppermute | solution.py:202
  14.8 7.5 %collective-permute-start.3 = (f32[160,128]{1,0:T(8,128)S(1)}, f32[160,128]{1,0:T(8,128)S(1)}, u32[]{:S(2)}, u32[]{:S(2)}) collective-permute-start(f32[160,128]{1,0:T(8,128)S(1)} %get-tuple-element.13), channel_id=1, source_target_pairs={{0,6},{1,7},{2,4},{3,5},{4,2},{5,3},{6,0},{7,1},{8,14},{9,15},{10,... | collective-permute-start | bytes 245768 | tf_op jit(solution)/shard_map/ppermute | solution.py:202
  17.3 7.8 %collective-permute-start.2 = (f32[160,128]{1,0:T(8,128)S(1)}, f32[160,128]{1,0:T(8,128)S(1)}, u32[]{:S(2)}, u32[]{:S(2)}) collective-permute-start(f32[160,128]{1,0:T(8,128)S(1)} %get-tuple-element.14), channel_id=1, source_target_pairs={{0,4},{1,5},{2,6},{3,7},{4,0},{5,1},{6,2},{7,3},{8,12},{9,13},{10,... | collective-permute-start | bytes 245768 | tf_op jit(solution)/shard_map/ppermute | solution.py:202
  25.2 4.5 %collective-permute-start.6 = (f32[160,128]{1,0:T(8,128)S(1)}, f32[160,128]{1,0:T(8,128)S(1)}, u32[]{:S(2)}, u32[]{:S(2)}) collective-permute-start(f32[160,128]{1,0:T(8,128)S(1)} %add_add_fusion), channel_id=1, source_target_pairs={{0,8},{8,0},{16,24},{24,16},{1,9},{9,1},{17,25},{25,17},{2,10},{10... | collective-permute-start | bytes 245768 | tf_op jit(solution)/shard_map/ppermute | solution.py:202
  26.7 4.4 %collective-permute-start.5 = (f32[160,128]{1,0:T(8,128)S(1)}, f32[160,128]{1,0:T(8,128)S(1)}, u32[]{:S(2)}, u32[]{:S(2)}) collective-permute-start(f32[160,128]{1,0:T(8,128)S(1)} %add_add_fusion), channel_id=1, source_target_pairs={{0,16},{8,24},{16,0},{24,8},{1,17},{9,25},{17,1},{25,9},{2,18},{10... | collective-permute-start | bytes 245768 | tf_op jit(solution)/shard_map/ppermute | solution.py:202
  28.3 5.3 %collective-permute-start.4 = (f32[160,128]{1,0:T(8,128)S(1)}, f32[160,128]{1,0:T(8,128)S(1)}, u32[]{:S(2)}, u32[]{:S(2)}) collective-permute-start(f32[160,128]{1,0:T(8,128)S(1)} %add_add_fusion), channel_id=1, source_target_pairs={{0,24},{8,16},{16,8},{24,0},{1,25},{9,17},{17,9},{25,1},{2,26},{10... | collective-permute-start | bytes 245768 | tf_op jit(solution)/shard_map/ppermute | solution.py:202
  33.7 4.5 %collective-permute-start.7 = (f32[160,128]{1,0:T(8,128)S(1)}, f32[160,128]{1,0:T(8,128)S(1)}, u32[]{:S(2)}, u32[]{:S(2)}) collective-permute-start(f32[160,128]{1,0:T(8,128)S(1)} %get-tuple-element.11), channel_id=1, source_target_pairs={{0,2},{1,3},{2,0},{3,1},{4,6},{5,7},{6,4},{7,5},{8,10},{9,11},{10,... | collective-permute-start | bytes 245768 | tf_op jit(solution)/shard_map/ppermute | solution.py:202
  33.8 7.4 %collective-permute-start.8 = (f32[160,128]{1,0:T(8,128)S(1)}, f32[160,128]{1,0:T(8,128)S(1)}, u32[]{:S(2)}, u32[]{:S(2)}) collective-permute-start(f32[160,128]{1,0:T(8,128)S(1)} %get-tuple-element.11), channel_id=1, source_target_pairs={{0,4},{1,5},{2,6},{3,7},{4,0},{5,1},{6,2},{7,3},{8,12},{9,13},{10,... | collective-permute-start | bytes 245768 | tf_op jit(solution)/shard_map/ppermute | solution.py:202
  37.0 6.2 %collective-permute-start.9 = (f32[160,128]{1,0:T(8,128)S(1)}, f32[160,128]{1,0:T(8,128)S(1)}, u32[]{:S(2)}, u32[]{:S(2)}) collective-permute-start(f32[160,128]{1,0:T(8,128)S(1)} %get-tuple-element.11), channel_id=1, source_target_pairs={{0,6},{1,7},{2,4},{3,5},{4,2},{5,3},{6,0},{7,1},{8,14},{9,15},{10,... | collective-permute-start | bytes 245768 | tf_op jit(solution)/shard_map/ppermute | solution.py:202
  43.2 1.7 %copy-start = (f32[640,128]{1,0:T(8,128)}, f32[640,128]{1,0:T(8,128)S(1)}, u32[]{:S(2)}) copy-start(f32[640,128]{1,0:T(8,128)S(1)} %constant_dynamic-update-slice_fusion.mine_ref) | copy-start | bytes 983044
  43.2 1.7 %collective-permute-start.10 = (f32[640,128]{1,0:T(8,128)S(1)}, f32[640,128]{1,0:T(8,128)S(1)}, u32[]{:S(2)}, u32[]{:S(2)}) collective-permute-start(f32[640,128]{1,0:T(8,128)S(1)} %constant_dynamic-update-slice_fusion.mine_ref), channel_id=1, source_target_pairs={{0,1},{1,0},{2,3},{3,2},{4,5},{5,4},{6,7},{7,6},{8,9},{9,8},{10,11... | collective-permute-start | bytes 983048 | tf_op jit(solution)/shard_map/ppermute | solution.py:202
  44.9 0.7 copy-start.1

commit v13 on v10

--- a/solution.py
+++ b/solution.py
@@ -12,25 +12,50 @@
 SLAB = 8
 
 
-STACK = 5 * BLOCK
+PAD = 32
+STACK = 4 * BLOCK + PAD
+
+
+def local_grid(size):
+    return lax.broadcasted_iota(jnp.int32, (size, size), 0), lax.broadcasted_iota(jnp.int32, (size, size), 1)
+
+
+def pack_pair(first, second):
+    r, c = local_grid(first.shape[0])
+    packed = jnp.where(r > c, first, second)
+    diagonal = jnp.sum(jnp.where(r == c, first, 0.0), axis=0, keepdims=True)
+    pad = jnp.concatenate([diagonal, jnp.zeros((PAD - 1, first.shape[0]), jnp.float32)], axis=0)
+    return packed, pad
+
+
+def unpack_pair(packed, diagonal):
+    r, c = local_grid(packed.shape[0])
+    flipped = packed.T
+    first = jnp.where(r > c, packed, jnp.where(r == c, diagonal, flipped))
+    second = jnp.where(r <= c, packed, flipped)
+    return first, second
 
 
 def lower_stacks(acc_ref):
     b = BLOCK
-    first = jnp.concatenate([acc_ref[:, 0:b], acc_ref[b:2 * b, b:2 * b]], axis=0)
-    second = jnp.concatenate(
-        [acc_ref[2 * b:4 * b, b:2 * b], acc_ref[2 * b:4 * b, 2 * b:3 * b], acc_ref[3 * b:4 * b, 3 * b:4 * b]], axis=0
-    )
+    p01, d0 = pack_pair(acc_ref[0:b, 0:b], acc_ref[b:2 * b, b:2 * b])
+    p23, d2 = pack_pair(acc_ref[2 * b:3 * b, 2 * b:3 * b], acc_ref[3 * b:4 * b, 3 * b:4 * b])
+    first = jnp.concatenate([acc_ref[b:4 * b, 0:b], p01, d0], axis=0)
+    second = jnp.concatenate([acc_ref[2 * b:4 * b, b:2 * b], acc_ref[3 * b:4 * b, 2 * b:3 * b], p23, d2], axis=0)
     return first, second
 
 
 def fill_gram(work_ref, first_ref, second_ref):
     b = BLOCK
-    work_ref[:, 0:b] = first_ref[0:4 * b, :]
-    work_ref[b:2 * b, b:2 * b] = first_ref[4 * b:5 * b, :]
+    work_ref[b:4 * b, 0:b] = first_ref[0:3 * b, :]
+    d0, d1 = unpack_pair(first_ref[3 * b:4 * b, :], first_ref[4 * b:4 * b + 1, :])
+    work_ref[0:b, 0:b] = d0
+    work_ref[b:2 * b, b:2 * b] = d1
     work_ref[2 * b:4 * b, b:2 * b] = second_ref[0:2 * b, :]
-    work_ref[2 * b:4 * b, 2 * b:3 * b] = second_ref[2 * b:4 * b, :]
-    work_ref[3 * b:4 * b, 3 * b:4 * b] = second_ref[4 * b:5 * b, :]
+    work_ref[3 * b:4 * b, 2 * b:3 * b] = second_ref[2 * b:3 * b, :]
+    d2, d3 = unpack_pair(second_ref[3 * b:4 * b, :], second_ref[4 * b:4 * b + 1, :])
+    work_ref[2 * b:3 * b, 2 * b:3 * b] = d2
+    work_ref[3 * b:4 * b, 3 * b:4 * b] = d3
     for i in range(4):
         for j in range(i + 1, 4):
             work_ref[i * b:(i + 1) * b, j * b:(j + 1) * b] = work_ref[j * b:(j + 1) * b, i * b:(i + 1) * b].T

time: 99.3 us -> 98.2 us (0.989)
  transfers between devices with their start and end apart: 11 -> 11, of which waited for: 11 -> 10; matrix products, arithmetic and copies ran while one was open for 0% -> 0% of each run, Pallas kernels for 0% -> 0%
where the time goes in v13:
time: 98.2 us; the launch traced here: 97.9 us
  Pallas kernels  64.8 us (66%)
  waiting for transfers between devices  17.6 us (18%)
  starting transfers between devices  13 us (13%)
  other arithmetic  1.06 us (1%)
    pallas_call x1, Pallas kernels, cholesky_and_inverse(): pl.pallas_call(chol_kernel, out_shape=(jax.ShapeDtypeStruct((n, n), jnp.f...  48.2 us
    ppermute x11, waiting for transfers between devices, partner_xor(): return lax.ppermute(value, axis, pairs)  17.6 us
    ppermute x11, starting transfers between devices, partner_xor(): return lax.ppermute(value, axis, pairs)  13 us
    pallas_call x1, Pallas kernels, rows_times(): pl.pallas_call(rows_kernel, out_shape=jax.ShapeDtypeStruct((rows, weights...  8.46 us
    pallas_call x1, Pallas kernels, gram_halves(): pl.pallas_call(functools.partial(gram_kernel, row_count), out_shape=(half...  8.19 us
  transfers between devices with their start and end apart: 11, of which 10 were waited for; matrix products, arithmetic and copies ran while one was open for 0% of the time, Pallas kernels for 0%

profile of v13, /device:TPU:0, one launch (start us, length us, event | category | flops | bytes accessed | tf_op | source)
XLA Modules:
  0.0 97.9 jit_solution(3276572639973712885)
XLA Ops:
  0.6 8.2 %shard_map.30 = (f32[544,128]{1,0:T(8,128)}, f32[544,128]{1,0:T(8,128)}) custom-call(s32[1]{0:T(128)} %bitcast.bit_ref, f32[2048,512]{1,0:T(8,128)} %a_ref.3), custom_call_target="tpu_custom_call" | custom-call | tf_op jit(solution)/shard_map/pallas_call | solution.py:204
  8.8 0.5 collective-permute-start
  9.3 1.4 %collective-permute-done = f32[544,128]{1,0:T(8,128)S(1)} collective-permute-done((f32[544,128]{1,0:T(8,128)}, f32[544,128]{1,0:T(8,128)S(1)}, u32[]{:S(2)}, u32[]{:S(2)}) %collective-permute-start) | collective-permute-done | bytes 278560 | tf_op jit(solution)/shard_map/ppermute | solution.py:227
  10.7 1.0 %add.37 = f32[544,128]{1,0:T(8,128)S(1)} add(f32[544,128]{1,0:T(8,128)} %get-tuple-element.6, f32[544,128]{1,0:T(8,128)S(1)} %collective-permute-done) | non-fusion elementwise | flops 69632 | bytes 835584 | tf_op jit(solution)/shard_map/add | solution.py:278
  11.7 2.9 %collective-permute-start.1 = (f32[136,128]{1,0:T(8,128)S(1)}, f32[136,128]{1,0:T(8,128)S(1)}, u32[]{:S(2)}, u32[]{:S(2)}) collective-permute-start(f32[136,128]{1,0:T(8,128)S(1)} %get-tuple-element.12), channel_id=1, source_target_pairs={{0,8},{8,0},{16,24},{24,16},{1,9},{9,1},{17,25},{25,17},{2,10},{10... | collective-permute-start | bytes 208904 | tf_op jit(solution)/shard_map/ppermute | solution.py:227
  14.6 1.5 %collective-permute-start.3 = (f32[136,128]{1,0:T(8,128)S(1)}, f32[136,128]{1,0:T(8,128)S(1)}, u32[]{:S(2)}, u32[]{:S(2)}) collective-permute-start(f32[136,128]{1,0:T(8,128)S(1)} %get-tuple-element.13), channel_id=1, source_target_pairs={{0,24},{8,16},{16,8},{24,0},{1,25},{9,17},{17,9},{25,1},{2,26},{10... | collective-permute-start | bytes 208904 | tf_op jit(solution)/shard_map/ppermute | solution.py:227
  16.2 0.9 collective-permute-done.1
  17.1 2.9 %collective-permute-done.3 = f32[136,128]{1,0:T(8,128)S(1)} collective-permute-done((f32[136,128]{1,0:T(8,128)S(1)}, f32[136,128]{1,0:T(8,128)S(1)}, u32[]{:S(2)}, u32[]{:S(2)}) %collective-permute-start.3) | collective-permute-done | bytes 69664 | tf_op jit(solution)/shard_map/ppermute | solution.py:227
  20.0 1.1 %collective-permute-done.2 = f32[136,128]{1,0:T(8,128)S(1)} collective-permute-done((f32[136,128]{1,0:T(8,128)S(1)}, f32[136,128]{1,0:T(8,128)S(1)}, u32[]{:S(2)}, u32[]{:S(2)}) %collective-permute-start.2) | collective-permute-done | bytes 69664 | tf_op jit(solution)/shard_map/ppermute | solution.py:227
  21.1 1.6 %collective-permute-start.6 = (f32[136,128]{1,0:T(8,128)S(1)}, f32[136,128]{1,0:T(8,128)S(1)}, u32[]{:S(2)}, u32[]{:S(2)}) collective-permute-start(f32[136,128]{1,0:T(8,128)S(1)} %add_add_fusion), channel_id=1, source_target_pairs={{0,2},{1,3},{2,0},{3,1},{4,6},{5,7},{6,4},{7,5},{8,10},{9,11},{10,... | collective-permute-start | bytes 208904 | tf_op jit(solution)/shard_map/ppermute | solution.py:227
  22.8 2.6 %collective-permute-start.5 = (f32[136,128]{1,0:T(8,128)S(1)}, f32[136,128]{1,0:T(8,128)S(1)}, u32[]{:S(2)}, u32[]{:S(2)}) collective-permute-start(f32[136,128]{1,0:T(8,128)S(1)} %add_add_fusion), channel_id=1, source_target_pairs={{0,4},{1,5},{2,6},{3,7},{4,0},{5,1},{6,2},{7,3},{8,12},{9,13},{10,... | collective-permute-start | bytes 208904 | tf_op jit(solution)/shard_map/ppermute | solution.py:227
  25.4 0.2 collective-permute-start.4
  25.6 4.6 %collective-permute-done.5 = f32[136,128]{1,0:T(8,128)S(1)} collective-permute-done((f32[136,128]{1,0:T(8,128)S(1)}, f32[136,128]{1,0:T(8,128)S(1)}, u32[]{:S(2)}, u32[]{:S(2)}) %collective-permute-start.5) | collective-permute-done | bytes 69664 | tf_op jit(solution)/shard_map/ppermute | solution.py:227
  30.2 1.4 %collective-permute-done.4 = f32[136,128]{1,0:T(8,128)S(1)} collective-permute-done((f32[136,128]{1,0:T(8,128)S(1)}, f32[136,128]{1,0:T(8,128)S(1)}, u32[]{:S(2)}, u32[]{:S(2)}) %collective-permute-start.4) | collective-permute-done | bytes 69664 | tf_op jit(solution)/shard_map/ppermute | solution.py:227
  31.7 1.2 %collective-permute-start.7 = (f32[136,128]{1,0:T(8,128)S(1)}, f32[136,128]{1,0:T(8,128)S(1)}, u32[]{:S(2)}, u32[]{:S(2)}) collective-permute-start(f32[136,128]{1,0:T(8,128)S(1)} %get-tuple-element.11), channel_id=1, source_target_pairs={{0,8},{8,0},{16,24},{24,16},{1,9},{9,1},{17,25},{25,17},{2,10},{10... | collective-permute-start | bytes 208904 | tf_op jit(solution)/shard_map/ppermute | solution.py:227
  32.9 0.8 collective-permute-start.8
  33.7 1.5 %collective-permute-start.9 = (f32[136,128]{1,0:T(8,128)S(1)}, f32[136,128]{1,0:T(8,128)S(1)}, u32[]{:S(2)}, u32[]{:S(2)}) collective-permute-start(f32[136,128]{1,0:T(8,128)S(1)} %get-tuple-element.11), channel_id=1, source_target_pairs={{0,24},{8,16},{16,8},{24,0},{1,25},{9,17},{17,9},{25,1},{2,26},{10... | collective-permute-start | bytes 208904 | tf_op jit(solution)/shard_map/ppermute | solution.py:227
  35.2 0.8 collective-permute-done.7
  36.0 1.2 %collective-permute-done.8 = f32[136,128]{1,0:T(8,128)S(1)} collective-permute-done((f32[136,128]{1,0:T(8,128)S(1)}, f32[136,128]{1,0:T(8,128)S(1)}, u32[]{:S(2)}, u32[]{:S(2)}) %collective-permute-start.8) | collective-permute-done | bytes 69664 | tf_op jit(solution)/shard_map/ppermute | solution.py:227
  37.2 1.7 %collective-permute-done.9 = f32[136,128]{1,0:T(8,128)S(1)} collective-permute-done((f32[136,128]{1,0:T(8,128)S(1)}, f32[136,128]{1,0:T(8,128)S(1)}, u32[]{:S(2)}, u32[]{:S(2)}) %collective-permute-start.9) | collective-permute-done | bytes 69664 | tf_op jit(solution)/shard_map/ppermute | solution.py:227
  39.0 1.5 %collective-permute-done.10.got_ref = f32[544,128]{1,0:T(8,128)S(1)} collective-permute-done((f32[544,128]{1,0:T(8,128)S(1)}, f32[544,128]{1,0:T(8,128)S(1)}, u32[]{:S(2)}, u32[]{:S(2)}) %collective-permute-start.10) | collective-permute-done | bytes 278560 | tf_op jit(solution)/shard_map/ppermute | solution.py:227
  40.6 0.7 copy-done.1
  41.3 48.2 %shard_map.31 = (f32[512,512]{1,0:T(8,128)}, f32[512,512]{1,0:T(8,128)}) custom-call(s32[1]{0:T(128)} %bitcast.bit_ref, f32[544,128]{1,0:T(8,128)} %copy-done, f32[544,128]{1,0:T(8,128)} %copy-done.1), custom_call_target="tpu_custom_call" | custom-call | tf_op jit(solution)/shard_map/pallas_call | solution.py:126
  89.5 8.5 %shard_map.32 = f32[2048,512]{1,0:T(8,128)} custom-call(f32[2048,512]{1,0:T(8,128)} %a_ref.3, f32[512,512]{1,0:T(8,128)} %get-tuple-element.9.w_ref), custom_call_target="tpu_custom_call" | custom-call | tf_op jit(solution)/shard_map/pallas_call | solution.py:145
  (13 shorter events, 0.3 us)
Async XLA Ops:
  8.8 1.9 %collective-permute-start = (f32[544,128]{1,0:T(8,128)}, f32[544,128]{1,0:T(8,128)S(1)}, u32[]{:S(2)}, u32[]{:S(2)}) collective-permute-start(f32[544,128]{1,0:T(8,128)} %get-tuple-element.7), channel_id=1, source_target_pairs={{0,1},{1,0},{2,3},{3,2},{4,5},{5,4},{6,7},{7,6},{8,9},{9,8},{10,11... | collective-permute-start | bytes 835592 | tf_op jit(solution)/shard_map/ppermute | solution.py:227
  11.7 5.4 %collective-permute-start.1 = (f32[136,128]{1,0:T(8,128)S(1)}, f32[136,128]{1,0:T(8,128)S(1)}, u32[]{:S(2)}, u32[]{:S(2)}) collective-permute-start(f32[136,128]{1,0:T(8,128)S(1)} %get-tuple-element.12), channel_id=1, source_target_pairs={{0,8},{8,0},{16,24},{24,16},{1,9},{9,1},{17,25},{25,17},{2,10},{10... | collective-permute-start | bytes 208904 | tf_op jit(solution)/shard_map/ppermute | solution.py:227
  14.6 5.4 %collective-permute-start.3 = (f32[136,128]{1,0:T(8,128)S(1)}, f32[136,128]{1,0:T(8,128)S(1)}, u32[]{:S(2)}, u32[]{:S(2)}) collective-permute-start(f32[136,128]{1,0:T(8,128)S(1)} %get-tuple-element.13), channel_id=1, source_target_pairs={{0,24},{8,16},{16,8},{24,0},{1,25},{9,17},{17,9},{25,1},{2,26},{10... | collective-permute-start | bytes 208904 | tf_op jit(solution)/shard_map/ppermute | solution.py:227
  16.1 5.0 %collective-permute-start.2 = (f32[136,128]{1,0:T(8,128)S(1)}, f32[136,128]{1,0:T(8,128)S(1)}, u32[]{:S(2)}, u32[]{:S(2)}) collective-permute-start(f32[136,128]{1,0:T(8,128)S(1)} %get-tuple-element.14), channel_id=1, source_target_pairs={{0,16},{8,24},{16,0},{24,8},{1,17},{9,25},{17,1},{25,9},{2,18},{10... | collective-permute-start | bytes 208904 | tf_op jit(solution)/shard_map/ppermute | solution.py:227
  21.1 4.5 %collective-permute-start.6 = (f32[136,128]{1,0:T(8,128)S(1)}, f32[136,128]{1,0:T(8,128)S(1)}, u32[]{:S(2)}, u32[]{:S(2)}) collective-permute-start(f32[136,128]{1,0:T(8,128)S(1)} %add_add_fusion), channel_id=1, source_target_pairs={{0,2},{1,3},{2,0},{3,1},{4,6},{5,7},{6,4},{7,5},{8,10},{9,11},{10,... | collective-permute-start | bytes 208904 | tf_op jit(solution)/shard_map/ppermute | solution.py:227
  22.8 7.4 %collective-permute-start.5 = (f32[136,128]{1,0:T(8,128)S(1)}, f32[136,128]{1,0:T(8,128)S(1)}, u32[]{:S(2)}, u32[]{:S(2)}) collective-permute-start(f32[136,128]{1,0:T(8,128)S(1)} %add_add_fusion), channel_id=1, source_target_pairs={{0,4},{1,5},{2,6},{3,7},{4,0},{5,1},{6,2},{7,3},{8,12},{9,13},{10,... | collective-permute-start | bytes 208904 | tf_op jit(solution)/shard_map/ppermute | solution.py:227
  25.4 6.2 %collective-permute-start.4 = (f32[136,128]{1,0:T(8,128)S(1)}, f32[136,128]{1,0:T(8,128)S(1)}, u32[]{:S(2)}, u32[]{:S(2)}) collective-permute-start(f32[136,128]{1,0:T(8,128)S(1)} %add_add_fusion), channel_id=1, source_target_pairs={{0,6},{1,7},{2,4},{3,5},{4,2},{5,3},{6,0},{7,1},{8,14},{9,15},{10,... | collective-permute-start | bytes 208904 | tf_op jit(solution)/shard_map/ppermute | solution.py:227
  31.7 4.4 %collective-permute-start.7 = (f32[136,128]{1,0:T(8,128)S(1)}, f32[136,128]{1,0:T(8,128)S(1)}, u32[]{:S(2)}, u32[]{:S(2)}) collective-permute-start(f32[136,128]{1,0:T(8,128)S(1)} %get-tuple-element.11), channel_id=1, source_target_pairs={{0,8},{8,0},{16,24},{24,16},{1,9},{9,1},{17,25},{25,17},{2,10},{10... | collective-permute-start | bytes 208904 | tf_op jit(solution)/shard_map/ppermute | solution.py:227
  32.9 4.3 %collective-permute-start.8 = (f32[136,128]{1,0:T(8,128)S(1)}, f32[136,128]{1,0:T(8,128)S(1)}, u32[]{:S(2)}, u32[]{:S(2)}) collective-permute-start(f32[136,128]{1,0:T(8,128)S(1)} %get-tuple-element.11), channel_id=1, source_target_pairs={{0,16},{8,24},{16,0},{24,8},{1,17},{9,25},{17,1},{25,9},{2,18},{10... | collective-permute-start | bytes 208904 | tf_op jit(solution)/shard_map/ppermute | solution.py:227
  33.7 5.2 %collective-permute-start.9 = (f32[136,128]{1,0:T(8,128)S(1)}, f32[136,128]{1,0:T(8,128)S(1)}, u32[]{:S(2)}, u32[]{:S(2)}) collective-permute-start(f32[136,128]{1,0:T(8,128)S(1)} %get-tuple-element.11), channel_id=1, source_target_pairs={{0,24},{8,16},{16,8},{24,0},{1,25},{9,17},{17,9},{25,1},{2,26},{10... | collective-permute-start | bytes 208904 | tf_op jit(solution)/shard_map/ppermute | solution.py:227
  38.9 1.6 %copy-start = (f32[544,128]{1,0:T(8,128)}, f32[544,128]{1,0:T(8,128)S(1)}, u32[]{:S(2)}) copy-start(f32[544,128]{1,0:T(8,128)S(1)} %constant_dynamic-update-slice_fusion.mine_ref) | copy-start | bytes 835588
  38.9 1.6 %collective-permute-start.10 = (f32[544,128]{1,0:T(8,128)S(1)}, f32[544,128]{1,0:T(8,128)S(1)}, u32[]{:S(2)}, u32[]{:S(2)}) collective-permute-start(f32[544,128]{1,0:T(8,128)S(1)} %constant_dynamic-update-slice_fusion.mine_ref), channel_id=1, source_target_pairs={{0,1},{1,0},{2,3},{3,2},{4,5},{5,4},{6,7},{7,6},{8,9},{9,8},{10,11... | collective-permute-start | bytes 835592 | tf_op jit(solution)/shard_map/ppermute | solution.py:227
  40.6 0.7 copy-start.1

commit v14 on v13

--- a/solution.py
+++ b/solution.py
@@ -141,7 +141,7 @@
 
 def rows_times(matrix, weights):
     rows, width = matrix.shape
-    tile = min(rows, 512)
+    tile = min(rows, 1024)
     return pl.pallas_call(
         rows_kernel,
         out_shape=jax.ShapeDtypeStruct((rows, weights.shape[1]), jnp.float32),

time: 98.2 us -> 98.1 us (level)
  no operation moved by 1% of the time
where the time goes in v14:
time: 98.1 us; the launch traced here: 97.9 us
  Pallas kernels  64.8 us (66%)
  waiting for transfers between devices  17.6 us (18%)
  starting transfers between devices  13 us (13%)
  other arithmetic  1.06 us (1%)
    pallas_call x1, Pallas kernels, cholesky_and_inverse(): pl.pallas_call(chol_kernel, out_shape=(jax.ShapeDtypeStruct((n, n), jnp.f...  48.2 us
    ppermute x11, waiting for transfers between devices, partner_xor(): return lax.ppermute(value, axis, pairs)  17.6 us
    ppermute x11, starting transfers between devices, partner_xor(): return lax.ppermute(value, axis, pairs)  13 us
    pallas_call x1, Pallas kernels, rows_times(): pl.pallas_call(rows_kernel, out_shape=jax.ShapeDtypeStruct((rows, weights...  8.44 us
    pallas_call x1, Pallas kernels, gram_halves(): pl.pallas_call(functools.partial(gram_kernel, row_count), out_shape=(half...  8.19 us
  transfers between devices with their start and end apart: 11, of which 10 were waited for; matrix products, arithmetic and copies ran while one was open for 0% of the time, Pallas kernels for 0%

profile of v14, /device:TPU:0, one launch (start us, length us, event | category | flops | bytes accessed | tf_op | source)
XLA Modules:
  0.0 97.9 jit_solution(8096985213235626755)
XLA Ops:
  0.6 8.2 %shard_map.30 = (f32[544,128]{1,0:T(8,128)}, f32[544,128]{1,0:T(8,128)}) custom-call(s32[1]{0:T(128)} %bitcast.bit_ref, f32[2048,512]{1,0:T(8,128)} %a_ref.3), custom_call_target="tpu_custom_call" | custom-call | tf_op jit(solution)/shard_map/pallas_call | solution.py:204
  8.8 0.5 collective-permute-start
  9.3 1.4 %collective-permute-done = f32[544,128]{1,0:T(8,128)S(1)} collective-permute-done((f32[544,128]{1,0:T(8,128)}, f32[544,128]{1,0:T(8,128)S(1)}, u32[]{:S(2)}, u32[]{:S(2)}) %collective-permute-start) | collective-permute-done | bytes 278560 | tf_op jit(solution)/shard_map/ppermute | solution.py:227
  10.7 1.0 %add.37 = f32[544,128]{1,0:T(8,128)S(1)} add(f32[544,128]{1,0:T(8,128)} %get-tuple-element.6, f32[544,128]{1,0:T(8,128)S(1)} %collective-permute-done) | non-fusion elementwise | flops 69632 | bytes 835584 | tf_op jit(solution)/shard_map/add | solution.py:278
  11.7 2.9 %collective-permute-start.1 = (f32[136,128]{1,0:T(8,128)S(1)}, f32[136,128]{1,0:T(8,128)S(1)}, u32[]{:S(2)}, u32[]{:S(2)}) collective-permute-start(f32[136,128]{1,0:T(8,128)S(1)} %get-tuple-element.12), channel_id=1, source_target_pairs={{0,8},{8,0},{16,24},{24,16},{1,9},{9,1},{17,25},{25,17},{2,10},{10... | collective-permute-start | bytes 208904 | tf_op jit(solution)/shard_map/ppermute | solution.py:227
  14.6 1.5 %collective-permute-start.3 = (f32[136,128]{1,0:T(8,128)S(1)}, f32[136,128]{1,0:T(8,128)S(1)}, u32[]{:S(2)}, u32[]{:S(2)}) collective-permute-start(f32[136,128]{1,0:T(8,128)S(1)} %get-tuple-element.13), channel_id=1, source_target_pairs={{0,24},{8,16},{16,8},{24,0},{1,25},{9,17},{17,9},{25,1},{2,26},{10... | collective-permute-start | bytes 208904 | tf_op jit(solution)/shard_map/ppermute | solution.py:227
  16.2 0.9 collective-permute-done.1
  17.1 2.9 %collective-permute-done.3 = f32[136,128]{1,0:T(8,128)S(1)} collective-permute-done((f32[136,128]{1,0:T(8,128)S(1)}, f32[136,128]{1,0:T(8,128)S(1)}, u32[]{:S(2)}, u32[]{:S(2)}) %collective-permute-start.3) | collective-permute-done | bytes 69664 | tf_op jit(solution)/shard_map/ppermute | solution.py:227
  20.0 1.1 %collective-permute-done.2 = f32[136,128]{1,0:T(8,128)S(1)} collective-permute-done((f32[136,128]{1,0:T(8,128)S(1)}, f32[136,128]{1,0:T(8,128)S(1)}, u32[]{:S(2)}, u32[]{:S(2)}) %collective-permute-start.2) | collective-permute-done | bytes 69664 | tf_op jit(solution)/shard_map/ppermute | solution.py:227
  21.1 1.6 %collective-permute-start.6 = (f32[136,128]{1,0:T(8,128)S(1)}, f32[136,128]{1,0:T(8,128)S(1)}, u32[]{:S(2)}, u32[]{:S(2)}) collective-permute-start(f32[136,128]{1,0:T(8,128)S(1)} %add_add_fusion), channel_id=1, source_target_pairs={{0,2},{1,3},{2,0},{3,1},{4,6},{5,7},{6,4},{7,5},{8,10},{9,11},{10,... | collective-permute-start | bytes 208904 | tf_op jit(solution)/shard_map/ppermute | solution.py:227
  22.8 2.6 %collective-permute-start.5 = (f32[136,128]{1,0:T(8,128)S(1)}, f32[136,128]{1,0:T(8,128)S(1)}, u32[]{:S(2)}, u32[]{:S(2)}) collective-permute-start(f32[136,128]{1,0:T(8,128)S(1)} %add_add_fusion), channel_id=1, source_target_pairs={{0,4},{1,5},{2,6},{3,7},{4,0},{5,1},{6,2},{7,3},{8,12},{9,13},{10,... | collective-permute-start | bytes 208904 | tf_op jit(solution)/shard_map/ppermute | solution.py:227
  25.4 0.2 collective-permute-start.4
  25.6 4.6 %collective-permute-done.5 = f32[136,128]{1,0:T(8,128)S(1)} collective-permute-done((f32[136,128]{1,0:T(8,128)S(1)}, f32[136,128]{1,0:T(8,128)S(1)}, u32[]{:S(2)}, u32[]{:S(2)}) %collective-permute-start.5) | collective-permute-done | bytes 69664 | tf_op jit(solution)/shard_map/ppermute | solution.py:227
  30.2 1.4 %collective-permute-done.4 = f32[136,128]{1,0:T(8,128)S(1)} collective-permute-done((f32[136,128]{1,0:T(8,128)S(1)}, f32[136,128]{1,0:T(8,128)S(1)}, u32[]{:S(2)}, u32[]{:S(2)}) %collective-permute-start.4) | collective-permute-done | bytes 69664 | tf_op jit(solution)/shard_map/ppermute | solution.py:227
  31.7 1.2 %collective-permute-start.7 = (f32[136,128]{1,0:T(8,128)S(1)}, f32[136,128]{1,0:T(8,128)S(1)}, u32[]{:S(2)}, u32[]{:S(2)}) collective-permute-start(f32[136,128]{1,0:T(8,128)S(1)} %get-tuple-element.11), channel_id=1, source_target_pairs={{0,8},{8,0},{16,24},{24,16},{1,9},{9,1},{17,25},{25,17},{2,10},{10... | collective-permute-start | bytes 208904 | tf_op jit(solution)/shard_map/ppermute | solution.py:227
  32.9 0.8 collective-permute-start.8
  33.7 1.5 %collective-permute-start.9 = (f32[136,128]{1,0:T(8,128)S(1)}, f32[136,128]{1,0:T(8,128)S(1)}, u32[]{:S(2)}, u32[]{:S(2)}) collective-permute-start(f32[136,128]{1,0:T(8,128)S(1)} %get-tuple-element.11), channel_id=1, source_target_pairs={{0,24},{8,16},{16,8},{24,0},{1,25},{9,17},{17,9},{25,1},{2,26},{10... | collective-permute-start | bytes 208904 | tf_op jit(solution)/shard_map/ppermute | solution.py:227
  35.2 0.8 collective-permute-done.7
  36.0 1.2 %collective-permute-done.8 = f32[136,128]{1,0:T(8,128)S(1)} collective-permute-done((f32[136,128]{1,0:T(8,128)S(1)}, f32[136,128]{1,0:T(8,128)S(1)}, u32[]{:S(2)}, u32[]{:S(2)}) %collective-permute-start.8) | collective-permute-done | bytes 69664 | tf_op jit(solution)/shard_map/ppermute | solution.py:227
  37.2 1.7 %collective-permute-done.9 = f32[136,128]{1,0:T(8,128)S(1)} collective-permute-done((f32[136,128]{1,0:T(8,128)S(1)}, f32[136,128]{1,0:T(8,128)S(1)}, u32[]{:S(2)}, u32[]{:S(2)}) %collective-permute-start.9) | collective-permute-done | bytes 69664 | tf_op jit(solution)/shard_map/ppermute | solution.py:227
  39.0 1.5 %collective-permute-done.10.got_ref = f32[544,128]{1,0:T(8,128)S(1)} collective-permute-done((f32[544,128]{1,0:T(8,128)S(1)}, f32[544,128]{1,0:T(8,128)S(1)}, u32[]{:S(2)}, u32[]{:S(2)}) %collective-permute-start.10) | collective-permute-done | bytes 278560 | tf_op jit(solution)/shard_map/ppermute | solution.py:227
  40.6 0.7 copy-done.1
  41.3 48.2 %shard_map.31 = (f32[512,512]{1,0:T(8,128)}, f32[512,512]{1,0:T(8,128)}) custom-call(s32[1]{0:T(128)} %bitcast.bit_ref, f32[544,128]{1,0:T(8,128)} %copy-done, f32[544,128]{1,0:T(8,128)} %copy-done.1), custom_call_target="tpu_custom_call" | custom-call | tf_op jit(solution)/shard_map/pallas_call | solution.py:126
  89.5 8.4 %shard_map.32 = f32[2048,512]{1,0:T(8,128)} custom-call(f32[2048,512]{1,0:T(8,128)} %a_ref.3, f32[512,512]{1,0:T(8,128)} %get-tuple-element.9.w_ref), custom_call_target="tpu_custom_call" | custom-call | tf_op jit(solution)/shard_map/pallas_call | solution.py:145
  (13 shorter events, 0.3 us)
Async XLA Ops:
  8.8 1.9 %collective-permute-start = (f32[544,128]{1,0:T(8,128)}, f32[544,128]{1,0:T(8,128)S(1)}, u32[]{:S(2)}, u32[]{:S(2)}) collective-permute-start(f32[544,128]{1,0:T(8,128)} %get-tuple-element.7), channel_id=1, source_target_pairs={{0,1},{1,0},{2,3},{3,2},{4,5},{5,4},{6,7},{7,6},{8,9},{9,8},{10,11... | collective-permute-start | bytes 835592 | tf_op jit(solution)/shard_map/ppermute | solution.py:227
  11.7 5.4 %collective-permute-start.1 = (f32[136,128]{1,0:T(8,128)S(1)}, f32[136,128]{1,0:T(8,128)S(1)}, u32[]{:S(2)}, u32[]{:S(2)}) collective-permute-start(f32[136,128]{1,0:T(8,128)S(1)} %get-tuple-element.12), channel_id=1, source_target_pairs={{0,8},{8,0},{16,24},{24,16},{1,9},{9,1},{17,25},{25,17},{2,10},{10... | collective-permute-start | bytes 208904 | tf_op jit(solution)/shard_map/ppermute | solution.py:227
  14.6 5.4 %collective-permute-start.3 = (f32[136,128]{1,0:T(8,128)S(1)}, f32[136,128]{1,0:T(8,128)S(1)}, u32[]{:S(2)}, u32[]{:S(2)}) collective-permute-start(f32[136,128]{1,0:T(8,128)S(1)} %get-tuple-element.13), channel_id=1, source_target_pairs={{0,24},{8,16},{16,8},{24,0},{1,25},{9,17},{17,9},{25,1},{2,26},{10... | collective-permute-start | bytes 208904 | tf_op jit(solution)/shard_map/ppermute | solution.py:227
  16.1 5.0 %collective-permute-start.2 = (f32[136,128]{1,0:T(8,128)S(1)}, f32[136,128]{1,0:T(8,128)S(1)}, u32[]{:S(2)}, u32[]{:S(2)}) collective-permute-start(f32[136,128]{1,0:T(8,128)S(1)} %get-tuple-element.14), channel_id=1, source_target_pairs={{0,16},{8,24},{16,0},{24,8},{1,17},{9,25},{17,1},{25,9},{2,18},{10... | collective-permute-start | bytes 208904 | tf_op jit(solution)/shard_map/ppermute | solution.py:227
  21.1 4.5 %collective-permute-start.6 = (f32[136,128]{1,0:T(8,128)S(1)}, f32[136,128]{1,0:T(8,128)S(1)}, u32[]{:S(2)}, u32[]{:S(2)}) collective-permute-start(f32[136,128]{1,0:T(8,128)S(1)} %add_add_fusion), channel_id=1, source_target_pairs={{0,2},{1,3},{2,0},{3,1},{4,6},{5,7},{6,4},{7,5},{8,10},{9,11},{10,... | collective-permute-start | bytes 208904 | tf_op jit(solution)/shard_map/ppermute | solution.py:227
  22.8 7.4 %collective-permute-start.5 = (f32[136,128]{1,0:T(8,128)S(1)}, f32[136,128]{1,0:T(8,128)S(1)}, u32[]{:S(2)}, u32[]{:S(2)}) collective-permute-start(f32[136,128]{1,0:T(8,128)S(1)} %add_add_fusion), channel_id=1, source_target_pairs={{0,4},{1,5},{2,6},{3,7},{4,0},{5,1},{6,2},{7,3},{8,12},{9,13},{10,... | collective-permute-start | bytes 208904 | tf_op jit(solution)/shard_map/ppermute | solution.py:227
  25.4 6.2 %collective-permute-start.4 = (f32[136,128]{1,0:T(8,128)S(1)}, f32[136,128]{1,0:T(8,128)S(1)}, u32[]{:S(2)}, u32[]{:S(2)}) collective-permute-start(f32[136,128]{1,0:T(8,128)S(1)} %add_add_fusion), channel_id=1, source_target_pairs={{0,6},{1,7},{2,4},{3,5},{4,2},{5,3},{6,0},{7,1},{8,14},{9,15},{10,... | collective-permute-start | bytes 208904 | tf_op jit(solution)/shard_map/ppermute | solution.py:227
  31.7 4.4 %collective-permute-start.7 = (f32[136,128]{1,0:T(8,128)S(1)}, f32[136,128]{1,0:T(8,128)S(1)}, u32[]{:S(2)}, u32[]{:S(2)}) collective-permute-start(f32[136,128]{1,0:T(8,128)S(1)} %get-tuple-element.11), channel_id=1, source_target_pairs={{0,8},{8,0},{16,24},{24,16},{1,9},{9,1},{17,25},{25,17},{2,10},{10... | collective-permute-start | bytes 208904 | tf_op jit(solution)/shard_map/ppermute | solution.py:227
  32.9 4.3 %collective-permute-start.8 = (f32[136,128]{1,0:T(8,128)S(1)}, f32[136,128]{1,0:T(8,128)S(1)}, u32[]{:S(2)}, u32[]{:S(2)}) collective-permute-start(f32[136,128]{1,0:T(8,128)S(1)} %get-tuple-element.11), channel_id=1, source_target_pairs={{0,16},{8,24},{16,0},{24,8},{1,17},{9,25},{17,1},{25,9},{2,18},{10... | collective-permute-start | bytes 208904 | tf_op jit(solution)/shard_map/ppermute | solution.py:227
  33.7 5.2 %collective-permute-start.9 = (f32[136,128]{1,0:T(8,128)S(1)}, f32[136,128]{1,0:T(8,128)S(1)}, u32[]{:S(2)}, u32[]{:S(2)}) collective-permute-start(f32[136,128]{1,0:T(8,128)S(1)} %get-tuple-element.11), channel_id=1, source_target_pairs={{0,24},{8,16},{16,8},{24,0},{1,25},{9,17},{17,9},{25,1},{2,26},{10... | collective-permute-start | bytes 208904 | tf_op jit(solution)/shard_map/ppermute | solution.py:227
  38.9 1.6 %copy-start = (f32[544,128]{1,0:T(8,128)}, f32[544,128]{1,0:T(8,128)S(1)}, u32[]{:S(2)}) copy-start(f32[544,128]{1,0:T(8,128)S(1)} %constant_dynamic-update-slice_fusion.mine_ref) | copy-start | bytes 835588
  38.9 1.6 %collective-permute-start.10 = (f32[544,128]{1,0:T(8,128)S(1)}, f32[544,128]{1,0:T(8,128)S(1)}, u32[]{:S(2)}, u32[]{:S(2)}) collective-permute-start(f32[544,128]{1,0:T(8,128)S(1)} %constant_dynamic-update-slice_fusion.mine_ref), channel_id=1, source_target_pairs={{0,1},{1,0},{2,3},{3,2},{4,5},{5,4},{6,7},{7,6},{8,9},{9,8},{10,11... | collective-permute-start | bytes 835592 | tf_op jit(solution)/shard_map/ppermute | solution.py:227
  40.6 0.7 copy-start.1

commit v15 on v14

--- a/solution.py
+++ b/solution.py
@@ -199,7 +199,7 @@
 
 def gram_halves(matrix, row_count, bit):
     rows, width = matrix.shape
-    tile = min(rows, 512)
+    tile = min(rows, 1024)
     half = jax.ShapeDtypeStruct((STACK, BLOCK), jnp.float32)
     return pl.pallas_call(
         functools.partial(gram_kernel, row_count),

time: 98.1 us -> 98.2 us (level)
  no operation moved by 1% of the time
where the time goes in v15:
time: 98.2 us; the launch traced here: 98 us
  Pallas kernels  64.9 us (66%)
  waiting for transfers between devices  17.6 us (18%)
  starting transfers between devices  13 us (13%)
  other arithmetic  1.06 us (1%)
    pallas_call x1, Pallas kernels, cholesky_and_inverse(): pl.pallas_call(chol_kernel, out_shape=(jax.ShapeDtypeStruct((n, n), jnp.f...  48.2 us
    ppermute x11, waiting for transfers between devices, partner_xor(): return lax.ppermute(value, axis, pairs)  17.6 us
    ppermute x11, starting transfers between devices, partner_xor(): return lax.ppermute(value, axis, pairs)  13 us
    pallas_call x1, Pallas kernels, rows_times(): pl.pallas_call(rows_kernel, out_shape=jax.ShapeDtypeStruct((rows, weights...  8.44 us
    pallas_call x1, Pallas kernels, gram_halves(): pl.pallas_call(functools.partial(gram_kernel, row_count), out_shape=(half...  8.31 us
  transfers between devices with their start and end apart: 11, of which 10 were waited for; matrix products, arithmetic and copies ran while one was open for 0% of the time, Pallas kernels for 0%

profile of v15, /device:TPU:0, one launch (start us, length us, event | category | flops | bytes accessed | tf_op | source)
XLA Modules:
  0.0 98.0 jit_solution(17275470790067725806)
XLA Ops:
  0.6 8.3 %shard_map.30 = (f32[544,128]{1,0:T(8,128)}, f32[544,128]{1,0:T(8,128)}) custom-call(s32[1]{0:T(128)} %bitcast.bit_ref, f32[2048,512]{1,0:T(8,128)} %a_ref.3), custom_call_target="tpu_custom_call" | custom-call | tf_op jit(solution)/shard_map/pallas_call | solution.py:204
  8.9 0.5 collective-permute-start
  9.4 1.4 %collective-permute-done = f32[544,128]{1,0:T(8,128)S(1)} collective-permute-done((f32[544,128]{1,0:T(8,128)}, f32[544,128]{1,0:T(8,128)S(1)}, u32[]{:S(2)}, u32[]{:S(2)}) %collective-permute-start) | collective-permute-done | bytes 278560 | tf_op jit(solution)/shard_map/ppermute | solution.py:227
  10.8 1.0 %add.37 = f32[544,128]{1,0:T(8,128)S(1)} add(f32[544,128]{1,0:T(8,128)} %get-tuple-element.6, f32[544,128]{1,0:T(8,128)S(1)} %collective-permute-done) | non-fusion elementwise | flops 69632 | bytes 835584 | tf_op jit(solution)/shard_map/add | solution.py:278
  11.8 2.9 %collective-permute-start.1 = (f32[136,128]{1,0:T(8,128)S(1)}, f32[136,128]{1,0:T(8,128)S(1)}, u32[]{:S(2)}, u32[]{:S(2)}) collective-permute-start(f32[136,128]{1,0:T(8,128)S(1)} %get-tuple-element.12), channel_id=1, source_target_pairs={{0,8},{8,0},{16,24},{24,16},{1,9},{9,1},{17,25},{25,17},{2,10},{10... | collective-permute-start | bytes 208904 | tf_op jit(solution)/shard_map/ppermute | solution.py:227
  14.7 1.5 %collective-permute-start.3 = (f32[136,128]{1,0:T(8,128)S(1)}, f32[136,128]{1,0:T(8,128)S(1)}, u32[]{:S(2)}, u32[]{:S(2)}) collective-permute-start(f32[136,128]{1,0:T(8,128)S(1)} %get-tuple-element.13), channel_id=1, source_target_pairs={{0,24},{8,16},{16,8},{24,0},{1,25},{9,17},{17,9},{25,1},{2,26},{10... | collective-permute-start | bytes 208904 | tf_op jit(solution)/shard_map/ppermute | solution.py:227
  16.3 0.9 collective-permute-done.1
  17.2 2.9 %collective-permute-done.3 = f32[136,128]{1,0:T(8,128)S(1)} collective-permute-done((f32[136,128]{1,0:T(8,128)S(1)}, f32[136,128]{1,0:T(8,128)S(1)}, u32[]{:S(2)}, u32[]{:S(2)}) %collective-permute-start.3) | collective-permute-done | bytes 69664 | tf_op jit(solution)/shard_map/ppermute | solution.py:227
  20.1 1.1 %collective-permute-done.2 = f32[136,128]{1,0:T(8,128)S(1)} collective-permute-done((f32[136,128]{1,0:T(8,128)S(1)}, f32[136,128]{1,0:T(8,128)S(1)}, u32[]{:S(2)}, u32[]{:S(2)}) %collective-permute-start.2) | collective-permute-done | bytes 69664 | tf_op jit(solution)/shard_map/ppermute | solution.py:227
  21.3 1.6 %collective-permute-start.6 = (f32[136,128]{1,0:T(8,128)S(1)}, f32[136,128]{1,0:T(8,128)S(1)}, u32[]{:S(2)}, u32[]{:S(2)}) collective-permute-start(f32[136,128]{1,0:T(8,128)S(1)} %add_add_fusion), channel_id=1, source_target_pairs={{0,2},{1,3},{2,0},{3,1},{4,6},{5,7},{6,4},{7,5},{8,10},{9,11},{10,... | collective-permute-start | bytes 208904 | tf_op jit(solution)/shard_map/ppermute | solution.py:227
  22.9 2.6 %collective-permute-start.5 = (f32[136,128]{1,0:T(8,128)S(1)}, f32[136,128]{1,0:T(8,128)S(1)}, u32[]{:S(2)}, u32[]{:S(2)}) collective-permute-start(f32[136,128]{1,0:T(8,128)S(1)} %add_add_fusion), channel_id=1, source_target_pairs={{0,4},{1,5},{2,6},{3,7},{4,0},{5,1},{6,2},{7,3},{8,12},{9,13},{10,... | collective-permute-start | bytes 208904 | tf_op jit(solution)/shard_map/ppermute | solution.py:227
  25.5 0.2 collective-permute-start.4
  25.7 4.6 %collective-permute-done.5 = f32[136,128]{1,0:T(8,128)S(1)} collective-permute-done((f32[136,128]{1,0:T(8,128)S(1)}, f32[136,128]{1,0:T(8,128)S(1)}, u32[]{:S(2)}, u32[]{:S(2)}) %collective-permute-start.5) | collective-permute-done | bytes 69664 | tf_op jit(solution)/shard_map/ppermute | solution.py:227
  30.3 1.4 %collective-permute-done.4 = f32[136,128]{1,0:T(8,128)S(1)} collective-permute-done((f32[136,128]{1,0:T(8,128)S(1)}, f32[136,128]{1,0:T(8,128)S(1)}, u32[]{:S(2)}, u32[]{:S(2)}) %collective-permute-start.4) | collective-permute-done | bytes 69664 | tf_op jit(solution)/shard_map/ppermute | solution.py:227
  31.8 1.2 %collective-permute-start.7 = (f32[136,128]{1,0:T(8,128)S(1)}, f32[136,128]{1,0:T(8,128)S(1)}, u32[]{:S(2)}, u32[]{:S(2)}) collective-permute-start(f32[136,128]{1,0:T(8,128)S(1)} %get-tuple-element.11), channel_id=1, source_target_pairs={{0,8},{8,0},{16,24},{24,16},{1,9},{9,1},{17,25},{25,17},{2,10},{10... | collective-permute-start | bytes 208904 | tf_op jit(solution)/shard_map/ppermute | solution.py:227
  33.0 0.8 collective-permute-start.8
  33.8 1.5 %collective-permute-start.9 = (f32[136,128]{1,0:T(8,128)S(1)}, f32[136,128]{1,0:T(8,128)S(1)}, u32[]{:S(2)}, u32[]{:S(2)}) collective-permute-start(f32[136,128]{1,0:T(8,128)S(1)} %get-tuple-element.11), channel_id=1, source_target_pairs={{0,24},{8,16},{16,8},{24,0},{1,25},{9,17},{17,9},{25,1},{2,26},{10... | collective-permute-start | bytes 208904 | tf_op jit(solution)/shard_map/ppermute | solution.py:227
  35.3 0.8 collective-permute-done.7
  36.2 1.2 %collective-permute-done.8 = f32[136,128]{1,0:T(8,128)S(1)} collective-permute-done((f32[136,128]{1,0:T(8,128)S(1)}, f32[136,128]{1,0:T(8,128)S(1)}, u32[]{:S(2)}, u32[]{:S(2)}) %collective-permute-start.8) | collective-permute-done | bytes 69664 | tf_op jit(solution)/shard_map/ppermute | solution.py:227
  37.3 1.7 %collective-permute-done.9 = f32[136,128]{1,0:T(8,128)S(1)} collective-permute-done((f32[136,128]{1,0:T(8,128)S(1)}, f32[136,128]{1,0:T(8,128)S(1)}, u32[]{:S(2)}, u32[]{:S(2)}) %collective-permute-start.9) | collective-permute-done | bytes 69664 | tf_op jit(solution)/shard_map/ppermute | solution.py:227
  39.1 1.5 %collective-permute-done.10.got_ref = f32[544,128]{1,0:T(8,128)S(1)} collective-permute-done((f32[544,128]{1,0:T(8,128)S(1)}, f32[544,128]{1,0:T(8,128)S(1)}, u32[]{:S(2)}, u32[]{:S(2)}) %collective-permute-start.10) | collective-permute-done | bytes 278560 | tf_op jit(solution)/shard_map/ppermute | solution.py:227
  40.7 0.7 copy-done.1
  41.4 48.2 %shard_map.31 = (f32[512,512]{1,0:T(8,128)}, f32[512,512]{1,0:T(8,128)}) custom-call(s32[1]{0:T(128)} %bitcast.bit_ref, f32[544,128]{1,0:T(8,128)} %copy-done, f32[544,128]{1,0:T(8,128)} %copy-done.1), custom_call_target="tpu_custom_call" | custom-call | tf_op jit(solution)/shard_map/pallas_call | solution.py:126
  89.6 8.4 %shard_map.32 = f32[2048,512]{1,0:T(8,128)} custom-call(f32[2048,512]{1,0:T(8,128)} %a_ref.3, f32[512,512]{1,0:T(8,128)} %get-tuple-element.9.w_ref), custom_call_target="tpu_custom_call" | custom-call | tf_op jit(solution)/shard_map/pallas_call | solution.py:145
  (13 shorter events, 0.3 us)
Async XLA Ops:
  8.9 1.9 %collective-permute-start = (f32[544,128]{1,0:T(8,128)}, f32[544,128]{1,0:T(8,128)S(1)}, u32[]{:S(2)}, u32[]{:S(2)}) collective-permute-start(f32[544,128]{1,0:T(8,128)} %get-tuple-element.7), channel_id=1, source_target_pairs={{0,1},{1,0},{2,3},{3,2},{4,5},{5,4},{6,7},{7,6},{8,9},{9,8},{10,11... | collective-permute-start | bytes 835592 | tf_op jit(solution)/shard_map/ppermute | solution.py:227
  11.8 5.4 %collective-permute-start.1 = (f32[136,128]{1,0:T(8,128)S(1)}, f32[136,128]{1,0:T(8,128)S(1)}, u32[]{:S(2)}, u32[]{:S(2)}) collective-permute-start(f32[136,128]{1,0:T(8,128)S(1)} %get-tuple-element.12), channel_id=1, source_target_pairs={{0,8},{8,0},{16,24},{24,16},{1,9},{9,1},{17,25},{25,17},{2,10},{10... | collective-permute-start | bytes 208904 | tf_op jit(solution)/shard_map/ppermute | solution.py:227
  14.7 5.4 %collective-permute-start.3 = (f32[136,128]{1,0:T(8,128)S(1)}, f32[136,128]{1,0:T(8,128)S(1)}, u32[]{:S(2)}, u32[]{:S(2)}) collective-permute-start(f32[136,128]{1,0:T(8,128)S(1)} %get-tuple-element.13), channel_id=1, source_target_pairs={{0,24},{8,16},{16,8},{24,0},{1,25},{9,17},{17,9},{25,1},{2,26},{10... | collective-permute-start | bytes 208904 | tf_op jit(solution)/shard_map/ppermute | solution.py:227
  16.2 5.0 %collective-permute-start.2 = (f32[136,128]{1,0:T(8,128)S(1)}, f32[136,128]{1,0:T(8,128)S(1)}, u32[]{:S(2)}, u32[]{:S(2)}) collective-permute-start(f32[136,128]{1,0:T(8,128)S(1)} %get-tuple-element.14), channel_id=1, source_target_pairs={{0,16},{8,24},{16,0},{24,8},{1,17},{9,25},{17,1},{25,9},{2,18},{10... | collective-permute-start | bytes 208904 | tf_op jit(solution)/shard_map/ppermute | solution.py:227
  21.3 4.5 %collective-permute-start.6 = (f32[136,128]{1,0:T(8,128)S(1)}, f32[136,128]{1,0:T(8,128)S(1)}, u32[]{:S(2)}, u32[]{:S(2)}) collective-permute-start(f32[136,128]{1,0:T(8,128)S(1)} %add_add_fusion), channel_id=1, source_target_pairs={{0,2},{1,3},{2,0},{3,1},{4,6},{5,7},{6,4},{7,5},{8,10},{9,11},{10,... | collective-permute-start | bytes 208904 | tf_op jit(solution)/shard_map/ppermute | solution.py:227
  22.9 7.4 %collective-permute-start.5 = (f32[136,128]{1,0:T(8,128)S(1)}, f32[136,128]{1,0:T(8,128)S(1)}, u32[]{:S(2)}, u32[]{:S(2)}) collective-permute-start(f32[136,128]{1,0:T(8,128)S(1)} %add_add_fusion), channel_id=1, source_target_pairs={{0,4},{1,5},{2,6},{3,7},{4,0},{5,1},{6,2},{7,3},{8,12},{9,13},{10,... | collective-permute-start | bytes 208904 | tf_op jit(solution)/shard_map/ppermute | solution.py:227
  25.5 6.2 %collective-permute-start.4 = (f32[136,128]{1,0:T(8,128)S(1)}, f32[136,128]{1,0:T(8,128)S(1)}, u32[]{:S(2)}, u32[]{:S(2)}) collective-permute-start(f32[136,128]{1,0:T(8,128)S(1)} %add_add_fusion), channel_id=1, source_target_pairs={{0,6},{1,7},{2,4},{3,5},{4,2},{5,3},{6,0},{7,1},{8,14},{9,15},{10,... | collective-permute-start | bytes 208904 | tf_op jit(solution)/shard_map/ppermute | solution.py:227
  31.8 4.4 %collective-permute-start.7 = (f32[136,128]{1,0:T(8,128)S(1)}, f32[136,128]{1,0:T(8,128)S(1)}, u32[]{:S(2)}, u32[]{:S(2)}) collective-permute-start(f32[136,128]{1,0:T(8,128)S(1)} %get-tuple-element.11), channel_id=1, source_target_pairs={{0,8},{8,0},{16,24},{24,16},{1,9},{9,1},{17,25},{25,17},{2,10},{10... | collective-permute-start | bytes 208904 | tf_op jit(solution)/shard_map/ppermute | solution.py:227
  33.0 4.3 %collective-permute-start.8 = (f32[136,128]{1,0:T(8,128)S(1)}, f32[136,128]{1,0:T(8,128)S(1)}, u32[]{:S(2)}, u32[]{:S(2)}) collective-permute-start(f32[136,128]{1,0:T(8,128)S(1)} %get-tuple-element.11), channel_id=1, source_target_pairs={{0,16},{8,24},{16,0},{24,8},{1,17},{9,25},{17,1},{25,9},{2,18},{10... | collective-permute-start | bytes 208904 | tf_op jit(solution)/shard_map/ppermute | solution.py:227
  33.8 5.2 %collective-permute-start.9 = (f32[136,128]{1,0:T(8,128)S(1)}, f32[136,128]{1,0:T(8,128)S(1)}, u32[]{:S(2)}, u32[]{:S(2)}) collective-permute-start(f32[136,128]{1,0:T(8,128)S(1)} %get-tuple-element.11), channel_id=1, source_target_pairs={{0,24},{8,16},{16,8},{24,0},{1,25},{9,17},{17,9},{25,1},{2,26},{10... | collective-permute-start | bytes 208904 | tf_op jit(solution)/shard_map/ppermute | solution.py:227
  39.0 1.6 %copy-start = (f32[544,128]{1,0:T(8,128)}, f32[544,128]{1,0:T(8,128)S(1)}, u32[]{:S(2)}) copy-start(f32[544,128]{1,0:T(8,128)S(1)} %constant_dynamic-update-slice_fusion.mine_ref) | copy-start | bytes 835588
  39.1 1.6 %collective-permute-start.10 = (f32[544,128]{1,0:T(8,128)S(1)}, f32[544,128]{1,0:T(8,128)S(1)}, u32[]{:S(2)}, u32[]{:S(2)}) collective-permute-start(f32[544,128]{1,0:T(8,128)S(1)} %constant_dynamic-update-slice_fusion.mine_ref), channel_id=1, source_target_pairs={{0,1},{1,0},{2,3},{3,2},{4,5},{5,4},{6,7},{7,6},{8,9},{9,8},{10,11... | collective-permute-start | bytes 835592 | tf_op jit(solution)/shard_map/ppermute | solution.py:227
  40.7 0.7 copy-start.1
